TPU v7x, 8 devices: a whole 2x2x1 slice. The times are simulated.
8 devices in a mesh: dp: 1 (over z), tp: 2 (over y), pp: 4 (over x, core).
Axes of the slice: x: 2, y: 2, z: 1, core: 2. Of those that a mesh axis runs over, the one named last changes fastest.
Arguments:
- acts_in: bfloat16 [4, 1, 1536, 2560], P(None, 'dp')
- layer_kind: int32 [4, 1], P('pp')
- w_q: bfloat16 [4, 1, 2560, 2048], P('pp', None, None, 'tp')
- w_k: bfloat16 [4, 1, 2560, 1024], P('pp', None, None, 'tp')
- w_v: bfloat16 [4, 1, 2560, 1024], P('pp', None, None, 'tp')
- w_o: bfloat16 [4, 1, 2048, 2560], P('pp', None, 'tp')
- w_gate: bfloat16 [4, 1, 2560, 10240], P('pp', None, None, 'tp')
- w_up: bfloat16 [4, 1, 2560, 10240], P('pp', None, None, 'tp')
- w_down: bfloat16 [4, 1, 10240, 2560], P('pp', None, 'tp')
- norm_gains: float32 [4, 1, 4, 2560], P('pp')
- qk_gains: float32 [4, 1, 2, 256], P('pp')
Outputs:
- output: bfloat16 [4, 1, 1536, 2560], P(None, 'dp', 'pp')
All inputs are finite; a program needn't handle non-finite values.
Results may differ from a plain program's by a relative error of at most 0.02.
Values are sent between devices in bfloat16 or wider.
A program may use at most 1 GiB of HBM per device.

v0:
```python
import jax
import jax.numpy as jnp
from jax import lax
from jax.sharding import PartitionSpec as P

WINDOW = 1024
QBLOCK = 256
MLP_ROWS = 512
EPS = 1e-6
LOCAL_BASE = 10000.0
GLOBAL_BASE = 1000000.0
GLOBAL_POS_SCALE = 0.125


def rms_norm(x, gain_vec):
    x_f32 = x.astype(jnp.float32)
    mean_sq = jnp.mean(x_f32 * x_f32, axis=-1, keepdims=True)
    return (x_f32 * lax.rsqrt(mean_sq + EPS) * (1.0 + gain_vec)).astype(jnp.bfloat16)


def rope_tables(kind_val, seq_len, head_dim):
    is_glob = kind_val == 1
    expo_vec = jnp.arange(head_dim // 2, dtype=jnp.float32) * (-2.0 / head_dim)
    inv_freq = jnp.power(jnp.where(is_glob, GLOBAL_BASE, LOCAL_BASE).astype(jnp.float32), expo_vec)
    positions = jnp.arange(seq_len, dtype=jnp.float32) * jnp.where(is_glob, GLOBAL_POS_SCALE, 1.0).astype(jnp.float32)
    angles = positions[:, None] * inv_freq[None, :]
    return jnp.cos(angles), jnp.sin(angles)


def norm_rope(heads_in, gain_vec, cos_tab, sin_tab):
    x_f32 = heads_in.astype(jnp.float32)
    mean_sq = jnp.mean(x_f32 * x_f32, axis=-1, keepdims=True)
    x_f32 = x_f32 * lax.rsqrt(mean_sq + EPS) * (1.0 + gain_vec)
    half_dim = heads_in.shape[-1] // 2
    cos_b = cos_tab[None, :, None, :]
    sin_b = sin_tab[None, :, None, :]
    lo_half = x_f32[..., :half_dim]
    hi_half = x_f32[..., half_dim:]
    return jnp.concatenate([lo_half * cos_b - hi_half * sin_b, hi_half * cos_b + lo_half * sin_b], axis=-1).astype(jnp.bfloat16)


def attend_block(q_blk, k_win, v_win, q_pos, k_pos, span_max, q_scale):
    scores = jnp.einsum('bqkgd,btkd->bkgqt', q_blk, k_win, preferred_element_type=jnp.float32) * q_scale
    q_minus_k = q_pos[:, None] - k_pos[None, :]
    allowed = (q_minus_k >= 0) & (q_minus_k < span_max)
    scores = jnp.where(allowed, scores, -1e30)
    row_max = jnp.max(scores, axis=-1, keepdims=True)
    exp_val = jnp.exp(scores - row_max)
    prob_bf = (exp_val / jnp.sum(exp_val, axis=-1, keepdims=True)).astype(jnp.bfloat16)
    blk_out = jnp.einsum('bkgqt,btkd->bqkgd', prob_bf, v_win, preferred_element_type=jnp.float32)
    return blk_out.astype(jnp.bfloat16)


def attention(q_rot, k_rot, v_heads, kind_val, q_scale):
    seq_len = q_rot.shape[1]
    win_len = WINDOW + QBLOCK
    blk_list = jnp.arange(seq_len // QBLOCK)

    def glob_block(blk_idx):
        q_start = blk_idx * QBLOCK
        q_blk = lax.dynamic_slice_in_dim(q_rot, q_start, QBLOCK, axis=1)
        q_pos = q_start + jnp.arange(QBLOCK)
        return attend_block(q_blk, k_rot, v_heads, q_pos, jnp.arange(seq_len), seq_len, q_scale)

    def loc_block(blk_idx):
        q_start = blk_idx * QBLOCK
        q_blk = lax.dynamic_slice_in_dim(q_rot, q_start, QBLOCK, axis=1)
        q_pos = q_start + jnp.arange(QBLOCK)
        k_start = jnp.maximum(q_start - WINDOW, 0)
        k_win = lax.dynamic_slice_in_dim(k_rot, k_start, win_len, axis=1)
        v_win = lax.dynamic_slice_in_dim(v_heads, k_start, win_len, axis=1)
        return attend_block(q_blk, k_win, v_win, q_pos, k_start + jnp.arange(win_len), WINDOW, q_scale)

    blocks = lax.cond(kind_val == 1, lambda ids_in: lax.map(glob_block, ids_in), lambda ids_in: lax.map(loc_block, ids_in), blk_list)
    return jnp.moveaxis(blocks, 0, 1).reshape(q_rot.shape)


def mlp_rows(h_rows, w_gate, w_up, w_down):
    gate_f = jnp.dot(h_rows, w_gate, preferred_element_type=jnp.float32)
    up_f = jnp.dot(h_rows, w_up, preferred_element_type=jnp.float32)
    act_bf = (jax.nn.gelu(gate_f, approximate=True) * up_f).astype(jnp.bfloat16)
    return jnp.dot(act_bf, w_down, preferred_element_type=jnp.float32).astype(jnp.bfloat16)


def layer_fwd(hidden, params, kind_val, q_scale):
    w_q, w_k, w_v, w_o, w_gate, w_up, w_down, norm_gains, qk_gains = params
    batch_n, seq_len, d_model = hidden.shape
    head_dim = qk_gains.shape[-1]
    q_heads = w_q.shape[-1] // head_dim
    kv_heads = w_k.shape[-1] // head_dim
    h_in = rms_norm(hidden, norm_gains[0])
    q_proj = jnp.einsum('bsd,dn->bsn', h_in, w_q, preferred_element_type=jnp.float32).astype(jnp.bfloat16)
    k_proj = jnp.einsum('bsd,dn->bsn', h_in, w_k, preferred_element_type=jnp.float32).astype(jnp.bfloat16)
    v_proj = jnp.einsum('bsd,dn->bsn', h_in, w_v, preferred_element_type=jnp.float32).astype(jnp.bfloat16)
    cos_tab, sin_tab = rope_tables(kind_val, seq_len, head_dim)
    q_rot = norm_rope(q_proj.reshape(batch_n, seq_len, q_heads, head_dim), qk_gains[0], cos_tab, sin_tab)
    k_rot = norm_rope(k_proj.reshape(batch_n, seq_len, kv_heads, head_dim), qk_gains[1], cos_tab, sin_tab)
    q_rot = q_rot.reshape(batch_n, seq_len, kv_heads, q_heads // kv_heads, head_dim)
    v_heads = v_proj.reshape(batch_n, seq_len, kv_heads, head_dim)
    attn_out = attention(q_rot, k_rot, v_heads, kind_val, q_scale).reshape(batch_n, seq_len, q_heads * head_dim)
    o_part = jnp.einsum('bsn,nd->bsd', attn_out, w_o, preferred_element_type=jnp.float32).astype(jnp.bfloat16)
    hidden = hidden + rms_norm(lax.psum(o_part, 'tp'), norm_gains[1])
    h_mid = rms_norm(hidden, norm_gains[2]).reshape(batch_n * seq_len // MLP_ROWS, MLP_ROWS, d_model)
    d_part = lax.map(lambda rows_in: mlp_rows(rows_in, w_gate, w_up, w_down), h_mid).reshape(batch_n, seq_len, d_model)
    return hidden + rms_norm(lax.psum(d_part, 'tp'), norm_gains[3])


def spread_sequence(collected, stage_idx, n_stages):
    last_stage = n_stages - 1
    piece_len = collected.shape[2] // n_stages
    own_piece = collected[:, :, last_stage * piece_len:]
    result = jnp.where(stage_idx == last_stage, own_piece, jnp.zeros_like(own_piece))
    for target in range(last_stage):
        got_piece = lax.ppermute(collected[:, :, target * piece_len:(target + 1) * piece_len], 'pp', [(last_stage, target)])
        result = result + got_piece
    return result


def solution(mesh):
    n_stages = mesh.shape['pp']
    last_stage = n_stages - 1
    fwd_perm = [(src_idx, src_idx + 1) for src_idx in range(last_stage)]
    col_split = P('pp', None, None, 'tp')
    row_split = P('pp', None, 'tp', None)
    stage_only = P('pp', None, None, None)
    in_specs = (P(None, 'dp', None, None), P('pp', None), col_split, col_split, col_split, row_split, col_split, col_split, row_split, stage_only, stage_only)
    out_spec = P(None, 'dp', 'pp', None)

    def run_all(acts_in, layer_kind, w_q, w_k, w_v, w_o, w_gate, w_up, w_down, norm_gains, qk_gains):
        head_dim = qk_gains.shape[-1]
        q_heads = w_q.shape[-1] // head_dim
        query_pre = acts_in.shape[-1] // q_heads if head_dim == 128 else head_dim
        q_scale = query_pre ** -0.5

        def device_fn(acts_loc, kind_loc, wq_loc, wk_loc, wv_loc, wo_loc, wg_loc, wu_loc, wd_loc, gain_loc, qk_loc):
            weights = (wq_loc, wk_loc, wv_loc, wo_loc, wg_loc, wu_loc, wd_loc, gain_loc, qk_loc)
            stage_idx = lax.axis_index('pp')
            n_micro = acts_loc.shape[0]
            kind_row = kind_loc[0]

            def stage_layers(hidden):
                for layer_idx in range(kind_row.shape[0]):
                    hidden = layer_fwd(hidden, [w_arr[0, layer_idx] for w_arr in weights], kind_row[layer_idx], q_scale)
                return hidden

            def time_step(t_idx, loop_state):
                from_prev, collected = loop_state
                micro_idx = t_idx - stage_idx
                is_valid = (micro_idx >= 0) & (micro_idx < n_micro)
                first_in = lax.dynamic_index_in_dim(acts_loc, jnp.minimum(t_idx, n_micro - 1), axis=0, keepdims=False)
                stage_in = jnp.where(stage_idx == 0, first_in, from_prev)
                stage_out = stage_layers(stage_in)
                out_slot = jnp.clip(micro_idx, 0, n_micro - 1)
                old_val = lax.dynamic_index_in_dim(collected, out_slot, axis=0, keepdims=False)
                keep_new = is_valid & (stage_idx == last_stage)
                collected = lax.dynamic_update_index_in_dim(collected, jnp.where(keep_new, stage_out, old_val), out_slot, 0)
                return lax.ppermute(stage_out, 'pp', fwd_perm), collected

            init_state = (jnp.zeros_like(acts_loc[0]), jnp.zeros_like(acts_loc))
            collected = lax.fori_loop(0, n_micro + last_stage, time_step, init_state)[1]
            return spread_sequence(collected, stage_idx, n_stages)

        return jax.shard_map(device_fn, mesh=mesh, in_specs=in_specs, out_specs=out_spec, check_vma=False)(acts_in, layer_kind, w_q, w_k, w_v, w_o, w_gate, w_up, w_down, norm_gains, qk_gains)

    return run_all
```

profile of v0, /device:TPU:1, one launch (start us, length us, event | category | flops | bytes accessed | tf_op | source)
XLA Modules:
  0.0 5926.9 jit_solution(2401544420435373596)
XLA Ops:
  21.4 5779.8 %while.68 = (s32[]{:T(128)}, bf16[1,1536,2560]{2,1,0:T(8,128)(2,1)}, bf16[4,1,1536,2560]{3,2,1,0:T(8,128)(2,1)}, pred[]{:T(512)}, bf16[4,1,1536,2560]{3,2,1,0:T(...) while((s32[]{:T(128)}, ...), condition=%wide.region_21.22_spmd, body=%wide.region_0.21_spmd.sunk | while | flops 66300633088 | bytes 717793856 | solution.py:160
  81.9 55.4 conditional.2
  81.9 49.0 while.64
  150.8 190.2 %all-reduce.3.cloned.1.call-done = bf16[1,1536,2560]{2,1,0:T(8,128)(2,1)} async-done(((bf16[1,1536,2560]{2,1,0:T(8,128)(2,1)}), bf16[1,1536,2560]{2,1,0:T(8,128)(2,1)}) %all-reduce.3.cloned.1.call-update) | async-done | bytes 7864336 | tf_op jit(solution)/shard_map/while/body/eval_jaxpr/psum | solution.py:102
  359.1 199.8 %while.69 = (s32[]{:T(128)}, bf16[3,512,2560]{2,1,0:T(8,128)(2,1)}, bf16[3,512,2560]{2,1,0:T(8,128)(2,1)}, bf16[2560,5120]{1,0:T(8,128)(2,1)}, bf16[2560,5120]{1...) while((s32[]{:T(128)}, bf16[3,512,2560]{2,1,0:T(8,128)(2,1)}, bf16[3,512,2560]{2,1,0:T(8,128)(2,1)}, ...), condition=%wide.region_18.18_spmd, body=%wide.region_17.17_spmd.sunk | while | flops 40292843520 | bytes 117964896 | solution.py:104
  447.5 23.6 fusion.56.clone.12
  565.9 174.5 %all-reduce.5.cloned.1.call-done = bf16[1,1536,2560]{2,1,0:T(8,128)(2,1)} async-done(((bf16[1,1536,2560]{2,1,0:T(8,128)(2,1)}), bf16[1,1536,2560]{2,1,0:T(8,128)(2,1)}) %all-reduce.5.cloned.1.call-update) | async-done | bytes 7864336 | tf_op jit(solution)/shard_map/while/body/eval_jaxpr/psum | solution.py:105
  762.7 84.7 %collective-permute-done = bf16[1,1536,2560]{2,1,0:T(8,128)(2,1)} collective-permute-done((bf16[1,1536,2560]{2,1,0:T(8,128)(2,1)}, bf16[1,1536,2560]{2,1,0:T(8,128)(2,1)}, u32[]{:S(2)}, u32[]{:S(2)}) %collective-permute-start) | collective-permute-done | bytes 7864352 | tf_op jit(solution)/shard_map/while/body/eval_jaxpr/ppermute | solution.py:157
  908.1 55.4 conditional.2
  908.1 49.0 while.64
  977.0 189.1 %all-reduce.3.cloned.1.call-done = bf16[1,1536,2560]{2,1,0:T(8,128)(2,1)} async-done(((bf16[1,1536,2560]{2,1,0:T(8,128)(2,1)}), bf16[1,1536,2560]{2,1,0:T(8,128)(2,1)}) %all-reduce.3.cloned.1.call-update) | async-done | bytes 7864336 | tf_op jit(solution)/shard_map/while/body/eval_jaxpr/psum | solution.py:102
  1184.2 199.8 %while.69 = (s32[]{:T(128)}, bf16[3,512,2560]{2,1,0:T(8,128)(2,1)}, bf16[3,512,2560]{2,1,0:T(8,128)(2,1)}, bf16[2560,5120]{1,0:T(8,128)(2,1)}, bf16[2560,5120]{1...) while((s32[]{:T(128)}, bf16[3,512,2560]{2,1,0:T(8,128)(2,1)}, bf16[3,512,2560]{2,1,0:T(8,128)(2,1)}, ...), condition=%wide.region_18.18_spmd, body=%wide.region_17.17_spmd.sunk | while | flops 40292843520 | bytes 117964896 | solution.py:104
  1272.7 23.6 fusion.56.clone.12
  1391.1 174.5 %all-reduce.5.cloned.1.call-done = bf16[1,1536,2560]{2,1,0:T(8,128)(2,1)} async-done(((bf16[1,1536,2560]{2,1,0:T(8,128)(2,1)}), bf16[1,1536,2560]{2,1,0:T(8,128)(2,1)}) %all-reduce.5.cloned.1.call-update) | async-done | bytes 7864336 | tf_op jit(solution)/shard_map/while/body/eval_jaxpr/psum | solution.py:105
  1587.8 84.7 %collective-permute-done = bf16[1,1536,2560]{2,1,0:T(8,128)(2,1)} collective-permute-done((bf16[1,1536,2560]{2,1,0:T(8,128)(2,1)}, bf16[1,1536,2560]{2,1,0:T(8,128)(2,1)}, u32[]{:S(2)}, u32[]{:S(2)}) %collective-permute-start) | collective-permute-done | bytes 7864352 | tf_op jit(solution)/shard_map/while/body/eval_jaxpr/ppermute | solution.py:157
  1733.2 55.4 conditional.2
  1733.2 49.0 while.64
  1802.2 189.1 %all-reduce.3.cloned.1.call-done = bf16[1,1536,2560]{2,1,0:T(8,128)(2,1)} async-done(((bf16[1,1536,2560]{2,1,0:T(8,128)(2,1)}), bf16[1,1536,2560]{2,1,0:T(8,128)(2,1)}) %all-reduce.3.cloned.1.call-update) | async-done | bytes 7864336 | tf_op jit(solution)/shard_map/while/body/eval_jaxpr/psum | solution.py:102
  2009.4 199.8 %while.69 = (s32[]{:T(128)}, bf16[3,512,2560]{2,1,0:T(8,128)(2,1)}, bf16[3,512,2560]{2,1,0:T(8,128)(2,1)}, bf16[2560,5120]{1,0:T(8,128)(2,1)}, bf16[2560,5120]{1...) while((s32[]{:T(128)}, bf16[3,512,2560]{2,1,0:T(8,128)(2,1)}, bf16[3,512,2560]{2,1,0:T(8,128)(2,1)}, ...), condition=%wide.region_18.18_spmd, body=%wide.region_17.17_spmd.sunk | while | flops 40292843520 | bytes 117964896 | solution.py:104
  2216.2 174.5 %all-reduce.5.cloned.1.call-done = bf16[1,1536,2560]{2,1,0:T(8,128)(2,1)} async-done(((bf16[1,1536,2560]{2,1,0:T(8,128)(2,1)}), bf16[1,1536,2560]{2,1,0:T(8,128)(2,1)}) %all-reduce.5.cloned.1.call-update) | async-done | bytes 7864336 | tf_op jit(solution)/shard_map/while/body/eval_jaxpr/psum | solution.py:105
  2413.0 84.7 %collective-permute-done = bf16[1,1536,2560]{2,1,0:T(8,128)(2,1)} collective-permute-done((bf16[1,1536,2560]{2,1,0:T(8,128)(2,1)}, bf16[1,1536,2560]{2,1,0:T(8,128)(2,1)}, u32[]{:S(2)}, u32[]{:S(2)}) %collective-permute-start) | collective-permute-done | bytes 7864352 | tf_op jit(solution)/shard_map/while/body/eval_jaxpr/ppermute | solution.py:157
  2558.4 55.4 conditional.2
  2558.4 49.0 while.64
  2627.3 189.1 %all-reduce.3.cloned.1.call-done = bf16[1,1536,2560]{2,1,0:T(8,128)(2,1)} async-done(((bf16[1,1536,2560]{2,1,0:T(8,128)(2,1)}), bf16[1,1536,2560]{2,1,0:T(8,128)(2,1)}) %all-reduce.3.cloned.1.call-update) | async-done | bytes 7864336 | tf_op jit(solution)/shard_map/while/body/eval_jaxpr/psum | solution.py:102
  2834.5 199.8 %while.69 = (s32[]{:T(128)}, bf16[3,512,2560]{2,1,0:T(8,128)(2,1)}, bf16[3,512,2560]{2,1,0:T(8,128)(2,1)}, bf16[2560,5120]{1,0:T(8,128)(2,1)}, bf16[2560,5120]{1...) while((s32[]{:T(128)}, bf16[3,512,2560]{2,1,0:T(8,128)(2,1)}, bf16[3,512,2560]{2,1,0:T(8,128)(2,1)}, ...), condition=%wide.region_18.18_spmd, body=%wide.region_17.17_spmd.sunk | while | flops 40292843520 | bytes 117964896 | solution.py:104
  2923.0 23.6 fusion.56.clone.12
  3041.4 174.5 %all-reduce.5.cloned.1.call-done = bf16[1,1536,2560]{2,1,0:T(8,128)(2,1)} async-done(((bf16[1,1536,2560]{2,1,0:T(8,128)(2,1)}), bf16[1,1536,2560]{2,1,0:T(8,128)(2,1)}) %all-reduce.5.cloned.1.call-update) | async-done | bytes 7864336 | tf_op jit(solution)/shard_map/while/body/eval_jaxpr/psum | solution.py:105
  3238.1 84.7 %collective-permute-done = bf16[1,1536,2560]{2,1,0:T(8,128)(2,1)} collective-permute-done((bf16[1,1536,2560]{2,1,0:T(8,128)(2,1)}, bf16[1,1536,2560]{2,1,0:T(8,128)(2,1)}, u32[]{:S(2)}, u32[]{:S(2)}) %collective-permute-start) | collective-permute-done | bytes 7864352 | tf_op jit(solution)/shard_map/while/body/eval_jaxpr/ppermute | solution.py:157
  3383.5 55.4 conditional.2
  3383.5 49.0 while.64
  3452.5 189.1 %all-reduce.3.cloned.1.call-done = bf16[1,1536,2560]{2,1,0:T(8,128)(2,1)} async-done(((bf16[1,1536,2560]{2,1,0:T(8,128)(2,1)}), bf16[1,1536,2560]{2,1,0:T(8,128)(2,1)}) %all-reduce.3.cloned.1.call-update) | async-done | bytes 7864336 | tf_op jit(solution)/shard_map/while/body/eval_jaxpr/psum | solution.py:102
  3659.7 199.8 %while.69 = (s32[]{:T(128)}, bf16[3,512,2560]{2,1,0:T(8,128)(2,1)}, bf16[3,512,2560]{2,1,0:T(8,128)(2,1)}, bf16[2560,5120]{1,0:T(8,128)(2,1)}, bf16[2560,5120]{1...) while((s32[]{:T(128)}, bf16[3,512,2560]{2,1,0:T(8,128)(2,1)}, bf16[3,512,2560]{2,1,0:T(8,128)(2,1)}, ...), condition=%wide.region_18.18_spmd, body=%wide.region_17.17_spmd.sunk | while | flops 40292843520 | bytes 117964896 | solution.py:104
  3866.5 174.5 %all-reduce.5.cloned.1.call-done = bf16[1,1536,2560]{2,1,0:T(8,128)(2,1)} async-done(((bf16[1,1536,2560]{2,1,0:T(8,128)(2,1)}), bf16[1,1536,2560]{2,1,0:T(8,128)(2,1)}) %all-reduce.5.cloned.1.call-update) | async-done | bytes 7864336 | tf_op jit(solution)/shard_map/while/body/eval_jaxpr/psum | solution.py:105
  4063.3 84.7 %collective-permute-done = bf16[1,1536,2560]{2,1,0:T(8,128)(2,1)} collective-permute-done((bf16[1,1536,2560]{2,1,0:T(8,128)(2,1)}, bf16[1,1536,2560]{2,1,0:T(8,128)(2,1)}, u32[]{:S(2)}, u32[]{:S(2)}) %collective-permute-start) | collective-permute-done | bytes 7864352 | tf_op jit(solution)/shard_map/while/body/eval_jaxpr/ppermute | solution.py:157
  4208.7 55.4 conditional.2
  4208.7 49.0 while.64
  4277.7 189.1 %all-reduce.3.cloned.1.call-done = bf16[1,1536,2560]{2,1,0:T(8,128)(2,1)} async-done(((bf16[1,1536,2560]{2,1,0:T(8,128)(2,1)}), bf16[1,1536,2560]{2,1,0:T(8,128)(2,1)}) %all-reduce.3.cloned.1.call-update) | async-done | bytes 7864336 | tf_op jit(solution)/shard_map/while/body/eval_jaxpr/psum | solution.py:102
  4484.9 199.8 %while.69 = (s32[]{:T(128)}, bf16[3,512,2560]{2,1,0:T(8,128)(2,1)}, bf16[3,512,2560]{2,1,0:T(8,128)(2,1)}, bf16[2560,5120]{1,0:T(8,128)(2,1)}, bf16[2560,5120]{1...) while((s32[]{:T(128)}, bf16[3,512,2560]{2,1,0:T(8,128)(2,1)}, bf16[3,512,2560]{2,1,0:T(8,128)(2,1)}, ...), condition=%wide.region_18.18_spmd, body=%wide.region_17.17_spmd.sunk | while | flops 40292843520 | bytes 117964896 | solution.py:104
  4573.3 23.6 fusion.56.clone.12
  4691.7 174.5 %all-reduce.5.cloned.1.call-done = bf16[1,1536,2560]{2,1,0:T(8,128)(2,1)} async-done(((bf16[1,1536,2560]{2,1,0:T(8,128)(2,1)}), bf16[1,1536,2560]{2,1,0:T(8,128)(2,1)}) %all-reduce.5.cloned.1.call-update) | async-done | bytes 7864336 | tf_op jit(solution)/shard_map/while/body/eval_jaxpr/psum | solution.py:105
  4888.5 84.7 %collective-permute-done = bf16[1,1536,2560]{2,1,0:T(8,128)(2,1)} collective-permute-done((bf16[1,1536,2560]{2,1,0:T(8,128)(2,1)}, bf16[1,1536,2560]{2,1,0:T(8,128)(2,1)}, u32[]{:S(2)}, u32[]{:S(2)}) %collective-permute-start) | collective-permute-done | bytes 7864352 | tf_op jit(solution)/shard_map/while/body/eval_jaxpr/ppermute | solution.py:157
  5033.9 55.4 conditional.2
  5033.9 49.0 while.64
  5102.8 189.1 %all-reduce.3.cloned.1.call-done = bf16[1,1536,2560]{2,1,0:T(8,128)(2,1)} async-done(((bf16[1,1536,2560]{2,1,0:T(8,128)(2,1)}), bf16[1,1536,2560]{2,1,0:T(8,128)(2,1)}) %all-reduce.3.cloned.1.call-update) | async-done | bytes 7864336 | tf_op jit(solution)/shard_map/while/body/eval_jaxpr/psum | solution.py:102
  5310.1 199.8 %while.69 = (s32[]{:T(128)}, bf16[3,512,2560]{2,1,0:T(8,128)(2,1)}, bf16[3,512,2560]{2,1,0:T(8,128)(2,1)}, bf16[2560,5120]{1,0:T(8,128)(2,1)}, bf16[2560,5120]{1...) while((s32[]{:T(128)}, bf16[3,512,2560]{2,1,0:T(8,128)(2,1)}, bf16[3,512,2560]{2,1,0:T(8,128)(2,1)}, ...), condition=%wide.region_18.18_spmd, body=%wide.region_17.17_spmd.sunk | while | flops 40292843520 | bytes 117964896 | solution.py:104
  5516.9 174.5 %all-reduce.5.cloned.1.call-done = bf16[1,1536,2560]{2,1,0:T(8,128)(2,1)} async-done(((bf16[1,1536,2560]{2,1,0:T(8,128)(2,1)}), bf16[1,1536,2560]{2,1,0:T(8,128)(2,1)}) %all-reduce.5.cloned.1.call-update) | async-done | bytes 7864336 | tf_op jit(solution)/shard_map/while/body/eval_jaxpr/psum | solution.py:105
  5713.7 84.7 %collective-permute-done = bf16[1,1536,2560]{2,1,0:T(8,128)(2,1)} collective-permute-done((bf16[1,1536,2560]{2,1,0:T(8,128)(2,1)}, bf16[1,1536,2560]{2,1,0:T(8,128)(2,1)}, u32[]{:S(2)}, u32[]{:S(2)}) %collective-permute-start) | collective-permute-done | bytes 7864352 | tf_op jit(solution)/shard_map/while/body/eval_jaxpr/ppermute | solution.py:157
  5816.1 94.8 %collective-permute-done.2 = bf16[4,1,384,2560]{3,2,1,0:T(8,128)(2,1)} collective-permute-done((bf16[4,1,384,2560]{3,2,1,0:T(8,128)(2,1)S(1)}, bf16[4,1,384,2560]{3,2,1,0:T(8,128)(2,1)}, u32[]{:S(2)}, u32[]{:S(2)}) %collective-permute-start.2) | collective-permute-done | bytes 7864352 | tf_op jit(solution)/shard_map/ppermute | solution.py:114
  (999 shorter events, 2542.8 us)
Async XLA Ops:
  21.4 319.6 %all-reduce.3.cloned.1.call-start = ((), (), s32[]{:S(2)}) async-start(), calls=%async_computation | async-start | bytes 15728640 | tf_op jit(solution)/shard_map/while/body/eval_jaxpr/psum | solution.py:102
  26.8 10.7 copy-start.4
  26.8 10.7 copy-start.6
  150.7 195.3 %copy-start.16 = (f32[2560]{0:T(1024)S(1)}, f32[2560]{0:T(1024)}, u32[]{:S(2)}) copy-start(f32[2560]{0:T(1024)} %get-tuple-element.892) | copy-start | bytes 30724 | tf_op jit(solution)/shard_map/while
  150.8 589.7 %all-reduce.5.cloned.1.call-start = ((), (), s32[]{:S(2)}) async-start(), calls=%async_computation.1 | async-start | bytes 15728640 | tf_op jit(solution)/shard_map/while/body/eval_jaxpr/psum | solution.py:105
  565.9 179.5 %copy-start.14 = (f32[2560]{0:T(1024)S(1)}, f32[2560]{0:T(1024)}, u32[]{:S(2)}) copy-start(f32[2560]{0:T(1024)} %get-tuple-element.907) | copy-start | bytes 30724 | tf_op jit(solution)/shard_map/while
  758.8 88.6 %collective-permute-start = (bf16[1,1536,2560]{2,1,0:T(8,128)(2,1)}, bf16[1,1536,2560]{2,1,0:T(8,128)(2,1)}, u32[]{:S(2)}, u32[]{:S(2)}) collective-permute-start(bf16[1,1536,2560]{2,1,0:T(8,128)(2,1)} %get-tuple-element.911), channel_id=1, source_target_pairs={{0,1},{1,2},{2,3},{4,5},{5,6},{6,7}} | collective-permute-start | bytes 23592968 | tf_op jit(solution)/shard_map/while/body/eval_jaxpr/ppermute | solution.py:157
  847.6 318.5 %all-reduce.3.cloned.1.call-start = ((), (), s32[]{:S(2)}) async-start(), calls=%async_computation | async-start | bytes 15728640 | tf_op jit(solution)/shard_map/while/body/eval_jaxpr/psum | solution.py:102
  853.1 10.6 copy-start.4
  853.1 10.6 copy-start.6
  976.9 194.2 %copy-start.16 = (f32[2560]{0:T(1024)S(1)}, f32[2560]{0:T(1024)}, u32[]{:S(2)}) copy-start(f32[2560]{0:T(1024)} %get-tuple-element.892) | copy-start | bytes 30724 | tf_op jit(solution)/shard_map/while
  977.0 588.6 %all-reduce.5.cloned.1.call-start = ((), (), s32[]{:S(2)}) async-start(), calls=%async_computation.1 | async-start | bytes 15728640 | tf_op jit(solution)/shard_map/while/body/eval_jaxpr/psum | solution.py:105
  1391.1 179.5 %copy-start.14 = (f32[2560]{0:T(1024)S(1)}, f32[2560]{0:T(1024)}, u32[]{:S(2)}) copy-start(f32[2560]{0:T(1024)} %get-tuple-element.907) | copy-start | bytes 30724 | tf_op jit(solution)/shard_map/while
  1583.9 88.6 %collective-permute-start = (bf16[1,1536,2560]{2,1,0:T(8,128)(2,1)}, bf16[1,1536,2560]{2,1,0:T(8,128)(2,1)}, u32[]{:S(2)}, u32[]{:S(2)}) collective-permute-start(bf16[1,1536,2560]{2,1,0:T(8,128)(2,1)} %get-tuple-element.911), channel_id=1, source_target_pairs={{0,1},{1,2},{2,3},{4,5},{5,6},{6,7}} | collective-permute-start | bytes 23592968 | tf_op jit(solution)/shard_map/while/body/eval_jaxpr/ppermute | solution.py:157
  1672.8 318.5 %all-reduce.3.cloned.1.call-start = ((), (), s32[]{:S(2)}) async-start(), calls=%async_computation | async-start | bytes 15728640 | tf_op jit(solution)/shard_map/while/body/eval_jaxpr/psum | solution.py:102
  1802.1 194.2 %copy-start.16 = (f32[2560]{0:T(1024)S(1)}, f32[2560]{0:T(1024)}, u32[]{:S(2)}) copy-start(f32[2560]{0:T(1024)} %get-tuple-element.892) | copy-start | bytes 30724 | tf_op jit(solution)/shard_map/while
  1802.1 588.6 %all-reduce.5.cloned.1.call-start = ((), (), s32[]{:S(2)}) async-start(), calls=%async_computation.1 | async-start | bytes 15728640 | tf_op jit(solution)/shard_map/while/body/eval_jaxpr/psum | solution.py:105
  2216.2 179.5 %copy-start.14 = (f32[2560]{0:T(1024)S(1)}, f32[2560]{0:T(1024)}, u32[]{:S(2)}) copy-start(f32[2560]{0:T(1024)} %get-tuple-element.907) | copy-start | bytes 30724 | tf_op jit(solution)/shard_map/while
  2409.0 88.7 %collective-permute-start = (bf16[1,1536,2560]{2,1,0:T(8,128)(2,1)}, bf16[1,1536,2560]{2,1,0:T(8,128)(2,1)}, u32[]{:S(2)}, u32[]{:S(2)}) collective-permute-start(bf16[1,1536,2560]{2,1,0:T(8,128)(2,1)} %get-tuple-element.911), channel_id=1, source_target_pairs={{0,1},{1,2},{2,3},{4,5},{5,6},{6,7}} | collective-permute-start | bytes 23592968 | tf_op jit(solution)/shard_map/while/body/eval_jaxpr/ppermute | solution.py:157
  2497.9 318.5 %all-reduce.3.cloned.1.call-start = ((), (), s32[]{:S(2)}) async-start(), calls=%async_computation | async-start | bytes 15728640 | tf_op jit(solution)/shard_map/while/body/eval_jaxpr/psum | solution.py:102
  2503.4 10.6 copy-start.4
  2503.4 10.6 copy-start.6
  2627.3 194.2 %copy-start.16 = (f32[2560]{0:T(1024)S(1)}, f32[2560]{0:T(1024)}, u32[]{:S(2)}) copy-start(f32[2560]{0:T(1024)} %get-tuple-element.892) | copy-start | bytes 30724 | tf_op jit(solution)/shard_map/while
  2627.3 588.6 %all-reduce.5.cloned.1.call-start = ((), (), s32[]{:S(2)}) async-start(), calls=%async_computation.1 | async-start | bytes 15728640 | tf_op jit(solution)/shard_map/while/body/eval_jaxpr/psum | solution.py:105
  3041.4 179.5 %copy-start.14 = (f32[2560]{0:T(1024)S(1)}, f32[2560]{0:T(1024)}, u32[]{:S(2)}) copy-start(f32[2560]{0:T(1024)} %get-tuple-element.907) | copy-start | bytes 30724 | tf_op jit(solution)/shard_map/while
  3234.3 88.6 %collective-permute-start = (bf16[1,1536,2560]{2,1,0:T(8,128)(2,1)}, bf16[1,1536,2560]{2,1,0:T(8,128)(2,1)}, u32[]{:S(2)}, u32[]{:S(2)}) collective-permute-start(bf16[1,1536,2560]{2,1,0:T(8,128)(2,1)} %get-tuple-element.911), channel_id=1, source_target_pairs={{0,1},{1,2},{2,3},{4,5},{5,6},{6,7}} | collective-permute-start | bytes 23592968 | tf_op jit(solution)/shard_map/while/body/eval_jaxpr/ppermute | solution.py:157
  3323.1 318.5 %all-reduce.3.cloned.1.call-start = ((), (), s32[]{:S(2)}) async-start(), calls=%async_computation | async-start | bytes 15728640 | tf_op jit(solution)/shard_map/while/body/eval_jaxpr/psum | solution.py:102
  3452.4 194.2 %copy-start.16 = (f32[2560]{0:T(1024)S(1)}, f32[2560]{0:T(1024)}, u32[]{:S(2)}) copy-start(f32[2560]{0:T(1024)} %get-tuple-element.892) | copy-start | bytes 30724 | tf_op jit(solution)/shard_map/while
  3452.4 588.6 %all-reduce.5.cloned.1.call-start = ((), (), s32[]{:S(2)}) async-start(), calls=%async_computation.1 | async-start | bytes 15728640 | tf_op jit(solution)/shard_map/while/body/eval_jaxpr/psum | solution.py:105
  3866.5 179.5 %copy-start.14 = (f32[2560]{0:T(1024)S(1)}, f32[2560]{0:T(1024)}, u32[]{:S(2)}) copy-start(f32[2560]{0:T(1024)} %get-tuple-element.907) | copy-start | bytes 30724 | tf_op jit(solution)/shard_map/while
  4059.4 88.7 %collective-permute-start = (bf16[1,1536,2560]{2,1,0:T(8,128)(2,1)}, bf16[1,1536,2560]{2,1,0:T(8,128)(2,1)}, u32[]{:S(2)}, u32[]{:S(2)}) collective-permute-start(bf16[1,1536,2560]{2,1,0:T(8,128)(2,1)} %get-tuple-element.911), channel_id=1, source_target_pairs={{0,1},{1,2},{2,3},{4,5},{5,6},{6,7}} | collective-permute-start | bytes 23592968 | tf_op jit(solution)/shard_map/while/body/eval_jaxpr/ppermute | solution.py:157
  4148.3 318.5 %all-reduce.3.cloned.1.call-start = ((), (), s32[]{:S(2)}) async-start(), calls=%async_computation | async-start | bytes 15728640 | tf_op jit(solution)/shard_map/while/body/eval_jaxpr/psum | solution.py:102
  4153.7 10.6 copy-start.4
  4153.7 10.6 copy-start.6
  4277.6 194.2 %copy-start.16 = (f32[2560]{0:T(1024)S(1)}, f32[2560]{0:T(1024)}, u32[]{:S(2)}) copy-start(f32[2560]{0:T(1024)} %get-tuple-element.892) | copy-start | bytes 30724 | tf_op jit(solution)/shard_map/while
  4277.6 588.6 %all-reduce.5.cloned.1.call-start = ((), (), s32[]{:S(2)}) async-start(), calls=%async_computation.1 | async-start | bytes 15728640 | tf_op jit(solution)/shard_map/while/body/eval_jaxpr/psum | solution.py:105
  4691.7 179.5 %copy-start.14 = (f32[2560]{0:T(1024)S(1)}, f32[2560]{0:T(1024)}, u32[]{:S(2)}) copy-start(f32[2560]{0:T(1024)} %get-tuple-element.907) | copy-start | bytes 30724 | tf_op jit(solution)/shard_map/while
  4884.6 88.6 %collective-permute-start = (bf16[1,1536,2560]{2,1,0:T(8,128)(2,1)}, bf16[1,1536,2560]{2,1,0:T(8,128)(2,1)}, u32[]{:S(2)}, u32[]{:S(2)}) collective-permute-start(bf16[1,1536,2560]{2,1,0:T(8,128)(2,1)} %get-tuple-element.911), channel_id=1, source_target_pairs={{0,1},{1,2},{2,3},{4,5},{5,6},{6,7}} | collective-permute-start | bytes 23592968 | tf_op jit(solution)/shard_map/while/body/eval_jaxpr/ppermute | solution.py:157
  4973.5 318.5 %all-reduce.3.cloned.1.call-start = ((), (), s32[]{:S(2)}) async-start(), calls=%async_computation | async-start | bytes 15728640 | tf_op jit(solution)/shard_map/while/body/eval_jaxpr/psum | solution.py:102
  4978.9 10.6 copy-start.4
  4978.9 10.6 copy-start.6
  5102.8 194.2 %copy-start.16 = (f32[2560]{0:T(1024)S(1)}, f32[2560]{0:T(1024)}, u32[]{:S(2)}) copy-start(f32[2560]{0:T(1024)} %get-tuple-element.892) | copy-start | bytes 30724 | tf_op jit(solution)/shard_map/while
  5102.8 588.6 %all-reduce.5.cloned.1.call-start = ((), (), s32[]{:S(2)}) async-start(), calls=%async_computation.1 | async-start | bytes 15728640 | tf_op jit(solution)/shard_map/while/body/eval_jaxpr/psum | solution.py:105
  5516.9 179.5 %copy-start.14 = (f32[2560]{0:T(1024)S(1)}, f32[2560]{0:T(1024)}, u32[]{:S(2)}) copy-start(f32[2560]{0:T(1024)} %get-tuple-element.907) | copy-start | bytes 30724 | tf_op jit(solution)/shard_map/while
  5709.8 88.6 %collective-permute-start = (bf16[1,1536,2560]{2,1,0:T(8,128)(2,1)}, bf16[1,1536,2560]{2,1,0:T(8,128)(2,1)}, u32[]{:S(2)}, u32[]{:S(2)}) collective-permute-start(bf16[1,1536,2560]{2,1,0:T(8,128)(2,1)} %get-tuple-element.911), channel_id=1, source_target_pairs={{0,1},{1,2},{2,3},{4,5},{5,6},{6,7}} | collective-permute-start | bytes 23592968 | tf_op jit(solution)/shard_map/while/body/eval_jaxpr/ppermute | solution.py:157
  5812.4 3.6 collective-permute-start.1
  5813.6 2.5 collective-permute-start.3
  5814.8 96.2 %collective-permute-start.2 = (bf16[4,1,384,2560]{3,2,1,0:T(8,128)(2,1)S(1)}, bf16[4,1,384,2560]{3,2,1,0:T(8,128)(2,1)}, u32[]{:S(2)}, u32[]{:S(2)}) collective-permute-start(bf16[4,1,384,2560]{3,2,1,0:T(8,128)(2,1)S(1)} %get-tuple-element.644), channel_id=1, source_target_pairs={{3,1},{7,5}} | collective-permute-start | bytes 23592968 | tf_op jit(solution)/shard_map/ppermute | solution.py:114
  (95 other events, 420.7 us)
Sparse Core Ops, SparseCore 0:
  150.9 190.0 all-reduce.2
  559.0 181.3 all-reduce.4
  977.1 189.0 all-reduce.2
  1384.2 181.3 all-reduce.4
  1802.2 189.0 all-reduce.2
  2209.4 181.3 all-reduce.4
  2627.4 189.0 all-reduce.2
  3034.5 181.3 all-reduce.4
  3452.5 189.0 all-reduce.2
  3859.7 181.3 all-reduce.4
  4277.7 189.0 all-reduce.2
  4684.9 181.3 all-reduce.4
  5102.9 189.0 all-reduce.2
  5510.0 181.3 all-reduce.4
where the time goes:
time: 5930 us
  waiting for transfers between devices  3230 us (54%)
  matrix products  1860 us (31%)
  other arithmetic  458 us (8%)
  local copies, waits for them, and re-layouts  284 us (5%)
    psum x7, waiting for transfers between devices, layer_fwd(): hidden = hidden + rms_norm(lax.psum(o_part, 'tp'), norm_gains[1])  1320 us
    psum x7, waiting for transfers between devices, layer_fwd(): return hidden + rms_norm(lax.psum(d_part, 'tp'), norm_gains[3])  1220 us
    ppermute x7, waiting for transfers between devices, time_step(): return (lax.ppermute(stage_out, 'pp', fwd_perm), collected)  593 us
    dot_general x21, matrix products, mlp_rows(): up_f = jnp.dot(h_rows, w_up, preferred_element_type=jnp.float32)  494 us
    dot_general x21, matrix products, mlp_rows(): gate_f = jnp.dot(h_rows, w_gate, preferred_element_type=jnp.float32)  457 us
    dot_general x21, matrix products, mlp_rows(): jnp.dot(act_bf, w_down, preferred_element_type=jnp.float32)  445 us
    reduce_sum x28, other arithmetic, rms_norm(): mean_sq = jnp.mean(x_f32 * x_f32, axis=-1, keepdims=True)  174 us
  transfers between devices with their start and end apart: 24, of which 22 were waited for; matrix products, arithmetic and copies ran while one was open for 1% of the time, Pallas kernels for 0%

commit v1 on v0

v1 whole, which is shorter than its diff:
```python
import functools

import jax
import jax.numpy as jnp
from jax import lax
from jax.experimental import pallas as pl
from jax.experimental.pallas import tpu as pltpu
from jax.sharding import PartitionSpec as P


WINDOW = 1024
EPS = 1e-6
LOCAL_BASE = 10000.0
GLOBAL_BASE = 1000000.0
GLOBAL_POS_SCALE = 0.125
CHUNK = 192
LAG = 3
FTILE = 512
KSTEP = 256
NEG = -1e30


def rms_norm(x, gain_vec):
    x_f32 = x.astype(jnp.float32)
    mean_sq = jnp.mean(x_f32 * x_f32, axis=-1, keepdims=True)
    return (x_f32 * lax.rsqrt(mean_sq + EPS) * (1.0 + gain_vec)).astype(jnp.bfloat16)


def rope_tables(kind_val, seq_len, head_dim):
    is_glob = kind_val == 1
    expo_vec = jnp.arange(head_dim // 2, dtype=jnp.float32) * (-2.0 / head_dim)
    inv_freq = jnp.power(jnp.where(is_glob, GLOBAL_BASE, LOCAL_BASE).astype(jnp.float32), expo_vec)
    positions = jnp.arange(seq_len, dtype=jnp.float32) * jnp.where(is_glob, GLOBAL_POS_SCALE, 1.0).astype(jnp.float32)
    angles = positions[:, None] * inv_freq[None, :]
    return jnp.cos(angles), jnp.sin(angles)


def attn_kernel(meta, q_ref, k_ref, v_ref, kc_ref, vc_ref, cos_ref, sin_ref, gain_ref, o_ref, ko_ref, vo_ref, *, n_group, q_scale):
    chunk = meta[1]
    is_glob = meta[2] == 1
    head_dim = k_ref.shape[-1]
    half = head_dim // 2
    rows = k_ref.shape[0]
    cos_b = cos_ref[...]
    sin_b = sin_ref[...]

    def norm_rope(x, gain):
        x = x.astype(jnp.float32)
        mean_sq = jnp.mean(x * x, axis=-1, keepdims=True)
        x = x * lax.rsqrt(mean_sq + EPS) * (1.0 + gain)
        lo = x[:, :half]
        hi = x[:, half:]
        return jnp.concatenate([lo * cos_b - hi * sin_b, hi * cos_b + lo * sin_b], axis=-1).astype(jnp.bfloat16)

    k_new = norm_rope(k_ref[...], gain_ref[1:2, :])
    v_new = v_ref[...]
    ko_ref[0, 0] = k_new
    vo_ref[0, 0] = v_new
    q_all = jnp.concatenate([norm_rope(q_ref[:, g * head_dim:(g + 1) * head_dim], gain_ref[0:1, :]) for g in range(n_group)], axis=0)
    n_rows = n_group * rows
    start = chunk * rows
    span = jnp.where(is_glob, kc_ref.shape[2], WINDOW)
    first = jnp.where(is_glob, 0, jnp.maximum(start - WINDOW, 0))
    first = pl.multiple_of(first, 64)
    n_old = (start - first + KSTEP - 1) // KSTEP

    dims = (((1,), (1,)), ((), ()))
    dims_pv = (((1,), (0,)), ((), ()))
    s_new = lax.dot_general(q_all, k_new, dims, preferred_element_type=jnp.float32) * q_scale
    q_row = lax.rem(lax.broadcasted_iota(jnp.int32, (n_rows, rows), 0), rows)
    k_col = lax.broadcasted_iota(jnp.int32, (n_rows, rows), 1)
    s_new = jnp.where(k_col <= q_row, s_new, NEG)

    def emit(res):
        res = res.astype(jnp.bfloat16)
        for g in range(n_group):
            o_ref[:, g * head_dim:(g + 1) * head_dim] = res[g * rows:(g + 1) * rows]

    @pl.when(n_old == 0)
    def _():
        mx = jnp.max(s_new, axis=-1, keepdims=True)
        e_new = jnp.exp(s_new - mx)
        inv = 1.0 / jnp.sum(e_new, axis=-1, keepdims=True)
        emit(lax.dot_general((e_new * inv).astype(jnp.bfloat16), v_new, dims_pv, preferred_element_type=jnp.float32))

    def with_old(n):
        width = n * KSTEP
        k_old = kc_ref[0, 0, pl.ds(first, width), :]
        v_old = vc_ref[0, 0, pl.ds(first, width), :]
        s_old = lax.dot_general(q_all, k_old, dims, preferred_element_type=jnp.float32) * q_scale
        k_pos = first + lax.broadcasted_iota(jnp.int32, (n_rows, width), 1)
        q_pos = start + lax.rem(lax.broadcasted_iota(jnp.int32, (n_rows, width), 0), rows)
        s_old = jnp.where((k_pos < start) & (q_pos - k_pos < span), s_old, NEG)
        mx = jnp.maximum(jnp.max(s_new, axis=-1, keepdims=True), jnp.max(s_old, axis=-1, keepdims=True))
        e_new = jnp.exp(s_new - mx)
        e_old = jnp.exp(s_old - mx)
        inv = 1.0 / (jnp.sum(e_new, axis=-1, keepdims=True) + jnp.sum(e_old, axis=-1, keepdims=True))
        res = lax.dot_general((e_new * inv).astype(jnp.bfloat16), v_new, dims_pv, preferred_element_type=jnp.float32)
        res = res + lax.dot_general((e_old * inv).astype(jnp.bfloat16), v_old, dims_pv, preferred_element_type=jnp.float32)
        emit(res)

    for n in range(1, kc_ref.shape[2] // KSTEP + 1):
        pl.when(n_old == n)(functools.partial(with_old, n))


def attend(meta, qkv, k_cache, v_cache, cos_tab, sin_tab, gains, q_scale):
    rows = qkv.shape[0]
    _, kv_heads, seq_len, head_dim = k_cache.shape
    n_group = qkv.shape[1] // (kv_heads * head_dim) - 2
    q_cols = n_group * kv_heads
    cache_in = pl.BlockSpec((1, 1, seq_len, head_dim), lambda h, m: (m[0], h, 0, 0))
    cache_out = pl.BlockSpec((1, 1, rows, head_dim), lambda h, m: (m[0], h, m[1], 0))
    table = pl.BlockSpec((rows, head_dim // 2), lambda h, m: (m[1], 0))
    grid_spec = pltpu.PrefetchScalarGridSpec(
        num_scalar_prefetch=1,
        grid=(kv_heads,),
        in_specs=[
            pl.BlockSpec((rows, n_group * head_dim), lambda h, m: (0, h)),
            pl.BlockSpec((rows, head_dim), lambda h, m: (0, q_cols + h)),
            pl.BlockSpec((rows, head_dim), lambda h, m: (0, q_cols + kv_heads + h)),
            cache_in,
            cache_in,
            table,
            table,
            pl.BlockSpec((2, head_dim), lambda h, m: (0, 0)),
        ],
        out_specs=[pl.BlockSpec((rows, n_group * head_dim), lambda h, m: (0, h)), cache_out, cache_out],
    )
    flops = 4 * rows * q_cols * head_dim * 900
    return pl.pallas_call(
        functools.partial(attn_kernel, n_group=n_group, q_scale=q_scale),
        grid_spec=grid_spec,
        out_shape=[
            jax.ShapeDtypeStruct((rows, q_cols * head_dim), jnp.bfloat16),
            jax.ShapeDtypeStruct(k_cache.shape, k_cache.dtype),
            jax.ShapeDtypeStruct(v_cache.shape, v_cache.dtype),
        ],
        input_output_aliases={4: 1, 5: 2},
        compiler_params=pltpu.CompilerParams(vmem_limit_bytes=32 * 2**20, dimension_semantics=("arbitrary",)),
        cost_estimate=pl.CostEstimate(flops=flops, bytes_accessed=8 * 2**20, transcendentals=0),
        name="attend",
    )(meta, qkv, qkv, qkv, k_cache, v_cache, cos_tab, sin_tab, gains)


def mlp_kernel(uo_ref, ux_ref, wg_ref, wu_ref, wd_ref, do_ref, dx_ref, u_all, acc, act):
    step = pl.program_id(0)
    last = pl.num_programs(0) - 1
    rows = uo_ref.shape[0]

    def gate_up():
        gate = jnp.dot(u_all[...], wg_ref[...], preferred_element_type=jnp.float32)
        up = jnp.dot(u_all[...], wu_ref[...], preferred_element_type=jnp.float32)
        return (jax.nn.gelu(gate, approximate=True) * up).astype(jnp.bfloat16)

    def down():
        return jnp.dot(act[...], wd_ref[...], preferred_element_type=jnp.float32)

    @pl.when(step == 0)
    def _():
        u_all[:rows] = uo_ref[...]
        u_all[rows:] = ux_ref[...]
        acc[...] = jnp.zeros_like(acc)
        act[...] = gate_up()

    @pl.when((step > 0) & (step < last))
    def _():
        acc[...] += down()
        act[...] = gate_up()

    @pl.when(step == last)
    def _():
        res = acc[...] + down()
        do_ref[...] = res[:rows]
        dx_ref[...] = res[rows:].astype(jnp.bfloat16)


def mlp(u_own, u_oth, w_gate, w_up, w_down):
    rows, d_model = u_own.shape
    ffn = w_gate.shape[1]
    n_tiles = ffn // FTILE
    whole = pl.BlockSpec((rows, d_model), lambda f: (0, 0))
    col = pl.BlockSpec((d_model, FTILE), lambda f: (0, jnp.minimum(f, n_tiles - 1)))
    row = pl.BlockSpec((FTILE, d_model), lambda f: (jnp.maximum(f - 1, 0), 0))
    return pl.pallas_call(
        mlp_kernel,
        grid=(n_tiles + 1,),
        in_specs=[whole, whole, col, col, row],
        out_specs=[whole, whole],
        out_shape=[jax.ShapeDtypeStruct((rows, d_model), jnp.float32), jax.ShapeDtypeStruct((rows, d_model), jnp.bfloat16)],
        scratch_shapes=[
            pltpu.VMEM((2 * rows, d_model), jnp.bfloat16),
            pltpu.VMEM((2 * rows, d_model), jnp.float32),
            pltpu.VMEM((2 * rows, FTILE), jnp.bfloat16),
        ],
        compiler_params=pltpu.CompilerParams(vmem_limit_bytes=40 * 2**20, dimension_semantics=("arbitrary",)),
        cost_estimate=pl.CostEstimate(flops=12 * rows * d_model * ffn, bytes_accessed=6 * d_model * ffn, transcendentals=0),
        name="mlp",
    )(u_own, u_oth, w_gate, w_up, w_down)


def solution(mesh):
    n_stages = mesh.shape['pp']
    last_stage = n_stages - 1
    col_split = P('pp', None, None, 'tp')
    row_split = P('pp', None, 'tp', None)
    stage_only = P('pp', None, None, None)
    in_specs = (P(None, 'dp', None, None), P('pp', None), col_split, col_split, col_split, row_split, col_split, col_split, row_split, stage_only, stage_only)
    out_spec = P(None, 'dp', 'pp', None)
    axes = ('tp', 'pp')

    def dev(t, s):
        return t * n_stages + s

    def run_all(acts_in, layer_kind, w_q, w_k, w_v, w_o, w_gate, w_up, w_down, norm_gains, qk_gains):
        head_dim = qk_gains.shape[-1]
        q_heads = w_q.shape[-1] // head_dim
        query_pre = acts_in.shape[-1] // q_heads if head_dim == 128 else head_dim
        q_scale = query_pre ** -0.5

        def device_fn(acts_loc, kind_loc, wq_loc, wk_loc, wv_loc, wo_loc, wg_loc, wu_loc, wd_loc, gain_loc, qk_loc):
            side = lax.axis_index('tp')
            stage = lax.axis_index('pp')
            at_first = stage == 0
            n_micro, _, seq_len, d_model = acts_loc.shape
            n_own = n_micro // 2
            n_chunks = seq_len // CHUNK
            n_units = n_own * n_chunks
            kv_heads = wk_loc.shape[-1] // head_dim
            kind_val = kind_loc[0, 0]
            gains = gain_loc[0, 0]
            qk_gain = qk_loc[0, 0]
            w_gate, w_up, w_down = wg_loc[0, 0], wu_loc[0, 0], wd_loc[0, 0]
            f32 = jnp.float32

            def swap(x, stages):
                pairs = [(dev(t, s), dev(1 - t, s)) for s in stages for t in (0, 1)]
                return lax.ppermute(x, axes, pairs)

            wqkv_own = jnp.concatenate([wq_loc[0, 0], wk_loc[0, 0], wv_loc[0, 0]], axis=1)
            wo_own = wo_loc[0, 0]
            later = range(1, n_stages)
            wqkv_oth = jnp.where(at_first, wqkv_own, swap(wqkv_own, later))
            wo_oth = jnp.where(at_first, wo_own, swap(wo_own, later))
            fill = LAG - 1
            cos_tab, sin_tab = rope_tables(kind_val, seq_len, head_dim)
            caches = [jnp.zeros((n_own, kv_heads, seq_len, head_dim), jnp.bfloat16) for _ in range(4)]

            def active(slot):
                return [s for s in range(n_stages) if 0 <= slot - LAG * s < n_units]

            n_slots = n_units + LAG * last_stage
            x_recv, x_mid, u_own, u_oth, d_own, d_oth = {}, {}, {}, {}, {}, {}
            pieces = {}
            for slot in range(n_slots + 2):
                if slot < n_slots:
                    unit = jnp.clip(slot - LAG * stage, 0, n_units - 1)
                    meta = jnp.stack([unit % n_own, unit // n_own, kind_val]).astype(jnp.int32)
                    if slot < n_units:
                        row0 = (slot // n_own) * CHUNK
                        at_own = (side * n_own + slot % n_own, 0, row0, 0)
                        at_oth = ((1 - side) * n_own + slot % n_own, 0, row0, 0)
                        size = (1, 1, CHUNK, d_model)
                        x_own = lax.dynamic_slice(acts_loc, at_own, size).reshape(CHUNK, d_model)
                        x_two = lax.dynamic_slice(acts_loc, at_oth, size).reshape(CHUNK, d_model)
                        if slot >= LAG:
                            x_own = jnp.where(at_first, x_own, x_recv[slot])
                            x_two = jnp.where(at_first, x_two, x_recv[slot])
                    else:
                        x_own = x_two = x_recv[slot]
                    if slot >= 2:
                        x_own, x_two, _ = lax.optimization_barrier((x_own, x_two, d_own[slot - 2]))
                    h_own = rms_norm(x_own, gains[0])
                    h_two = rms_norm(x_two, gains[0]) if slot < n_units else h_own
                    qkv_a = jnp.dot(h_own, wqkv_own, preferred_element_type=f32).astype(jnp.bfloat16)
                    wqkv_two, wo_two = (wqkv_oth, wo_oth) if slot > fill else (wqkv_own, wo_own)
                    qkv_b = jnp.dot(h_two, wqkv_two, preferred_element_type=f32).astype(jnp.bfloat16)
                    att_a, caches[0], caches[1] = attend(meta, qkv_a, caches[0], caches[1], cos_tab, sin_tab, qk_gain, q_scale)
                    att_b, caches[2], caches[3] = attend(meta, qkv_b, caches[2], caches[3], cos_tab, sin_tab, qk_gain, q_scale)
                    o_b = jnp.dot(att_b, wo_two, preferred_element_type=f32)
                    if slot < n_units:
                        o_b = jnp.where(at_first, swap(o_b.astype(jnp.bfloat16), [0]).astype(f32), o_b)
                    o_sum = (jnp.dot(att_a, wo_own, preferred_element_type=f32) + o_b).astype(jnp.bfloat16)
                    x_mid[slot] = x_own + rms_norm(o_sum, gains[1])
                    u_own[slot] = rms_norm(x_mid[slot], gains[2])
                    u_oth[slot] = swap(u_own[slot], active(slot))
                x_out = None
                if 0 <= slot - 2 < n_slots:
                    done = slot - 2
                    d_sum = (d_own[done] + d_oth[done].astype(f32)).astype(jnp.bfloat16)
                    x_out = x_mid[done] + rms_norm(d_sum, gains[3])
                    movers = [s for s in active(done) if s < last_stage]
                    if movers:
                        x_recv[done + LAG] = lax.ppermute(x_out, 'pp', [(s, s + 1) for s in movers])
                    out_unit = done - LAG * last_stage
                    if out_unit >= 0:
                        stream, chunk = out_unit % n_own, out_unit // n_own
                        per = n_chunks // n_stages
                        target, part = chunk // per, chunk % per
                        if target == last_stage:
                            mine = jnp.where(stage == last_stage, x_out, jnp.zeros_like(x_out))
                        else:
                            mine = lax.ppermute(x_out, axes, [(dev(t, last_stage), dev(t, target)) for t in (0, 1)])
                        theirs = lax.ppermute(x_out, axes, [(dev(t, last_stage), dev(1 - t, target)) for t in (0, 1)])
                        for key, val in (((0, stream, part), mine), ((1, stream, part), theirs)):
                            pieces[key] = pieces[key] + val if key in pieces else val

                if 0 <= slot - 1 < n_slots:
                    prev = slot - 1
                    u_in = u_own[prev]
                    if slot < n_slots:
                        u_in = lax.optimization_barrier((u_in, u_own[slot]))[0]
                    if x_out is not None:
                        u_in = lax.optimization_barrier((u_in, x_out))[0]
                    d_own[prev], d_send = mlp(u_in, u_oth[prev], w_gate, w_up, w_down)
                    d_oth[prev] = swap(d_send, active(prev))

            per = n_chunks // n_stages
            mine = [jnp.concatenate([pieces[(0, m, r)] for r in range(per)], axis=0) for m in range(n_own)]
            theirs = [jnp.concatenate([pieces[(1, m, r)] for r in range(per)], axis=0) for m in range(n_own)]
            on_zero = side == 0
            out = [jnp.where(on_zero, a, b) for a, b in zip(mine, theirs)] + [jnp.where(on_zero, b, a) for a, b in zip(mine, theirs)]
            return jnp.stack(out)[:, None]

        return jax.shard_map(device_fn, mesh=mesh, in_specs=in_specs, out_specs=out_spec, check_vma=False)(acts_in, layer_kind, w_q, w_k, w_v, w_o, w_gate, w_up, w_down, norm_gains, qk_gains)

    return run_all
```

time: 5930 us -> 2470 us (0.42)
  waiting for transfers between devices: 3230 us -> 375 us
  matrix products: 1860 us -> 488 us
  Pallas kernels: 0 us -> 1130 us
  other arithmetic: 458 us -> 168 us
  local copies, waits for them, and re-layouts: 284 us -> 20.6 us
  starting transfers between devices: 31.4 us -> 270 us
    psum x14 -> x0, waiting for transfers between devices: 2550 us -> none  [the longest x7 1320 us: layer_fwd(): hidden = hidden + rms_norm(lax.psum(o_part, 'tp'), norm_gains[1])]
    dot_general x175 -> x100, matrix products: 1860 us -> 488 us  [the longest x25 160 us: device_fn(): jnp.dot(h_own, wqkv_own, preferred_element_type=f32).astype(jnp.bfloat16)]
    pallas_call x0 -> x75, Pallas kernels: none -> 1130 us  [the longest x25 929 us: mlp(): pl.pallas_call(mlp_kernel, grid=(n_tiles + 1,), in_specs=[whole, whole, c...]
    ppermute x10 -> x118, waiting for transfers between devices: 688 us -> 375 us  [the longest x68 162 us: swap(): return lax.ppermute(x, axes, pairs)]
    ppermute x10 -> x118, starting transfers between devices: 30.9 us -> 270 us  [the longest x22 142 us: device_fn(): x_recv[done + LAG] = lax.ppermute(x_out, 'pp', [(s, s + 1) for s in movers])]
    reduce_sum x28 -> x100, other arithmetic: 174 us -> 49.7 us  [rms_norm(): mean_sq = jnp.mean(x_f32 * x_f32, axis=-1, keepdims=True)]
    dynamic_update_slice x7 -> x0, other arithmetic: 90.2 us -> none  [time_step(): lax.dynamic_update_index_in_dim(collected, jnp.where(keep_new, stage_out,...]
    dynamic_slice x49 -> x0, local copies, waits for them, and re-layouts: 74.4 us -> none  [the longest x7 48.7 us: time_step(): lax.dynamic_index_in_dim(collected, out_slot, axis=0, keepdims=False)]
  transfers between devices with their start and end apart: 24 -> 118, of which waited for: 22 -> 19; matrix products, arithmetic and copies ran while one was open for 1% -> 25% of each run, Pallas kernels for 0% -> 35%
where the time goes in v1:
time: 2470 us; the launch traced here: 2460 us
  Pallas kernels  1130 us (46%)
  matrix products  488 us (20%)
  waiting for transfers between devices  375 us (15%)
  starting transfers between devices  270 us (11%)
  other arithmetic  168 us (7%)
    pallas_call x25, Pallas kernels, mlp(): pl.pallas_call(mlp_kernel, grid=(n_tiles + 1,), in_specs=[whole, whole, c...  929 us
    pallas_call x50, Pallas kernels, attend(): pl.pallas_call(functools.partial(attn_kernel, n_group=n_group, q_scale=q_...  202 us
    ppermute x68, waiting for transfers between devices, swap(): return lax.ppermute(x, axes, pairs)  162 us
    dot_general x25, matrix products, device_fn(): jnp.dot(h_own, wqkv_own, preferred_element_type=f32).astype(jnp.bfloat16)  160 us
    dot_general x25, matrix products, device_fn(): jnp.dot(h_two, wqkv_two, preferred_element_type=f32).astype(jnp.bfloat16)  155 us
    ppermute x22, starting transfers between devices, device_fn(): x_recv[done + LAG] = lax.ppermute(x_out, 'pp', [(s, s + 1) for s in movers])  142 us
    ppermute x12, waiting for transfers between devices, device_fn(): lax.ppermute(x_out, axes, [(dev(t, last_stage), dev(t, target)) for t in...  108 us
    dot_general x25, matrix products, device_fn(): jnp.dot(att_a, wo_own, preferred_element_type=f32) + o_b  102 us
  transfers between devices with their start and end apart: 118, of which 19 were waited for; matrix products, arithmetic and copies ran while one was open for 25% of the time, Pallas kernels for 35%

profile of v1, /device:TPU:1, one launch (start us, length us, event | category | flops | bytes accessed | tf_op | source)
XLA Modules:
  0.0 2457.5 jit_solution(14500638856907734738)
XLA Ops:
  7.8 7.8 pad_maximum_fusion
  41.3 7.5 fusion.606
  50.9 7.4 convolution_convert_fusion.49.q_ref.k_ref.v_ref
  58.3 7.4 convolution_convert_fusion.47.q_ref.k_ref.v_ref
  97.2 38.1 %mlp.25 = (f32[192,2560]{1,0:T(8,128)S(1)}, bf16[192,2560]{1,0:T(8,128)(2,1)S(1)}) custom-call(bf16[192,2560]{1,0:T(8,128)(2,1)} %get-tuple-element.294.uo_ref, bf16[192,2560]{1,0:T(8,128)(2,1)} %collective-permute-done.2.ux_ref, bf16[2560,5120]{1,0:T(8,128)(2,1)} %bitcast.465, bf16[2560,5120]{1,0:T(8,128)(2,1)} %bitcast.490, bf16[5120,2560]{1,0:T(8,128)(2,1)} %bitcast.515), custom_call_target="tpu_custom_call" | custom-call | flops 30198988800 | bytes 78643200 | tf_op jit(solution)/shard_map/mlp/pallas_call | solution.py:184
  168.7 36.8 %mlp.26 = (f32[192,2560]{1,0:T(8,128)S(1)}, bf16[192,2560]{1,0:T(8,128)(2,1)S(1)}) custom-call(bf16[192,2560]{1,0:T(8,128)(2,1)S(1)} %copy-done.69, bf16[192,2560]{1,0:T(8,128)(2,1)S(1)} %collective-permute-done.6.ux_ref, bf16[2560,5120]{1,0:T(8,128)(2,1)} %bitcast.466, bf16[2560,5120]{1,0:T(8,128)(2,1)} %bitcast.491, bf16[5120,2560]{1,0:T(8,128)(2,1)} %bitcast.516), custom_call_target="tpu_custom_call" | custom-call | flops 30198988800 | bytes 78643200 | tf_op jit(solution)/shard_map/mlp/pallas_call | solution.py:184
  206.3 10.8 collective-permute-done.4
  235.2 100.5 %collective-permute-done.8 = bf16[1024,2560]{1,0:T(8,128)(2,1)} collective-permute-done((bf16[1024,2560]{1,0:T(8,128)(2,1)}, bf16[1024,2560]{1,0:T(8,128)(2,1)}, u32[]{:S(2)}, u32[]{:S(2)}) %collective-permute-start.8) | collective-permute-done | bytes 5242912 | tf_op jit(solution)/shard_map/ppermute | solution.py:237
  335.7 7.0 broadcast_select_fusion.1
  342.6 10.3 broadcast_select_fusion
  367.6 37.8 %mlp.27 = (f32[192,2560]{1,0:T(8,128)S(1)}, bf16[192,2560]{1,0:T(8,128)(2,1)S(1)}) custom-call(bf16[192,2560]{1,0:T(8,128)(2,1)S(1)} %fusion.50.uo_ref, bf16[192,2560]{1,0:T(8,128)(2,1)} %collective-permute-done.12.ux_ref, bf16[2560,5120]{1,0:T(8,128)(2,1)} %bitcast.467, bf16[2560,5120]{1,0:T(8,128)(2,1)} %bitcast.492, bf16[5120,2560]{1,0:T(8,128)(2,1)} %bitcast.517), custom_call_target="tpu_custom_call" | custom-call | flops 30198988800 | bytes 78643200 | tf_op jit(solution)/shard_map/mlp/pallas_call | solution.py:184
  448.4 36.8 %mlp.28 = (f32[192,2560]{1,0:T(8,128)S(1)}, bf16[192,2560]{1,0:T(8,128)(2,1)S(1)}) custom-call(bf16[192,2560]{1,0:T(8,128)(2,1)S(1)} %copy-done.68, bf16[192,2560]{1,0:T(8,128)(2,1)S(1)} %collective-permute-done.15.ux_ref, bf16[2560,5120]{1,0:T(8,128)(2,1)} %bitcast.468, bf16[2560,5120]{1,0:T(8,128)(2,1)} %bitcast.493, bf16[5120,2560]{1,0:T(8,128)(2,1)} %bitcast.518), custom_call_target="tpu_custom_call" | custom-call | flops 30198988800 | bytes 78643200 | tf_op jit(solution)/shard_map/mlp/pallas_call | solution.py:184
  524.5 37.0 %mlp.29 = (f32[192,2560]{1,0:T(8,128)S(1)}, bf16[192,2560]{1,0:T(8,128)(2,1)S(1)}) custom-call(bf16[192,2560]{1,0:T(8,128)(2,1)S(1)} %fusion.77.uo_ref, bf16[192,2560]{1,0:T(8,128)(2,1)S(1)} %collective-permute-done.20.ux_ref, bf16[2560,5120]{1,0:T(8,128)(2,1)} %bitcast.469, bf16[2560,5120]{1,0:T(8,128)(2,1)} %bitcast.494, bf16[5120,2560]{1,0:T(8,128)(2,1)} %bitcast.519), custom_call_target="tpu_custom_call" | custom-call | flops 30198988800 | bytes 78643200 | tf_op jit(solution)/shard_map/mlp/pallas_call | solution.py:184
  564.8 88.4 %collective-permute-start.17 = (bf16[192,2560]{1,0:T(8,128)(2,1)}, bf16[192,2560]{1,0:T(8,128)(2,1)}, u32[]{:S(2)}, u32[]{:S(2)}) collective-permute-start(bf16[192,2560]{1,0:T(8,128)(2,1)} %fusion.404), channel_id=1, source_target_pairs={{0,1},{1,2},{4,5},{5,6}} | collective-permute-start | bytes 2949128 | tf_op jit(solution)/shard_map/ppermute | solution.py:293
  664.6 10.5 collective-permute-done.23
  709.4 37.1 %mlp.30 = (f32[192,2560]{1,0:T(8,128)S(1)}, bf16[192,2560]{1,0:T(8,128)(2,1)S(1)}) custom-call(bf16[192,2560]{1,0:T(8,128)(2,1)S(1)} %copy-done.64, bf16[192,2560]{1,0:T(8,128)(2,1)S(1)} %collective-permute-done.24.ux_ref, bf16[2560,5120]{1,0:T(8,128)(2,1)} %bitcast.470, bf16[2560,5120]{1,0:T(8,128)(2,1)} %bitcast.495, bf16[5120,2560]{1,0:T(8,128)(2,1)} %bitcast.520), custom_call_target="tpu_custom_call" | custom-call | flops 30198988800 | bytes 78643200 | tf_op jit(solution)/shard_map/mlp/pallas_call | solution.py:184
  788.3 37.0 %mlp.31 = (f32[192,2560]{1,0:T(8,128)S(1)}, bf16[192,2560]{1,0:T(8,128)(2,1)S(1)}) custom-call(bf16[192,2560]{1,0:T(8,128)(2,1)S(1)} %fusion.107.uo_ref, bf16[192,2560]{1,0:T(8,128)(2,1)S(1)} %collective-permute-done.27.ux_ref, bf16[2560,5120]{1,0:T(8,128)(2,1)} %bitcast.471, bf16[2560,5120]{1,0:T(8,128)(2,1)} %bitcast.496, bf16[5120,2560]{1,0:T(8,128)(2,1)} %bitcast.521), custom_call_target="tpu_custom_call" | custom-call | flops 30198988800 | bytes 78643200 | tf_op jit(solution)/shard_map/mlp/pallas_call | solution.py:184
  830.4 16.0 collective-permute-done.28
  852.4 9.1 collective-permute-done.29
  894.9 37.0 %mlp.32 = (f32[192,2560]{1,0:T(8,128)S(1)}, bf16[192,2560]{1,0:T(8,128)(2,1)S(1)}) custom-call(bf16[192,2560]{1,0:T(8,128)(2,1)S(1)} %copy-done.65, bf16[192,2560]{1,0:T(8,128)(2,1)S(1)} %collective-permute-done.32.ux_ref, bf16[2560,5120]{1,0:T(8,128)(2,1)} %bitcast.472, bf16[2560,5120]{1,0:T(8,128)(2,1)} %bitcast.497, bf16[5120,2560]{1,0:T(8,128)(2,1)} %bitcast.522), custom_call_target="tpu_custom_call" | custom-call | flops 30198988800 | bytes 78643200 | tf_op jit(solution)/shard_map/mlp/pallas_call | solution.py:184
  977.4 37.0 %mlp.33 = (f32[192,2560]{1,0:T(8,128)S(1)}, bf16[192,2560]{1,0:T(8,128)(2,1)S(1)}) custom-call(bf16[192,2560]{1,0:T(8,128)(2,1)S(1)} %fusion.140.uo_ref, bf16[192,2560]{1,0:T(8,128)(2,1)S(1)} %collective-permute-done.36.ux_ref, bf16[2560,5120]{1,0:T(8,128)(2,1)} %bitcast.473, bf16[2560,5120]{1,0:T(8,128)(2,1)} %bitcast.498, bf16[5120,2560]{1,0:T(8,128)(2,1)} %bitcast.523), custom_call_target="tpu_custom_call" | custom-call | flops 30198988800 | bytes 78643200 | tf_op jit(solution)/shard_map/mlp/pallas_call | solution.py:184
  1019.5 13.0 collective-permute-done.38
  1037.7 10.0 collective-permute-done.42
  1081.3 37.0 %mlp.34 = (f32[192,2560]{1,0:T(8,128)S(1)}, bf16[192,2560]{1,0:T(8,128)(2,1)S(1)}) custom-call(bf16[192,2560]{1,0:T(8,128)(2,1)S(1)} %copy-done.66, bf16[192,2560]{1,0:T(8,128)(2,1)S(1)} %collective-permute-done.39.ux_ref, bf16[2560,5120]{1,0:T(8,128)(2,1)} %bitcast.474, bf16[2560,5120]{1,0:T(8,128)(2,1)} %bitcast.499, bf16[5120,2560]{1,0:T(8,128)(2,1)} %bitcast.524), custom_call_target="tpu_custom_call" | custom-call | flops 30198988800 | bytes 78643200 | tf_op jit(solution)/shard_map/mlp/pallas_call | solution.py:184
  1157.9 37.0 %mlp.35 = (f32[192,2560]{1,0:T(8,128)S(1)}, bf16[192,2560]{1,0:T(8,128)(2,1)S(1)}) custom-call(bf16[192,2560]{1,0:T(8,128)(2,1)S(1)} %fusion.167.uo_ref, bf16[192,2560]{1,0:T(8,128)(2,1)S(1)} %collective-permute-done.44.ux_ref, bf16[2560,5120]{1,0:T(8,128)(2,1)} %bitcast.475, bf16[2560,5120]{1,0:T(8,128)(2,1)} %bitcast.500, bf16[5120,2560]{1,0:T(8,128)(2,1)} %bitcast.525), custom_call_target="tpu_custom_call" | custom-call | flops 30198988800 | bytes 78643200 | tf_op jit(solution)/shard_map/mlp/pallas_call | solution.py:184
  1199.2 12.2 collective-permute-done.45
  1219.6 11.0 collective-permute-done.46
  1264.2 37.0 %mlp.36 = (f32[192,2560]{1,0:T(8,128)S(1)}, bf16[192,2560]{1,0:T(8,128)(2,1)S(1)}) custom-call(bf16[192,2560]{1,0:T(8,128)(2,1)S(1)} %copy-done.67, bf16[192,2560]{1,0:T(8,128)(2,1)S(1)} %collective-permute-done.49.ux_ref, bf16[2560,5120]{1,0:T(8,128)(2,1)} %bitcast.476, bf16[2560,5120]{1,0:T(8,128)(2,1)} %bitcast.501, bf16[5120,2560]{1,0:T(8,128)(2,1)} %bitcast.526), custom_call_target="tpu_custom_call" | custom-call | flops 30198988800 | bytes 78643200 | tf_op jit(solution)/shard_map/mlp/pallas_call | solution.py:184
  1343.6 37.0 %mlp.37 = (f32[192,2560]{1,0:T(8,128)S(1)}, bf16[192,2560]{1,0:T(8,128)(2,1)S(1)}) custom-call(bf16[192,2560]{1,0:T(8,128)(2,1)S(1)} %fusion.200.uo_ref, bf16[192,2560]{1,0:T(8,128)(2,1)S(1)} %collective-permute-done.53.ux_ref, bf16[2560,5120]{1,0:T(8,128)(2,1)} %bitcast.477, bf16[2560,5120]{1,0:T(8,128)(2,1)} %bitcast.502, bf16[5120,2560]{1,0:T(8,128)(2,1)} %bitcast.527), custom_call_target="tpu_custom_call" | custom-call | flops 30198988800 | bytes 78643200 | tf_op jit(solution)/shard_map/mlp/pallas_call | solution.py:184
  1384.9 16.3 collective-permute-done.55
  1408.7 7.6 collective-permute-done.59
  1451.0 37.0 %mlp.38 = (f32[192,2560]{1,0:T(8,128)S(1)}, bf16[192,2560]{1,0:T(8,128)(2,1)S(1)}) custom-call(bf16[192,2560]{1,0:T(8,128)(2,1)S(1)} %copy-done.63, bf16[192,2560]{1,0:T(8,128)(2,1)S(1)} %collective-permute-done.56.ux_ref, bf16[2560,5120]{1,0:T(8,128)(2,1)} %bitcast.478, bf16[2560,5120]{1,0:T(8,128)(2,1)} %bitcast.503, bf16[5120,2560]{1,0:T(8,128)(2,1)} %bitcast.528), custom_call_target="tpu_custom_call" | custom-call | flops 30198988800 | bytes 78643200 | tf_op jit(solution)/shard_map/mlp/pallas_call | solution.py:184
  1528.4 37.1 %mlp.39 = (f32[192,2560]{1,0:T(8,128)S(1)}, bf16[192,2560]{1,0:T(8,128)(2,1)S(1)}) custom-call(bf16[192,2560]{1,0:T(8,128)(2,1)S(1)} %fusion.227.uo_ref, bf16[192,2560]{1,0:T(8,128)(2,1)S(1)} %collective-permute-done.61.ux_ref, bf16[2560,5120]{1,0:T(8,128)(2,1)} %bitcast.479, bf16[2560,5120]{1,0:T(8,128)(2,1)} %bitcast.504, bf16[5120,2560]{1,0:T(8,128)(2,1)} %bitcast.529), custom_call_target="tpu_custom_call" | custom-call | flops 30198988800 | bytes 78643200 | tf_op jit(solution)/shard_map/mlp/pallas_call | solution.py:184
  1602.2 37.1 %mlp.40 = (f32[192,2560]{1,0:T(8,128)S(1)}, bf16[192,2560]{1,0:T(8,128)(2,1)S(1)}) custom-call(bf16[192,2560]{1,0:T(8,128)(2,1)S(1)} %fusion.245.uo_ref, bf16[192,2560]{1,0:T(8,128)(2,1)S(1)} %collective-permute-done.65.ux_ref, bf16[2560,5120]{1,0:T(8,128)(2,1)} %bitcast.480, bf16[2560,5120]{1,0:T(8,128)(2,1)} %bitcast.505, bf16[5120,2560]{1,0:T(8,128)(2,1)} %bitcast.530), custom_call_target="tpu_custom_call" | custom-call | flops 30198988800 | bytes 78643200 | tf_op jit(solution)/shard_map/mlp/pallas_call | solution.py:184
  1677.6 37.1 %mlp.41 = (f32[192,2560]{1,0:T(8,128)S(1)}, bf16[192,2560]{1,0:T(8,128)(2,1)S(1)}) custom-call(bf16[192,2560]{1,0:T(8,128)(2,1)S(1)} %fusion.254.uo_ref, bf16[192,2560]{1,0:T(8,128)(2,1)S(1)} %collective-permute-done.68.ux_ref, bf16[2560,5120]{1,0:T(8,128)(2,1)} %bitcast.481, bf16[2560,5120]{1,0:T(8,128)(2,1)} %bitcast.506, bf16[5120,2560]{1,0:T(8,128)(2,1)} %bitcast.531), custom_call_target="tpu_custom_call" | custom-call | flops 30198988800 | bytes 78643200 | tf_op jit(solution)/shard_map/mlp/pallas_call | solution.py:184
  1754.2 37.1 %mlp.42 = (f32[192,2560]{1,0:T(8,128)S(1)}, bf16[192,2560]{1,0:T(8,128)(2,1)S(1)}) custom-call(bf16[192,2560]{1,0:T(8,128)(2,1)S(1)} %fusion.260.uo_ref, bf16[192,2560]{1,0:T(8,128)(2,1)S(1)} %collective-permute-done.70.ux_ref, bf16[2560,5120]{1,0:T(8,128)(2,1)} %bitcast.482, bf16[2560,5120]{1,0:T(8,128)(2,1)} %bitcast.507, bf16[5120,2560]{1,0:T(8,128)(2,1)} %bitcast.532), custom_call_target="tpu_custom_call" | custom-call | flops 30198988800 | bytes 78643200 | tf_op jit(solution)/shard_map/mlp/pallas_call | solution.py:184
  1830.0 37.1 %mlp.43 = (f32[192,2560]{1,0:T(8,128)S(1)}, bf16[192,2560]{1,0:T(8,128)(2,1)S(1)}) custom-call(bf16[192,2560]{1,0:T(8,128)(2,1)S(1)} %fusion.269.uo_ref, bf16[192,2560]{1,0:T(8,128)(2,1)S(1)} %collective-permute-done.74.ux_ref, bf16[2560,5120]{1,0:T(8,128)(2,1)} %bitcast.483, bf16[2560,5120]{1,0:T(8,128)(2,1)} %bitcast.508, bf16[5120,2560]{1,0:T(8,128)(2,1)} %bitcast.533), custom_call_target="tpu_custom_call" | custom-call | flops 30198988800 | bytes 78643200 | tf_op jit(solution)/shard_map/mlp/pallas_call | solution.py:184
  1908.3 37.1 %mlp.44 = (f32[192,2560]{1,0:T(8,128)S(1)}, bf16[192,2560]{1,0:T(8,128)(2,1)S(1)}) custom-call(bf16[192,2560]{1,0:T(8,128)(2,1)S(1)} %fusion.281.uo_ref, bf16[192,2560]{1,0:T(8,128)(2,1)S(1)} %collective-permute-done.78.ux_ref, bf16[2560,5120]{1,0:T(8,128)(2,1)} %bitcast.484, bf16[2560,5120]{1,0:T(8,128)(2,1)} %bitcast.509, bf16[5120,2560]{1,0:T(8,128)(2,1)} %bitcast.534), custom_call_target="tpu_custom_call" | custom-call | flops 30198988800 | bytes 78643200 | tf_op jit(solution)/shard_map/mlp/pallas_call | solution.py:184
  1978.2 37.1 %mlp.45 = (f32[192,2560]{1,0:T(8,128)S(1)}, bf16[192,2560]{1,0:T(8,128)(2,1)S(1)}) custom-call(bf16[192,2560]{1,0:T(8,128)(2,1)S(1)} %fusion.290.uo_ref, bf16[192,2560]{1,0:T(8,128)(2,1)S(1)} %collective-permute-done.81.ux_ref, bf16[2560,5120]{1,0:T(8,128)(2,1)} %bitcast.485, bf16[2560,5120]{1,0:T(8,128)(2,1)} %bitcast.510, bf16[5120,2560]{1,0:T(8,128)(2,1)} %bitcast.535), custom_call_target="tpu_custom_call" | custom-call | flops 30198988800 | bytes 78643200 | tf_op jit(solution)/shard_map/mlp/pallas_call | solution.py:184
  2048.3 37.1 %mlp.46 = (f32[192,2560]{1,0:T(8,128)S(1)}, bf16[192,2560]{1,0:T(8,128)(2,1)S(1)}) custom-call(bf16[192,2560]{1,0:T(8,128)(2,1)S(1)} %fusion.296.uo_ref, bf16[192,2560]{1,0:T(8,128)(2,1)S(1)} %collective-permute-done.83.ux_ref, bf16[2560,5120]{1,0:T(8,128)(2,1)} %bitcast.486, bf16[2560,5120]{1,0:T(8,128)(2,1)} %bitcast.511, bf16[5120,2560]{1,0:T(8,128)(2,1)} %bitcast.536), custom_call_target="tpu_custom_call" | custom-call | flops 30198988800 | bytes 78643200 | tf_op jit(solution)/shard_map/mlp/pallas_call | solution.py:184
  2124.6 37.1 %mlp.47 = (f32[192,2560]{1,0:T(8,128)S(1)}, bf16[192,2560]{1,0:T(8,128)(2,1)S(1)}) custom-call(bf16[192,2560]{1,0:T(8,128)(2,1)S(1)} %fusion.305.uo_ref, bf16[192,2560]{1,0:T(8,128)(2,1)S(1)} %collective-permute-done.90.ux_ref, bf16[2560,5120]{1,0:T(8,128)(2,1)} %bitcast.487, bf16[2560,5120]{1,0:T(8,128)(2,1)} %bitcast.512, bf16[5120,2560]{1,0:T(8,128)(2,1)} %bitcast.537), custom_call_target="tpu_custom_call" | custom-call | flops 30198988800 | bytes 78643200 | tf_op jit(solution)/shard_map/mlp/pallas_call | solution.py:184
  2196.0 38.0 %mlp.48 = (f32[192,2560]{1,0:T(8,128)S(1)}, bf16[192,2560]{1,0:T(8,128)(2,1)}) custom-call(bf16[192,2560]{1,0:T(8,128)(2,1)S(1)} %fusion.317.uo_ref, bf16[192,2560]{1,0:T(8,128)(2,1)S(1)} %collective-permute-done.92.ux_ref, bf16[2560,5120]{1,0:T(8,128)(2,1)} %bitcast.488, bf16[2560,5120]{1,0:T(8,128)(2,1)} %bitcast.513, bf16[5120,2560]{1,0:T(8,128)(2,1)} %bitcast.538), custom_call_target="tpu_custom_call" | custom-call | flops 30198988800 | bytes 78643200 | tf_op jit(solution)/shard_map/mlp/pallas_call | solution.py:184
  2244.6 74.5 %collective-permute-done.86 = bf16[192,2560]{1,0:T(8,128)(2,1)} collective-permute-done((bf16[192,2560]{1,0:T(8,128)(2,1)}, bf16[192,2560]{1,0:T(8,128)(2,1)}, u32[]{:S(2)}, u32[]{:S(2)}) %collective-permute-start.86) | collective-permute-done | bytes 983072 | tf_op jit(solution)/shard_map/ppermute | solution.py:302
  2325.0 15.2 collective-permute-done.95
  2342.4 37.1 %mlp.49 = (f32[192,2560]{1,0:T(8,128)S(1)}, bf16[192,2560]{1,0:T(8,128)(2,1)S(1)}) custom-call(bf16[192,2560]{1,0:T(8,128)(2,1)S(1)} %fusion.323.uo_ref, bf16[192,2560]{1,0:T(8,128)(2,1)S(1)} %collective-permute-done.108.ux_ref, bf16[2560,5120]{1,0:T(8,128)(2,1)} %bitcast.489, bf16[2560,5120]{1,0:T(8,128)(2,1)} %bitcast.514, bf16[5120,2560]{1,0:T(8,128)(2,1)} %bitcast.539), custom_call_target="tpu_custom_call" | custom-call | flops 30198988800 | bytes 78643200 | tf_op jit(solution)/shard_map/mlp/pallas_call | solution.py:184
  2386.9 33.3 %collective-permute-done.106 = bf16[192,2560]{1,0:T(8,128)(2,1)S(1)} collective-permute-done((bf16[192,2560]{1,0:T(8,128)(2,1)S(1)}, bf16[192,2560]{1,0:T(8,128)(2,1)S(1)}, u32[]{:S(2)}, u32[]{:S(2)}) %collective-permute-start.106) | collective-permute-done | bytes 983072 | tf_op jit(solution)/shard_map/ppermute | solution.py:302
  2424.1 7.4 collective-permute-done.99
  2434.2 18.4 collective-permute-done.115
  (995 shorter events, 1021.1 us)
Async XLA Ops:
  30.7 41.7 %collective-permute-start = (bf16[192,2560]{1,0:T(8,128)(2,1)}, bf16[192,2560]{1,0:T(8,128)(2,1)}, u32[]{:S(2)}, u32[]{:S(2)}) collective-permute-start(bf16[192,2560]{1,0:T(8,128)(2,1)} %get-tuple-element.713), channel_id=1, source_target_pairs={{0,4},{4,0}} | collective-permute-start | bytes 2949128 | tf_op jit(solution)/shard_map/ppermute | solution.py:237
  88.2 254.4 %collective-permute-start.7 = (bf16[2560,2048]{1,0:T(8,128)(2,1)}, bf16[2560,2048]{1,0:T(8,128)(2,1)}, u32[]{:S(2)}, u32[]{:S(2)}) collective-permute-start(bf16[2560,2048]{1,0:T(8,128)(2,1)} %pad_maximum_fusion), channel_id=1, source_target_pairs={{1,5},{5,1},{2,6},{6,2},{3,7},{7,3}} | collective-permute-start | bytes 31457288 | tf_op jit(solution)/shard_map/ppermute | solution.py:237
  92.1 243.5 %collective-permute-start.8 = (bf16[1024,2560]{1,0:T(8,128)(2,1)}, bf16[1024,2560]{1,0:T(8,128)(2,1)}, u32[]{:S(2)}, u32[]{:S(2)}) collective-permute-start(bf16[1024,2560]{1,0:T(8,128)(2,1)} %bitcast.13), channel_id=1, source_target_pairs={{1,5},{5,1},{2,6},{6,2},{3,7},{7,3}} | collective-permute-start | bytes 15728648 | tf_op jit(solution)/shard_map/ppermute | solution.py:237
  96.1 72.6 %collective-permute-start.6 = (bf16[192,2560]{1,0:T(8,128)(2,1)S(1)}, bf16[192,2560]{1,0:T(8,128)(2,1)S(1)}, u32[]{:S(2)}, u32[]{:S(2)}) collective-permute-start(bf16[192,2560]{1,0:T(8,128)(2,1)S(1)} %copy-done.69), channel_id=1, source_target_pairs={{0,4},{4,0}} | collective-permute-start | bytes 2949128 | tf_op jit(solution)/shard_map/ppermute | solution.py:237
  164.5 203.1 %collective-permute-start.12 = (bf16[192,2560]{1,0:T(8,128)(2,1)S(1)}, bf16[192,2560]{1,0:T(8,128)(2,1)}, u32[]{:S(2)}, u32[]{:S(2)}) collective-permute-start(bf16[192,2560]{1,0:T(8,128)(2,1)S(1)} %fusion.50.uo_ref), channel_id=1, source_target_pairs={{0,4},{4,0}} | collective-permute-start | bytes 2949128 | tf_op jit(solution)/shard_map/ppermute | solution.py:237
  167.4 49.7 %collective-permute-start.4 = (bf16[192,2560]{1,0:T(8,128)(2,1)S(1)}, bf16[192,2560]{1,0:T(8,128)(2,1)S(1)}, u32[]{:S(2)}, u32[]{:S(2)}) collective-permute-start(bf16[192,2560]{1,0:T(8,128)(2,1)S(1)} %fusion.416), channel_id=1, source_target_pairs={{0,1},{4,5}} | collective-permute-start | bytes 2949128 | tf_op jit(solution)/shard_map/ppermute | solution.py:293
  444.6 79.9 %collective-permute-start.20 = (bf16[192,2560]{1,0:T(8,128)(2,1)S(1)}, bf16[192,2560]{1,0:T(8,128)(2,1)S(1)}, u32[]{:S(2)}, u32[]{:S(2)}) collective-permute-start(bf16[192,2560]{1,0:T(8,128)(2,1)S(1)} %fusion.77.uo_ref), channel_id=1, source_target_pairs={{0,4},{4,0},{1,5},{5,1}} | collective-permute-start | bytes 2949128 | tf_op jit(solution)/shard_map/ppermute | solution.py:237
  561.5 91.7 %collective-permute-start.22 = (bf16[192,2560]{1,0:T(8,128)(2,1)S(1)}, bf16[192,2560]{1,0:T(8,128)(2,1)S(1)}, u32[]{:S(2)}, u32[]{:S(2)}) collective-permute-start(bf16[192,2560]{1,0:T(8,128)(2,1)S(1)} %get-tuple-element.352), channel_id=1, source_target_pairs={{0,4},{4,0},{1,5},{5,1}} | collective-permute-start | bytes 2949128 | tf_op jit(solution)/shard_map/ppermute | solution.py:237
  564.8 99.7 %collective-permute-start.17 = (bf16[192,2560]{1,0:T(8,128)(2,1)}, bf16[192,2560]{1,0:T(8,128)(2,1)}, u32[]{:S(2)}, u32[]{:S(2)}) collective-permute-start(bf16[192,2560]{1,0:T(8,128)(2,1)} %fusion.404), channel_id=1, source_target_pairs={{0,1},{1,2},{4,5},{5,6}} | collective-permute-start | bytes 2949128 | tf_op jit(solution)/shard_map/ppermute | solution.py:293
  657.2 52.2 %collective-permute-start.24 = (bf16[192,2560]{1,0:T(8,128)(2,1)}, bf16[192,2560]{1,0:T(8,128)(2,1)S(1)}, u32[]{:S(2)}, u32[]{:S(2)}) collective-permute-start(bf16[192,2560]{1,0:T(8,128)(2,1)} %fusion.95.uo_ref), channel_id=1, source_target_pairs={{0,4},{4,0},{1,5},{5,1}} | collective-permute-start | bytes 2949128 | tf_op jit(solution)/shard_map/ppermute | solution.py:237
  706.2 82.1 %collective-permute-start.27 = (bf16[192,2560]{1,0:T(8,128)(2,1)S(1)}, bf16[192,2560]{1,0:T(8,128)(2,1)S(1)}, u32[]{:S(2)}, u32[]{:S(2)}) collective-permute-start(bf16[192,2560]{1,0:T(8,128)(2,1)S(1)} %fusion.107.uo_ref), channel_id=1, source_target_pairs={{0,4},{4,0},{1,5},{5,1},{2,6},{6,2}} | collective-permute-start | bytes 2949128 | tf_op jit(solution)/shard_map/ppermute | solution.py:237
  850.2 44.6 %collective-permute-start.32 = (bf16[192,2560]{1,0:T(8,128)(2,1)}, bf16[192,2560]{1,0:T(8,128)(2,1)S(1)}, u32[]{:S(2)}, u32[]{:S(2)}) collective-permute-start(bf16[192,2560]{1,0:T(8,128)(2,1)} %fusion.122.uo_ref), channel_id=1, source_target_pairs={{0,4},{4,0},{1,5},{5,1},{2,6},{6,2}} | collective-permute-start | bytes 2949128 | tf_op jit(solution)/shard_map/ppermute | solution.py:237
  892.7 84.7 %collective-permute-start.36 = (bf16[192,2560]{1,0:T(8,128)(2,1)S(1)}, bf16[192,2560]{1,0:T(8,128)(2,1)S(1)}, u32[]{:S(2)}, u32[]{:S(2)}) collective-permute-start(bf16[192,2560]{1,0:T(8,128)(2,1)S(1)} %fusion.140.uo_ref), channel_id=1, source_target_pairs={{0,4},{4,0},{1,5},{5,1},{2,6},{6,2}} | collective-permute-start | bytes 2949128 | tf_op jit(solution)/shard_map/ppermute | solution.py:237
  1036.4 44.9 %collective-permute-start.39 = (bf16[192,2560]{1,0:T(8,128)(2,1)}, bf16[192,2560]{1,0:T(8,128)(2,1)S(1)}, u32[]{:S(2)}, u32[]{:S(2)}) collective-permute-start(bf16[192,2560]{1,0:T(8,128)(2,1)} %fusion.152.uo_ref), channel_id=1, source_target_pairs={{0,4},{4,0},{1,5},{5,1},{2,6},{6,2},{3,7},{7,3}} | collective-permute-start | bytes 2949128 | tf_op jit(solution)/shard_map/ppermute | solution.py:237
  1079.9 77.9 %collective-permute-start.44 = (bf16[192,2560]{1,0:T(8,128)(2,1)S(1)}, bf16[192,2560]{1,0:T(8,128)(2,1)S(1)}, u32[]{:S(2)}, u32[]{:S(2)}) collective-permute-start(bf16[192,2560]{1,0:T(8,128)(2,1)S(1)} %fusion.167.uo_ref), channel_id=1, source_target_pairs={{0,4},{4,0},{1,5},{5,1},{2,6},{6,2},{3,7},{7,3}} | collective-permute-start | bytes 2949128 | tf_op jit(solution)/shard_map/ppermute | solution.py:237
  1219.4 44.8 %collective-permute-start.49 = (bf16[192,2560]{1,0:T(8,128)(2,1)}, bf16[192,2560]{1,0:T(8,128)(2,1)S(1)}, u32[]{:S(2)}, u32[]{:S(2)}) collective-permute-start(bf16[192,2560]{1,0:T(8,128)(2,1)} %fusion.185.uo_ref), channel_id=1, source_target_pairs={{0,4},{4,0},{1,5},{5,1},{2,6},{6,2},{3,7},{7,3}} | collective-permute-start | bytes 2949128 | tf_op jit(solution)/shard_map/ppermute | solution.py:237
  1263.9 79.7 %collective-permute-start.53 = (bf16[192,2560]{1,0:T(8,128)(2,1)S(1)}, bf16[192,2560]{1,0:T(8,128)(2,1)S(1)}, u32[]{:S(2)}, u32[]{:S(2)}) collective-permute-start(bf16[192,2560]{1,0:T(8,128)(2,1)S(1)} %fusion.200.uo_ref), channel_id=1, source_target_pairs={{0,4},{4,0},{1,5},{5,1},{2,6},{6,2},{3,7},{7,3}} | collective-permute-start | bytes 2949128 | tf_op jit(solution)/shard_map/ppermute | solution.py:237
  1405.4 710.7 %collective-permute-start.41 = (bf16[192,2560]{1,0:T(8,128)(2,1)}, bf16[192,2560]{1,0:T(8,128)(2,1)}, u32[]{:S(2)}, u32[]{:S(2)}) collective-permute-start(bf16[192,2560]{1,0:T(8,128)(2,1)} %fusion.380), channel_id=1, source_target_pairs={{3,0},{7,4}} | collective-permute-start | bytes 2949128 | tf_op jit(solution)/shard_map/ppermute | solution.py:302
  1407.0 784.8 %collective-permute-start.102 = (bf16[192,2560]{1,0:T(8,128)(2,1)}, bf16[192,2560]{1,0:T(8,128)(2,1)}, u32[]{:S(2)}, u32[]{:S(2)}) collective-permute-start(bf16[192,2560]{1,0:T(8,128)(2,1)} %fusion.376), channel_id=1, source_target_pairs={{3,0},{7,4}} | collective-permute-start | bytes 2949128 | tf_op jit(solution)/shard_map/ppermute | solution.py:302
  1408.7 42.2 %collective-permute-start.56 = (bf16[192,2560]{1,0:T(8,128)(2,1)}, bf16[192,2560]{1,0:T(8,128)(2,1)S(1)}, u32[]{:S(2)}, u32[]{:S(2)}) collective-permute-start(bf16[192,2560]{1,0:T(8,128)(2,1)} %fusion.212.uo_ref), channel_id=1, source_target_pairs={{0,4},{4,0},{1,5},{5,1},{2,6},{6,2},{3,7},{7,3}} | collective-permute-start | bytes 2949128 | tf_op jit(solution)/shard_map/ppermute | solution.py:237
  1450.8 76.3 %collective-permute-start.61 = (bf16[192,2560]{1,0:T(8,128)(2,1)S(1)}, bf16[192,2560]{1,0:T(8,128)(2,1)S(1)}, u32[]{:S(2)}, u32[]{:S(2)}) collective-permute-start(bf16[192,2560]{1,0:T(8,128)(2,1)S(1)} %fusion.227.uo_ref), channel_id=1, source_target_pairs={{0,4},{4,0},{1,5},{5,1},{2,6},{6,2},{3,7},{7,3}} | collective-permute-start | bytes 2949128 | tf_op jit(solution)/shard_map/ppermute | solution.py:237
  1521.9 77.9 %collective-permute-start.65 = (bf16[192,2560]{1,0:T(8,128)(2,1)S(1)}, bf16[192,2560]{1,0:T(8,128)(2,1)S(1)}, u32[]{:S(2)}, u32[]{:S(2)}) collective-permute-start(bf16[192,2560]{1,0:T(8,128)(2,1)S(1)} %fusion.245.uo_ref), channel_id=1, source_target_pairs={{0,4},{4,0},{1,5},{5,1},{2,6},{6,2},{3,7},{7,3}} | collective-permute-start | bytes 2949128 | tf_op jit(solution)/shard_map/ppermute | solution.py:237
  1527.1 590.2 %collective-permute-start.58 = (bf16[192,2560]{1,0:T(8,128)(2,1)}, bf16[192,2560]{1,0:T(8,128)(2,1)}, u32[]{:S(2)}, u32[]{:S(2)}) collective-permute-start(bf16[192,2560]{1,0:T(8,128)(2,1)} %fusion.364), channel_id=1, source_target_pairs={{3,1},{7,5}} | collective-permute-start | bytes 2949128 | tf_op jit(solution)/shard_map/ppermute | solution.py:302
  1597.3 42.0 %collective-permute-start.63 = (bf16[192,2560]{1,0:T(8,128)(2,1)}, bf16[192,2560]{1,0:T(8,128)(2,1)S(1)}, u32[]{:S(2)}, u32[]{:S(2)}) collective-permute-start(bf16[192,2560]{1,0:T(8,128)(2,1)} %fusion.360), channel_id=1, source_target_pairs={{0,1},{1,2},{2,3},{4,5},{5,6},{6,7}} | collective-permute-start | bytes 2949128 | tf_op jit(solution)/shard_map/ppermute | solution.py:293
  1599.8 75.4 %collective-permute-start.68 = (bf16[192,2560]{1,0:T(8,128)(2,1)S(1)}, bf16[192,2560]{1,0:T(8,128)(2,1)S(1)}, u32[]{:S(2)}, u32[]{:S(2)}) collective-permute-start(bf16[192,2560]{1,0:T(8,128)(2,1)S(1)} %fusion.254.uo_ref), channel_id=1, source_target_pairs={{1,5},{5,1},{2,6},{6,2},{3,7},{7,3}} | collective-permute-start | bytes 2949128 | tf_op jit(solution)/shard_map/ppermute | solution.py:237
  1671.1 43.6 %collective-permute-start.67 = (bf16[192,2560]{1,0:T(8,128)(2,1)}, bf16[192,2560]{1,0:T(8,128)(2,1)S(1)}, u32[]{:S(2)}, u32[]{:S(2)}) collective-permute-start(bf16[192,2560]{1,0:T(8,128)(2,1)} %fusion.359), channel_id=1, source_target_pairs={{0,1},{1,2},{2,3},{4,5},{5,6},{6,7}} | collective-permute-start | bytes 2949128 | tf_op jit(solution)/shard_map/ppermute | solution.py:293
  1675.2 76.5 %collective-permute-start.70 = (bf16[192,2560]{1,0:T(8,128)(2,1)S(1)}, bf16[192,2560]{1,0:T(8,128)(2,1)S(1)}, u32[]{:S(2)}, u32[]{:S(2)}) collective-permute-start(bf16[192,2560]{1,0:T(8,128)(2,1)S(1)} %fusion.260.uo_ref), channel_id=1, source_target_pairs={{1,5},{5,1},{2,6},{6,2},{3,7},{7,3}} | collective-permute-start | bytes 2949128 | tf_op jit(solution)/shard_map/ppermute | solution.py:237
  1748.1 43.2 %collective-permute-start.73 = (bf16[192,2560]{1,0:T(8,128)(2,1)S(1)}, bf16[192,2560]{1,0:T(8,128)(2,1)S(1)}, u32[]{:S(2)}, u32[]{:S(2)}) collective-permute-start(bf16[192,2560]{1,0:T(8,128)(2,1)S(1)} %fusion.358), channel_id=1, source_target_pairs={{1,2},{2,3},{5,6},{6,7}} | collective-permute-start | bytes 2949128 | tf_op jit(solution)/shard_map/ppermute | solution.py:293
  1751.7 77.5 %collective-permute-start.74 = (bf16[192,2560]{1,0:T(8,128)(2,1)S(1)}, bf16[192,2560]{1,0:T(8,128)(2,1)S(1)}, u32[]{:S(2)}, u32[]{:S(2)}) collective-permute-start(bf16[192,2560]{1,0:T(8,128)(2,1)S(1)} %fusion.269.uo_ref), channel_id=1, source_target_pairs={{1,5},{5,1},{2,6},{6,2},{3,7},{7,3}} | collective-permute-start | bytes 2949128 | tf_op jit(solution)/shard_map/ppermute | solution.py:237
  1825.6 41.5 %collective-permute-start.77 = (bf16[192,2560]{1,0:T(8,128)(2,1)}, bf16[192,2560]{1,0:T(8,128)(2,1)S(1)}, u32[]{:S(2)}, u32[]{:S(2)}) collective-permute-start(bf16[192,2560]{1,0:T(8,128)(2,1)} %fusion.357), channel_id=1, source_target_pairs={{1,2},{2,3},{5,6},{6,7}} | collective-permute-start | bytes 2949128 | tf_op jit(solution)/shard_map/ppermute | solution.py:293
  1829.3 72.4 %collective-permute-start.78 = (bf16[192,2560]{1,0:T(8,128)(2,1)S(1)}, bf16[192,2560]{1,0:T(8,128)(2,1)S(1)}, u32[]{:S(2)}, u32[]{:S(2)}) collective-permute-start(bf16[192,2560]{1,0:T(8,128)(2,1)S(1)} %fusion.281.uo_ref), channel_id=1, source_target_pairs={{2,6},{6,2},{3,7},{7,3}} | collective-permute-start | bytes 2949128 | tf_op jit(solution)/shard_map/ppermute | solution.py:237
  1898.2 220.8 %collective-permute-start.72 = (bf16[192,2560]{1,0:T(8,128)(2,1)}, bf16[192,2560]{1,0:T(8,128)(2,1)}, u32[]{:S(2)}, u32[]{:S(2)}) collective-permute-start(bf16[192,2560]{1,0:T(8,128)(2,1)} %fusion.357), channel_id=1, source_target_pairs={{3,2},{7,6}} | collective-permute-start | bytes 2949128 | tf_op jit(solution)/shard_map/ppermute | solution.py:302
  1901.6 43.8 %collective-permute-start.76 = (bf16[192,2560]{1,0:T(8,128)(2,1)}, bf16[192,2560]{1,0:T(8,128)(2,1)S(1)}, u32[]{:S(2)}, u32[]{:S(2)}) collective-permute-start(bf16[192,2560]{1,0:T(8,128)(2,1)} %fusion.356), channel_id=1, source_target_pairs={{1,2},{2,3},{5,6},{6,7}} | collective-permute-start | bytes 2949128 | tf_op jit(solution)/shard_map/ppermute | solution.py:293
  2116.0 75.8 %collective-permute-start.103 = (bf16[192,2560]{1,0:T(8,128)(2,1)}, bf16[192,2560]{1,0:T(8,128)(2,1)}, u32[]{:S(2)}, u32[]{:S(2)}) collective-permute-start(bf16[192,2560]{1,0:T(8,128)(2,1)} %fusion.360), channel_id=1, source_target_pairs={{3,1},{7,5}} | collective-permute-start | bytes 2949128 | tf_op jit(solution)/shard_map/ppermute | solution.py:302
  2117.3 74.5 %collective-permute-start.104 = (bf16[192,2560]{1,0:T(8,128)(2,1)}, bf16[192,2560]{1,0:T(8,128)(2,1)}, u32[]{:S(2)}, u32[]{:S(2)}) collective-permute-start(bf16[192,2560]{1,0:T(8,128)(2,1)} %fusion.356), channel_id=1, source_target_pairs={{3,2},{7,6}} | collective-permute-start | bytes 2949128 | tf_op jit(solution)/shard_map/ppermute | solution.py:302
  2123.9 72.1 %collective-permute-start.92 = (bf16[192,2560]{1,0:T(8,128)(2,1)S(1)}, bf16[192,2560]{1,0:T(8,128)(2,1)S(1)}, u32[]{:S(2)}, u32[]{:S(2)}) collective-permute-start(bf16[192,2560]{1,0:T(8,128)(2,1)S(1)} %fusion.317.uo_ref), channel_id=1, source_target_pairs={{3,7},{7,3}} | collective-permute-start | bytes 2949128 | tf_op jit(solution)/shard_map/ppermute | solution.py:237
  2237.2 81.8 %collective-permute-start.86 = (bf16[192,2560]{1,0:T(8,128)(2,1)}, bf16[192,2560]{1,0:T(8,128)(2,1)}, u32[]{:S(2)}, u32[]{:S(2)}) collective-permute-start(bf16[192,2560]{1,0:T(8,128)(2,1)} %fusion.359), channel_id=1, source_target_pairs={{3,1},{7,5}} | collective-permute-start | bytes 2949128 | tf_op jit(solution)/shard_map/ppermute | solution.py:302
  2238.5 81.3 %collective-permute-start.87 = (bf16[192,2560]{1,0:T(8,128)(2,1)}, bf16[192,2560]{1,0:T(8,128)(2,1)}, u32[]{:S(2)}, u32[]{:S(2)}) collective-permute-start(bf16[192,2560]{1,0:T(8,128)(2,1)} %fusion.355), channel_id=1, source_target_pairs={{3,2},{7,6}} | collective-permute-start | bytes 2949128 | tf_op jit(solution)/shard_map/ppermute | solution.py:302
  2240.2 83.5 %collective-permute-start.94 = (bf16[192,2560]{1,0:T(8,128)(2,1)}, bf16[192,2560]{1,0:T(8,128)(2,1)S(1)}, u32[]{:S(2)}, u32[]{:S(2)}) collective-permute-start(bf16[192,2560]{1,0:T(8,128)(2,1)} %fusion.380), channel_id=1, source_target_pairs={{3,4},{7,0}} | collective-permute-start | bytes 2949128 | tf_op jit(solution)/shard_map/ppermute | solution.py:303
  2241.0 99.2 %collective-permute-start.95 = (bf16[192,2560]{1,0:T(8,128)(2,1)}, bf16[192,2560]{1,0:T(8,128)(2,1)S(1)}, u32[]{:S(2)}, u32[]{:S(2)}) collective-permute-start(bf16[192,2560]{1,0:T(8,128)(2,1)} %fusion.364), channel_id=1, source_target_pairs={{3,5},{7,1}} | collective-permute-start | bytes 2949128 | tf_op jit(solution)/shard_map/ppermute | solution.py:303
  2243.9 97.0 %collective-permute-start.96 = (bf16[192,2560]{1,0:T(8,128)(2,1)}, bf16[192,2560]{1,0:T(8,128)(2,1)S(1)}, u32[]{:S(2)}, u32[]{:S(2)}) collective-permute-start(bf16[192,2560]{1,0:T(8,128)(2,1)} %fusion.357), channel_id=1, source_target_pairs={{3,6},{7,2}} | collective-permute-start | bytes 2949128 | tf_op jit(solution)/shard_map/ppermute | solution.py:303
  2319.8 60.8 %collective-permute-start.110 = (bf16[192,2560]{1,0:T(8,128)(2,1)}, bf16[192,2560]{1,0:T(8,128)(2,1)S(1)}, u32[]{:S(2)}, u32[]{:S(2)}) collective-permute-start(bf16[192,2560]{1,0:T(8,128)(2,1)} %fusion.376), channel_id=1, source_target_pairs={{3,4},{7,0}} | collective-permute-start | bytes 2949128 | tf_op jit(solution)/shard_map/ppermute | solution.py:303
  2323.7 57.6 %collective-permute-start.111 = (bf16[192,2560]{1,0:T(8,128)(2,1)}, bf16[192,2560]{1,0:T(8,128)(2,1)S(1)}, u32[]{:S(2)}, u32[]{:S(2)}) collective-permute-start(bf16[192,2560]{1,0:T(8,128)(2,1)} %fusion.360), channel_id=1, source_target_pairs={{3,5},{7,1}} | collective-permute-start | bytes 2949128 | tf_op jit(solution)/shard_map/ppermute | solution.py:303
  2340.2 41.9 %collective-permute-start.112 = (bf16[192,2560]{1,0:T(8,128)(2,1)}, bf16[192,2560]{1,0:T(8,128)(2,1)S(1)}, u32[]{:S(2)}, u32[]{:S(2)}) collective-permute-start(bf16[192,2560]{1,0:T(8,128)(2,1)} %fusion.356), channel_id=1, source_target_pairs={{3,6},{7,2}} | collective-permute-start | bytes 2949128 | tf_op jit(solution)/shard_map/ppermute | solution.py:303
  2341.7 41.7 %collective-permute-start.113 = (bf16[192,2560]{1,0:T(8,128)(2,1)S(1)}, bf16[192,2560]{1,0:T(8,128)(2,1)S(1)}, u32[]{:S(2)}, u32[]{:S(2)}) collective-permute-start(bf16[192,2560]{1,0:T(8,128)(2,1)S(1)} %copy-done.124), channel_id=1, source_target_pairs={{3,7},{7,3}} | collective-permute-start | bytes 2949128 | tf_op jit(solution)/shard_map/ppermute | solution.py:303
  2380.6 42.2 %collective-permute-start.98 = (bf16[192,2560]{1,0:T(8,128)(2,1)}, bf16[192,2560]{1,0:T(8,128)(2,1)S(1)}, u32[]{:S(2)}, u32[]{:S(2)}) collective-permute-start(bf16[192,2560]{1,0:T(8,128)(2,1)} %fusion.369), channel_id=1, source_target_pairs={{3,4},{7,0}} | collective-permute-start | bytes 2949128 | tf_op jit(solution)/shard_map/ppermute | solution.py:303
  2384.4 47.1 %collective-permute-start.99 = (bf16[192,2560]{1,0:T(8,128)(2,1)}, bf16[192,2560]{1,0:T(8,128)(2,1)S(1)}, u32[]{:S(2)}, u32[]{:S(2)}) collective-permute-start(bf16[192,2560]{1,0:T(8,128)(2,1)} %fusion.359), channel_id=1, source_target_pairs={{3,5},{7,1}} | collective-permute-start | bytes 2949128 | tf_op jit(solution)/shard_map/ppermute | solution.py:303
  2386.2 46.1 %collective-permute-start.100 = (bf16[192,2560]{1,0:T(8,128)(2,1)}, bf16[192,2560]{1,0:T(8,128)(2,1)S(1)}, u32[]{:S(2)}, u32[]{:S(2)}) collective-permute-start(bf16[192,2560]{1,0:T(8,128)(2,1)} %fusion.355), channel_id=1, source_target_pairs={{3,6},{7,2}} | collective-permute-start | bytes 2949128 | tf_op jit(solution)/shard_map/ppermute | solution.py:303
  (227 other events, 2693.6 us)

commit v2 on v1

--- a/solution.py
+++ b/solution.py
@@ -35,29 +35,39 @@
     return jnp.cos(angles), jnp.sin(angles)
 
 
-def attn_kernel(meta, q_ref, k_ref, v_ref, kc_ref, vc_ref, cos_ref, sin_ref, gain_ref, o_ref, ko_ref, vo_ref, *, n_group, q_scale):
+def attn_kernel(meta, x_ref, w_ref, wo_ref, kc_ref, vc_ref, cos_ref, sin_ref, gain0_ref, gain_ref, o_ref, ko_ref, vo_ref, h_ref, acc, *, n_group, q_scale):
+    head = pl.program_id(0)
     chunk = meta[1]
     is_glob = meta[2] == 1
-    head_dim = k_ref.shape[-1]
+    head_dim = ko_ref.shape[-1]
     half = head_dim // 2
-    rows = k_ref.shape[0]
+    rows = x_ref.shape[0]
+    n_rows = n_group * rows
+    q_cols = n_group * head_dim
     cos_b = cos_ref[...]
     sin_b = sin_ref[...]
 
+    @pl.when(head == 0)
+    def _():
+        x = x_ref[...].astype(jnp.float32)
+        mean_sq = jnp.mean(x * x, axis=-1, keepdims=True)
+        h_ref[...] = (x * lax.rsqrt(mean_sq + EPS) * (1.0 + gain0_ref[...])).astype(jnp.bfloat16)
+        acc[...] = jnp.zeros_like(acc)
+
     def norm_rope(x, gain):
-        x = x.astype(jnp.float32)
+        x = x.astype(jnp.bfloat16).astype(jnp.float32)
         mean_sq = jnp.mean(x * x, axis=-1, keepdims=True)
         x = x * lax.rsqrt(mean_sq + EPS) * (1.0 + gain)
         lo = x[:, :half]
         hi = x[:, half:]
         return jnp.concatenate([lo * cos_b - hi * sin_b, hi * cos_b + lo * sin_b], axis=-1).astype(jnp.bfloat16)
 
-    k_new = norm_rope(k_ref[...], gain_ref[1:2, :])
-    v_new = v_ref[...]
+    qkv = jnp.dot(h_ref[...], w_ref[...], preferred_element_type=jnp.float32)
+    k_new = norm_rope(qkv[:, q_cols:q_cols + head_dim], gain_ref[1:2, :])
+    v_new = qkv[:, q_cols + head_dim:].astype(jnp.bfloat16)
     ko_ref[0, 0] = k_new
     vo_ref[0, 0] = v_new
-    q_all = jnp.concatenate([norm_rope(q_ref[:, g * head_dim:(g + 1) * head_dim], gain_ref[0:1, :]) for g in range(n_group)], axis=0)
-    n_rows = n_group * rows
+    q_all = jnp.concatenate([norm_rope(qkv[:, g * head_dim:(g + 1) * head_dim], gain_ref[0:1, :]) for g in range(n_group)], axis=0)
     start = chunk * rows
     span = jnp.where(is_glob, kc_ref.shape[2], WINDOW)
     first = jnp.where(is_glob, 0, jnp.maximum(start - WINDOW, 0))
@@ -73,8 +83,8 @@
 
     def emit(res):
         res = res.astype(jnp.bfloat16)
-        for g in range(n_group):
-            o_ref[:, g * head_dim:(g + 1) * head_dim] = res[g * rows:(g + 1) * rows]
+        att = jnp.concatenate([res[g * rows:(g + 1) * rows] for g in range(n_group)], axis=1)
+        acc[...] += jnp.dot(att, wo_ref[...], preferred_element_type=jnp.float32)
 
     @pl.when(n_old == 0)
     def _():
@@ -102,12 +112,16 @@
     for n in range(1, kc_ref.shape[2] // KSTEP + 1):
         pl.when(n_old == n)(functools.partial(with_old, n))
 
-
-def attend(meta, qkv, k_cache, v_cache, cos_tab, sin_tab, gains, q_scale):
-    rows = qkv.shape[0]
+    @pl.when(head == pl.num_programs(0) - 1)
+    def _():
+        o_ref[...] = acc[...]
+
+
+def attend(meta, x, w_qkv, w_o, k_cache, v_cache, cos_tab, sin_tab, gain0, gains, q_scale):
+    rows, d_model = x.shape
     _, kv_heads, seq_len, head_dim = k_cache.shape
-    n_group = qkv.shape[1] // (kv_heads * head_dim) - 2
-    q_cols = n_group * kv_heads
+    cols = w_qkv.shape[1] // kv_heads
+    n_group = cols // head_dim - 2
     cache_in = pl.BlockSpec((1, 1, seq_len, head_dim), lambda h, m: (m[0], h, 0, 0))
     cache_out = pl.BlockSpec((1, 1, rows, head_dim), lambda h, m: (m[0], h, m[1], 0))
     table = pl.BlockSpec((rows, head_dim // 2), lambda h, m: (m[1], 0))
@@ -115,31 +129,33 @@
         num_scalar_prefetch=1,
         grid=(kv_heads,),
         in_specs=[
-            pl.BlockSpec((rows, n_group * head_dim), lambda h, m: (0, h)),
-            pl.BlockSpec((rows, head_dim), lambda h, m: (0, q_cols + h)),
-            pl.BlockSpec((rows, head_dim), lambda h, m: (0, q_cols + kv_heads + h)),
+            pl.BlockSpec((rows, d_model), lambda h, m: (0, 0)),
+            pl.BlockSpec((d_model, cols), lambda h, m: (0, h)),
+            pl.BlockSpec((n_group * head_dim, d_model), lambda h, m: (h, 0)),
             cache_in,
             cache_in,
             table,
             table,
+            pl.BlockSpec((1, d_model), lambda h, m: (0, 0)),
             pl.BlockSpec((2, head_dim), lambda h, m: (0, 0)),
         ],
-        out_specs=[pl.BlockSpec((rows, n_group * head_dim), lambda h, m: (0, h)), cache_out, cache_out],
+        out_specs=[pl.BlockSpec((rows, d_model), lambda h, m: (0, 0)), cache_out, cache_out],
+        scratch_shapes=[pltpu.VMEM((rows, d_model), jnp.bfloat16), pltpu.VMEM((rows, d_model), jnp.float32)],
     )
-    flops = 4 * rows * q_cols * head_dim * 900
+    flops = 2 * rows * d_model * (w_qkv.shape[1] + w_o.shape[0]) + 4 * rows * w_o.shape[0] * 900
     return pl.pallas_call(
         functools.partial(attn_kernel, n_group=n_group, q_scale=q_scale),
         grid_spec=grid_spec,
         out_shape=[
-            jax.ShapeDtypeStruct((rows, q_cols * head_dim), jnp.bfloat16),
+            jax.ShapeDtypeStruct((rows, d_model), jnp.float32),
             jax.ShapeDtypeStruct(k_cache.shape, k_cache.dtype),
             jax.ShapeDtypeStruct(v_cache.shape, v_cache.dtype),
         ],
         input_output_aliases={4: 1, 5: 2},
-        compiler_params=pltpu.CompilerParams(vmem_limit_bytes=32 * 2**20, dimension_semantics=("arbitrary",)),
-        cost_estimate=pl.CostEstimate(flops=flops, bytes_accessed=8 * 2**20, transcendentals=0),
+        compiler_params=pltpu.CompilerParams(vmem_limit_bytes=44 * 2**20, dimension_semantics=("arbitrary",)),
+        cost_estimate=pl.CostEstimate(flops=flops, bytes_accessed=20 * 2**20, transcendentals=0),
         name="attend",
-    )(meta, qkv, qkv, qkv, k_cache, v_cache, cos_tab, sin_tab, gains)
+    )(meta, x, w_qkv, w_o, k_cache, v_cache, cos_tab, sin_tab, gain0, gains)
 
 
 def mlp_kernel(uo_ref, ux_ref, wg_ref, wu_ref, wd_ref, do_ref, dx_ref, u_all, acc, act):
@@ -236,7 +252,12 @@
                 pairs = [(dev(t, s), dev(1 - t, s)) for s in stages for t in (0, 1)]
                 return lax.ppermute(x, axes, pairs)
 
-            wqkv_own = jnp.concatenate([wq_loc[0, 0], wk_loc[0, 0], wv_loc[0, 0]], axis=1)
+            n_group = q_heads // (w_k.shape[-1] // head_dim)
+            groups = []
+            for g in range(kv_heads):
+                at_kv = slice(g * head_dim, (g + 1) * head_dim)
+                groups += [wq_loc[0, 0][:, g * n_group * head_dim:(g + 1) * n_group * head_dim], wk_loc[0, 0][:, at_kv], wv_loc[0, 0][:, at_kv]]
+            wqkv_own = jnp.concatenate(groups, axis=1)
             wo_own = wo_loc[0, 0]
             later = range(1, n_stages)
             wqkv_oth = jnp.where(at_first, wqkv_own, swap(wqkv_own, later))
@@ -251,6 +272,7 @@
             n_slots = n_units + LAG * last_stage
             x_recv, x_mid, u_own, u_oth, d_own, d_oth = {}, {}, {}, {}, {}, {}
             pieces = {}
+            landed, landing = [], []
             for slot in range(n_slots + 2):
                 if slot < n_slots:
                     unit = jnp.clip(slot - LAG * stage, 0, n_units - 1)
@@ -263,23 +285,19 @@
                         x_own = lax.dynamic_slice(acts_loc, at_own, size).reshape(CHUNK, d_model)
                         x_two = lax.dynamic_slice(acts_loc, at_oth, size).reshape(CHUNK, d_model)
                         if slot >= LAG:
-                            x_own = jnp.where(at_first, x_own, x_recv[slot])
-                            x_two = jnp.where(at_first, x_two, x_recv[slot])
+                            x_got = lax.optimization_barrier((x_recv[slot], d_own[slot - 2]))[0]
+                            x_own = jnp.where(at_first, x_own, x_got)
+                            x_two = jnp.where(at_first, x_two, x_got)
+                        elif slot >= 2:
+                            x_own, x_two, _ = lax.optimization_barrier((x_own, x_two, d_own[slot - 2]))
                     else:
-                        x_own = x_two = x_recv[slot]
-                    if slot >= 2:
-                        x_own, x_two, _ = lax.optimization_barrier((x_own, x_two, d_own[slot - 2]))
-                    h_own = rms_norm(x_own, gains[0])
-                    h_two = rms_norm(x_two, gains[0]) if slot < n_units else h_own
-                    qkv_a = jnp.dot(h_own, wqkv_own, preferred_element_type=f32).astype(jnp.bfloat16)
+                        x_own = x_two = lax.optimization_barrier((x_recv[slot], d_own[slot - 2]))[0]
                     wqkv_two, wo_two = (wqkv_oth, wo_oth) if slot > fill else (wqkv_own, wo_own)
-                    qkv_b = jnp.dot(h_two, wqkv_two, preferred_element_type=f32).astype(jnp.bfloat16)
-                    att_a, caches[0], caches[1] = attend(meta, qkv_a, caches[0], caches[1], cos_tab, sin_tab, qk_gain, q_scale)
-                    att_b, caches[2], caches[3] = attend(meta, qkv_b, caches[2], caches[3], cos_tab, sin_tab, qk_gain, q_scale)
-                    o_b = jnp.dot(att_b, wo_two, preferred_element_type=f32)
+                    o_b, caches[2], caches[3] = attend(meta, x_two, wqkv_two, wo_two, caches[2], caches[3], cos_tab, sin_tab, gains[:1], qk_gain, q_scale)
                     if slot < n_units:
                         o_b = jnp.where(at_first, swap(o_b.astype(jnp.bfloat16), [0]).astype(f32), o_b)
-                    o_sum = (jnp.dot(att_a, wo_own, preferred_element_type=f32) + o_b).astype(jnp.bfloat16)
+                    o_a, caches[0], caches[1] = attend(meta, x_own, wqkv_own, wo_own, caches[0], caches[1], cos_tab, sin_tab, gains[:1], qk_gain, q_scale)
+                    o_sum = (o_a + o_b).astype(jnp.bfloat16)
                     x_mid[slot] = x_own + rms_norm(o_sum, gains[1])
                     u_own[slot] = rms_norm(x_mid[slot], gains[2])
                     u_oth[slot] = swap(u_own[slot], active(slot))
@@ -302,7 +320,8 @@
                             mine = lax.ppermute(x_out, axes, [(dev(t, last_stage), dev(t, target)) for t in (0, 1)])
                         theirs = lax.ppermute(x_out, axes, [(dev(t, last_stage), dev(1 - t, target)) for t in (0, 1)])
                         for key, val in (((0, stream, part), mine), ((1, stream, part), theirs)):
-                            pieces[key] = pieces[key] + val if key in pieces else val
+                            pieces.setdefault(key, []).append(val)
+                        landing = [(0, stream, part), (1, stream, part)]
 
                 if 0 <= slot - 1 < n_slots:
                     prev = slot - 1
@@ -311,12 +330,18 @@
                         u_in = lax.optimization_barrier((u_in, u_own[slot]))[0]
                     if x_out is not None:
                         u_in = lax.optimization_barrier((u_in, x_out))[0]
+                    for key in landed:
+                        *rest, newest = pieces[key]
+                        u_in, newest = lax.optimization_barrier((u_in, newest))
+                        pieces[key] = [sum(rest, newest)]
                     d_own[prev], d_send = mlp(u_in, u_oth[prev], w_gate, w_up, w_down)
                     d_oth[prev] = swap(d_send, active(prev))
+                landed, landing = landing, []
 
             per = n_chunks // n_stages
-            mine = [jnp.concatenate([pieces[(0, m, r)] for r in range(per)], axis=0) for m in range(n_own)]
-            theirs = [jnp.concatenate([pieces[(1, m, r)] for r in range(per)], axis=0) for m in range(n_own)]
+            total = {key: sum(vals[1:], vals[0]) for key, vals in pieces.items()}
+            mine = [jnp.concatenate([total[(0, m, r)] for r in range(per)], axis=0) for m in range(n_own)]
+            theirs = [jnp.concatenate([total[(1, m, r)] for r in range(per)], axis=0) for m in range(n_own)]
             on_zero = side == 0
             out = [jnp.where(on_zero, a, b) for a, b in zip(mine, theirs)] + [jnp.where(on_zero, b, a) for a, b in zip(mine, theirs)]
             return jnp.stack(out)[:, None]

time: 2470 us -> 2480 us (level)
  the two profiles are of different devices: /device:TPU:1 before, /device:TPU:3 now
where the time goes in v2:
time: 2480 us; the launch traced here: 2470 us
  Pallas kernels  1540 us (62%)
  starting transfers between devices  338 us (14%)
  waiting for transfers between devices  322 us (13%)
  other arithmetic  203 us (8%)
  local copies, waits for them, and re-layouts  68.6 us (3%)
    pallas_call x25, Pallas kernels, mlp(): pl.pallas_call(mlp_kernel, grid=(n_tiles + 1,), in_specs=[whole, whole, c...  924 us
    pallas_call x50, Pallas kernels, attend(): pl.pallas_call(functools.partial(attn_kernel, n_group=n_group, q_scale=q_...  612 us
    ppermute x68, waiting for transfers between devices, swap(): return lax.ppermute(x, axes, pairs)  306 us
    ppermute x68, starting transfers between devices, swap(): return lax.ppermute(x, axes, pairs)  134 us
    ppermute x12, starting transfers between devices, device_fn(): lax.ppermute(x_out, axes, [(dev(t, last_stage), dev(t, target)) for t in...  127 us
    reduce_sum x74, other arithmetic, rms_norm(): mean_sq = jnp.mean(x_f32 * x_f32, axis=-1, keepdims=True)  59.9 us
    unnamed x305, local copies, waits for them, and re-layouts  58.3 us
  transfers between devices with their start and end apart: 118, of which 13 were waited for; matrix products, arithmetic and copies ran while one was open for 7% of the time, Pallas kernels for 50%

profile of v2, /device:TPU:3, one launch (start us, length us, event | category | flops | bytes accessed | tf_op | source)
XLA Modules:
  0.0 2471.3 jit_solution(2833163798441916987)
XLA Ops:
  92.0 38.0 %mlp.25 = (f32[192,2560]{1,0:T(8,128)S(1)}, bf16[192,2560]{1,0:T(8,128)(2,1)S(1)}) custom-call(bf16[192,2560]{1,0:T(8,128)(2,1)} %get-tuple-element.337.uo_ref, bf16[192,2560]{1,0:T(8,128)(2,1)} %collective-permute-done.2.ux_ref, bf16[2560,5120]{1,0:T(8,128)(2,1)} %bitcast.248, bf16[2560,5120]{1,0:T(8,128)(2,1)} %bitcast.273, bf16[5120,2560]{1,0:T(8,128)(2,1)} %bitcast.298), custom_call_target="tpu_custom_call" | custom-call | flops 30198988800 | bytes 78643200 | tf_op jit(solution)/shard_map/mlp/pallas_call | solution.py:200
  164.6 37.5 %mlp.26 = (f32[192,2560]{1,0:T(8,128)S(1)}, bf16[192,2560]{1,0:T(8,128)(2,1)}) custom-call(bf16[192,2560]{1,0:T(8,128)(2,1)S(1)} %copy-done.91, bf16[192,2560]{1,0:T(8,128)(2,1)S(1)} %collective-permute-done.6.ux_ref, bf16[2560,5120]{1,0:T(8,128)(2,1)} %bitcast.249, bf16[2560,5120]{1,0:T(8,128)(2,1)} %bitcast.274, bf16[5120,2560]{1,0:T(8,128)(2,1)} %bitcast.299), custom_call_target="tpu_custom_call" | custom-call | flops 30198988800 | bytes 78643200 | tf_op jit(solution)/shard_map/mlp/pallas_call | solution.py:200
  210.0 219.5 %collective-permute-done.8 = bf16[1024,2560]{1,0:T(8,128)(2,1)} collective-permute-done((bf16[1024,2560]{1,0:T(8,128)(2,1)}, bf16[1024,2560]{1,0:T(8,128)(2,1)}, u32[]{:S(2)}, u32[]{:S(2)}) %collective-permute-start.8) | collective-permute-done | bytes 5242912 | tf_op jit(solution)/shard_map/ppermute | solution.py:253
  462.1 14.4 attend.56
  478.2 36.6 %mlp.27 = (f32[192,2560]{1,0:T(8,128)S(1)}, bf16[192,2560]{1,0:T(8,128)(2,1)S(1)}) custom-call(bf16[192,2560]{1,0:T(8,128)(2,1)S(1)} %copy-done.88, bf16[192,2560]{1,0:T(8,128)(2,1)S(1)} %collective-permute-done.11.ux_ref, bf16[2560,5120]{1,0:T(8,128)(2,1)} %bitcast.250, bf16[2560,5120]{1,0:T(8,128)(2,1)} %bitcast.275, bf16[5120,2560]{1,0:T(8,128)(2,1)} %bitcast.300), custom_call_target="tpu_custom_call" | custom-call | flops 30198988800 | bytes 78643200 | tf_op jit(solution)/shard_map/mlp/pallas_call | solution.py:200
  548.6 37.5 %mlp.28 = (f32[192,2560]{1,0:T(8,128)S(1)}, bf16[192,2560]{1,0:T(8,128)(2,1)}) custom-call(bf16[192,2560]{1,0:T(8,128)(2,1)S(1)} %fusion.26.uo_ref, bf16[192,2560]{1,0:T(8,128)(2,1)S(1)} %collective-permute-done.16.ux_ref, bf16[2560,5120]{1,0:T(8,128)(2,1)} %bitcast.251, bf16[2560,5120]{1,0:T(8,128)(2,1)} %bitcast.276, bf16[5120,2560]{1,0:T(8,128)(2,1)} %bitcast.301), custom_call_target="tpu_custom_call" | custom-call | flops 30198988800 | bytes 78643200 | tf_op jit(solution)/shard_map/mlp/pallas_call | solution.py:200
  611.8 14.4 attend.60
  628.7 36.6 %mlp.29 = (f32[192,2560]{1,0:T(8,128)S(1)}, bf16[192,2560]{1,0:T(8,128)(2,1)S(1)}) custom-call(bf16[192,2560]{1,0:T(8,128)(2,1)S(1)} %copy-done.87, bf16[192,2560]{1,0:T(8,128)(2,1)S(1)} %collective-permute-done.20.ux_ref, bf16[2560,5120]{1,0:T(8,128)(2,1)} %bitcast.252, bf16[2560,5120]{1,0:T(8,128)(2,1)} %bitcast.277, bf16[5120,2560]{1,0:T(8,128)(2,1)} %bitcast.302), custom_call_target="tpu_custom_call" | custom-call | flops 30198988800 | bytes 78643200 | tf_op jit(solution)/shard_map/mlp/pallas_call | solution.py:200
  707.2 36.6 %mlp.30 = (f32[192,2560]{1,0:T(8,128)S(1)}, bf16[192,2560]{1,0:T(8,128)(2,1)S(1)}) custom-call(bf16[192,2560]{1,0:T(8,128)(2,1)S(1)} %copy-done.89, bf16[192,2560]{1,0:T(8,128)(2,1)S(1)} %collective-permute-done.23.ux_ref, bf16[2560,5120]{1,0:T(8,128)(2,1)} %bitcast.253, bf16[2560,5120]{1,0:T(8,128)(2,1)} %bitcast.278, bf16[5120,2560]{1,0:T(8,128)(2,1)} %bitcast.303), custom_call_target="tpu_custom_call" | custom-call | flops 30198988800 | bytes 78643200 | tf_op jit(solution)/shard_map/mlp/pallas_call | solution.py:200
  761.5 14.4 attend.64
  778.4 36.6 %mlp.31 = (f32[192,2560]{1,0:T(8,128)S(1)}, bf16[192,2560]{1,0:T(8,128)(2,1)S(1)}) custom-call(bf16[192,2560]{1,0:T(8,128)(2,1)S(1)} %fusion.53.uo_ref, bf16[192,2560]{1,0:T(8,128)(2,1)S(1)} %collective-permute-done.28.ux_ref, bf16[2560,5120]{1,0:T(8,128)(2,1)} %bitcast.254, bf16[2560,5120]{1,0:T(8,128)(2,1)} %bitcast.279, bf16[5120,2560]{1,0:T(8,128)(2,1)} %bitcast.304), custom_call_target="tpu_custom_call" | custom-call | flops 30198988800 | bytes 78643200 | tf_op jit(solution)/shard_map/mlp/pallas_call | solution.py:200
  834.9 28.5 %collective-permute-start.32 = (bf16[192,2560]{1,0:T(8,128)(2,1)}, bf16[192,2560]{1,0:T(8,128)(2,1)S(1)}, u32[]{:S(2)}, u32[]{:S(2)}) collective-permute-start(bf16[192,2560]{1,0:T(8,128)(2,1)} %fusion.65.uo_ref), channel_id=1, source_target_pairs={{0,4},{4,0},{1,5},{5,1},{2,6},{6,2}} | collective-permute-start | bytes 2949128 | tf_op jit(solution)/shard_map/ppermute | solution.py:253
  890.2 36.6 %mlp.32 = (f32[192,2560]{1,0:T(8,128)S(1)}, bf16[192,2560]{1,0:T(8,128)(2,1)S(1)}) custom-call(bf16[192,2560]{1,0:T(8,128)(2,1)S(1)} %copy-done.90, bf16[192,2560]{1,0:T(8,128)(2,1)S(1)} %collective-permute-done.32.ux_ref, bf16[2560,5120]{1,0:T(8,128)(2,1)} %bitcast.255, bf16[2560,5120]{1,0:T(8,128)(2,1)} %bitcast.280, bf16[5120,2560]{1,0:T(8,128)(2,1)} %bitcast.305), custom_call_target="tpu_custom_call" | custom-call | flops 30198988800 | bytes 78643200 | tf_op jit(solution)/shard_map/mlp/pallas_call | solution.py:200
  946.0 14.3 attend.68
  962.4 36.6 %mlp.33 = (f32[192,2560]{1,0:T(8,128)S(1)}, bf16[192,2560]{1,0:T(8,128)(2,1)S(1)}) custom-call(bf16[192,2560]{1,0:T(8,128)(2,1)S(1)} %fusion.71.uo_ref, bf16[192,2560]{1,0:T(8,128)(2,1)S(1)} %collective-permute-done.35.ux_ref, bf16[2560,5120]{1,0:T(8,128)(2,1)} %bitcast.256, bf16[2560,5120]{1,0:T(8,128)(2,1)} %bitcast.281, bf16[5120,2560]{1,0:T(8,128)(2,1)} %bitcast.306), custom_call_target="tpu_custom_call" | custom-call | flops 30198988800 | bytes 78643200 | tf_op jit(solution)/shard_map/mlp/pallas_call | solution.py:200
  1035.8 37.5 %mlp.34 = (f32[192,2560]{1,0:T(8,128)S(1)}, bf16[192,2560]{1,0:T(8,128)(2,1)}) custom-call(bf16[192,2560]{1,0:T(8,128)(2,1)S(1)} %fusion.80.uo_ref, bf16[192,2560]{1,0:T(8,128)(2,1)S(1)} %collective-permute-done.40.ux_ref, bf16[2560,5120]{1,0:T(8,128)(2,1)} %bitcast.257, bf16[2560,5120]{1,0:T(8,128)(2,1)} %bitcast.282, bf16[5120,2560]{1,0:T(8,128)(2,1)} %bitcast.307), custom_call_target="tpu_custom_call" | custom-call | flops 30198988800 | bytes 78643200 | tf_op jit(solution)/shard_map/mlp/pallas_call | solution.py:200
  1115.7 68.4 %collective-permute-start.47 = (bf16[192,2560]{1,0:T(8,128)(2,1)}, bf16[192,2560]{1,0:T(8,128)(2,1)}, u32[]{:S(2)}, u32[]{:S(2)}) collective-permute-start(bf16[192,2560]{1,0:T(8,128)(2,1)} %fusion.253), channel_id=1, source_target_pairs={{3,0},{7,4}} | collective-permute-start | bytes 2949128 | tf_op jit(solution)/shard_map/ppermute | solution.py:320
  1186.4 14.2 attend.72
  1203.3 36.6 %mlp.35 = (f32[192,2560]{1,0:T(8,128)S(1)}, bf16[192,2560]{1,0:T(8,128)(2,1)S(1)}) custom-call(bf16[192,2560]{1,0:T(8,128)(2,1)S(1)} %copy-done.82, bf16[192,2560]{1,0:T(8,128)(2,1)S(1)} %collective-permute-done.44.ux_ref, bf16[2560,5120]{1,0:T(8,128)(2,1)} %bitcast.258, bf16[2560,5120]{1,0:T(8,128)(2,1)} %bitcast.283, bf16[5120,2560]{1,0:T(8,128)(2,1)} %bitcast.308), custom_call_target="tpu_custom_call" | custom-call | flops 30198988800 | bytes 78643200 | tf_op jit(solution)/shard_map/mlp/pallas_call | solution.py:200
  1285.7 36.6 %mlp.36 = (f32[192,2560]{1,0:T(8,128)S(1)}, bf16[192,2560]{1,0:T(8,128)(2,1)S(1)}) custom-call(bf16[192,2560]{1,0:T(8,128)(2,1)S(1)} %fusion.98.uo_ref, bf16[192,2560]{1,0:T(8,128)(2,1)S(1)} %collective-permute-done.49.ux_ref, bf16[2560,5120]{1,0:T(8,128)(2,1)} %bitcast.259, bf16[2560,5120]{1,0:T(8,128)(2,1)} %bitcast.284, bf16[5120,2560]{1,0:T(8,128)(2,1)} %bitcast.309), custom_call_target="tpu_custom_call" | custom-call | flops 30198988800 | bytes 78643200 | tf_op jit(solution)/shard_map/mlp/pallas_call | solution.py:200
  1343.7 14.3 attend.76
  1366.3 36.6 %mlp.37 = (f32[192,2560]{1,0:T(8,128)S(1)}, bf16[192,2560]{1,0:T(8,128)(2,1)S(1)}) custom-call(bf16[192,2560]{1,0:T(8,128)(2,1)S(1)} %fusion.107.uo_ref, bf16[192,2560]{1,0:T(8,128)(2,1)S(1)} %collective-permute-done.56.ux_ref, bf16[2560,5120]{1,0:T(8,128)(2,1)} %bitcast.260, bf16[2560,5120]{1,0:T(8,128)(2,1)} %bitcast.285, bf16[5120,2560]{1,0:T(8,128)(2,1)} %bitcast.310), custom_call_target="tpu_custom_call" | custom-call | flops 30198988800 | bytes 78643200 | tf_op jit(solution)/shard_map/mlp/pallas_call | solution.py:200
  1448.8 36.6 %mlp.38 = (f32[192,2560]{1,0:T(8,128)S(1)}, bf16[192,2560]{1,0:T(8,128)(2,1)S(1)}) custom-call(bf16[192,2560]{1,0:T(8,128)(2,1)S(1)} %fusion.119.uo_ref, bf16[192,2560]{1,0:T(8,128)(2,1)S(1)} %collective-permute-done.62.ux_ref, bf16[2560,5120]{1,0:T(8,128)(2,1)} %bitcast.261, bf16[2560,5120]{1,0:T(8,128)(2,1)} %bitcast.286, bf16[5120,2560]{1,0:T(8,128)(2,1)} %bitcast.311), custom_call_target="tpu_custom_call" | custom-call | flops 30198988800 | bytes 78643200 | tf_op jit(solution)/shard_map/mlp/pallas_call | solution.py:200
  1507.8 14.1 attend.80
  1528.5 36.6 %mlp.39 = (f32[192,2560]{1,0:T(8,128)S(1)}, bf16[192,2560]{1,0:T(8,128)(2,1)S(1)}) custom-call(bf16[192,2560]{1,0:T(8,128)(2,1)S(1)} %fusion.125.uo_ref, bf16[192,2560]{1,0:T(8,128)(2,1)S(1)} %collective-permute-done.67.ux_ref, bf16[2560,5120]{1,0:T(8,128)(2,1)} %bitcast.262, bf16[2560,5120]{1,0:T(8,128)(2,1)} %bitcast.287, bf16[5120,2560]{1,0:T(8,128)(2,1)} %bitcast.312), custom_call_target="tpu_custom_call" | custom-call | flops 30198988800 | bytes 78643200 | tf_op jit(solution)/shard_map/mlp/pallas_call | solution.py:200
  1577.5 13.0 attend.82
  1593.9 19.3 collective-permute-done.68
  1615.1 37.6 %mlp.40 = (f32[192,2560]{1,0:T(8,128)S(1)}, bf16[192,2560]{1,0:T(8,128)(2,1)}) custom-call(bf16[192,2560]{1,0:T(8,128)(2,1)S(1)} %fusion.134.uo_ref, bf16[192,2560]{1,0:T(8,128)(2,1)S(1)} %collective-permute-done.73.ux_ref, bf16[2560,5120]{1,0:T(8,128)(2,1)} %bitcast.263, bf16[2560,5120]{1,0:T(8,128)(2,1)} %bitcast.288, bf16[5120,2560]{1,0:T(8,128)(2,1)} %bitcast.313), custom_call_target="tpu_custom_call" | custom-call | flops 30198988800 | bytes 78643200 | tf_op jit(solution)/shard_map/mlp/pallas_call | solution.py:200
  1705.1 14.1 attend.84
  1726.1 36.6 %mlp.41 = (f32[192,2560]{1,0:T(8,128)S(1)}, bf16[192,2560]{1,0:T(8,128)(2,1)S(1)}) custom-call(bf16[192,2560]{1,0:T(8,128)(2,1)S(1)} %copy-done.84, bf16[192,2560]{1,0:T(8,128)(2,1)S(1)} %collective-permute-done.78.ux_ref, bf16[2560,5120]{1,0:T(8,128)(2,1)} %bitcast.264, bf16[2560,5120]{1,0:T(8,128)(2,1)} %bitcast.289, bf16[5120,2560]{1,0:T(8,128)(2,1)} %bitcast.314), custom_call_target="tpu_custom_call" | custom-call | flops 30198988800 | bytes 78643200 | tf_op jit(solution)/shard_map/mlp/pallas_call | solution.py:200
  1777.8 13.0 attend.86
  1796.9 37.6 %mlp.42 = (f32[192,2560]{1,0:T(8,128)S(1)}, bf16[192,2560]{1,0:T(8,128)(2,1)}) custom-call(bf16[192,2560]{1,0:T(8,128)(2,1)S(1)} %fusion.152.uo_ref, bf16[192,2560]{1,0:T(8,128)(2,1)S(1)} %collective-permute-done.82.ux_ref, bf16[2560,5120]{1,0:T(8,128)(2,1)} %bitcast.265, bf16[2560,5120]{1,0:T(8,128)(2,1)} %bitcast.290, bf16[5120,2560]{1,0:T(8,128)(2,1)} %bitcast.315), custom_call_target="tpu_custom_call" | custom-call | flops 30198988800 | bytes 78643200 | tf_op jit(solution)/shard_map/mlp/pallas_call | solution.py:200
  1873.8 13.1 attend.89
  1886.8 14.1 attend.88
  1908.0 36.6 %mlp.43 = (f32[192,2560]{1,0:T(8,128)S(1)}, bf16[192,2560]{1,0:T(8,128)(2,1)S(1)}) custom-call(bf16[192,2560]{1,0:T(8,128)(2,1)S(1)} %copy-done.85, bf16[192,2560]{1,0:T(8,128)(2,1)S(1)} %collective-permute-done.88.ux_ref, bf16[2560,5120]{1,0:T(8,128)(2,1)} %bitcast.266, bf16[2560,5120]{1,0:T(8,128)(2,1)} %bitcast.291, bf16[5120,2560]{1,0:T(8,128)(2,1)} %bitcast.316), custom_call_target="tpu_custom_call" | custom-call | flops 30198988800 | bytes 78643200 | tf_op jit(solution)/shard_map/mlp/pallas_call | solution.py:200
  1960.6 13.5 attend.90
  1980.0 37.5 %mlp.44 = (f32[192,2560]{1,0:T(8,128)S(1)}, bf16[192,2560]{1,0:T(8,128)(2,1)}) custom-call(bf16[192,2560]{1,0:T(8,128)(2,1)S(1)} %fusion.173.uo_ref, bf16[192,2560]{1,0:T(8,128)(2,1)S(1)} %collective-permute-done.93.ux_ref, bf16[2560,5120]{1,0:T(8,128)(2,1)} %bitcast.267, bf16[2560,5120]{1,0:T(8,128)(2,1)} %bitcast.292, bf16[5120,2560]{1,0:T(8,128)(2,1)} %bitcast.317), custom_call_target="tpu_custom_call" | custom-call | flops 30198988800 | bytes 78643200 | tf_op jit(solution)/shard_map/mlp/pallas_call | solution.py:200
  2055.5 13.1 attend.93
  2068.5 14.1 attend.92
  2091.3 36.6 %mlp.45 = (f32[192,2560]{1,0:T(8,128)S(1)}, bf16[192,2560]{1,0:T(8,128)(2,1)S(1)}) custom-call(bf16[192,2560]{1,0:T(8,128)(2,1)S(1)} %copy-done.86, bf16[192,2560]{1,0:T(8,128)(2,1)S(1)} %collective-permute-done.97.ux_ref, bf16[2560,5120]{1,0:T(8,128)(2,1)} %bitcast.268, bf16[2560,5120]{1,0:T(8,128)(2,1)} %bitcast.293, bf16[5120,2560]{1,0:T(8,128)(2,1)} %bitcast.318), custom_call_target="tpu_custom_call" | custom-call | flops 30198988800 | bytes 78643200 | tf_op jit(solution)/shard_map/mlp/pallas_call | solution.py:200
  2143.9 13.5 attend.94
  2162.5 37.6 %mlp.46 = (f32[192,2560]{1,0:T(8,128)S(1)}, bf16[192,2560]{1,0:T(8,128)(2,1)}) custom-call(bf16[192,2560]{1,0:T(8,128)(2,1)S(1)} %fusion.188.uo_ref, bf16[192,2560]{1,0:T(8,128)(2,1)S(1)} %collective-permute-done.103.ux_ref, bf16[2560,5120]{1,0:T(8,128)(2,1)} %bitcast.269, bf16[2560,5120]{1,0:T(8,128)(2,1)} %bitcast.294, bf16[5120,2560]{1,0:T(8,128)(2,1)} %bitcast.319), custom_call_target="tpu_custom_call" | custom-call | flops 30198988800 | bytes 78643200 | tf_op jit(solution)/shard_map/mlp/pallas_call | solution.py:200
  2232.4 13.1 attend.97
  2245.5 14.1 attend.96
  2265.0 36.6 %mlp.47 = (f32[192,2560]{1,0:T(8,128)S(1)}, bf16[192,2560]{1,0:T(8,128)(2,1)S(1)}) custom-call(bf16[192,2560]{1,0:T(8,128)(2,1)S(1)} %copy-done.83, bf16[192,2560]{1,0:T(8,128)(2,1)S(1)} %collective-permute-done.108.ux_ref, bf16[2560,5120]{1,0:T(8,128)(2,1)} %bitcast.270, bf16[2560,5120]{1,0:T(8,128)(2,1)} %bitcast.295, bf16[5120,2560]{1,0:T(8,128)(2,1)} %bitcast.320), custom_call_target="tpu_custom_call" | custom-call | flops 30198988800 | bytes 78643200 | tf_op jit(solution)/shard_map/mlp/pallas_call | solution.py:200
  2316.7 13.4 attend.98
  2337.9 36.6 %mlp.48 = (f32[192,2560]{1,0:T(8,128)S(1)}, bf16[192,2560]{1,0:T(8,128)(2,1)S(1)}) custom-call(bf16[192,2560]{1,0:T(8,128)(2,1)S(1)} %fusion.206.uo_ref, bf16[192,2560]{1,0:T(8,128)(2,1)S(1)} %collective-permute-done.111.ux_ref, bf16[2560,5120]{1,0:T(8,128)(2,1)} %bitcast.271, bf16[2560,5120]{1,0:T(8,128)(2,1)} %bitcast.296, bf16[5120,2560]{1,0:T(8,128)(2,1)} %bitcast.321), custom_call_target="tpu_custom_call" | custom-call | flops 30198988800 | bytes 78643200 | tf_op jit(solution)/shard_map/mlp/pallas_call | solution.py:200
  2395.6 37.0 %mlp.49 = (f32[192,2560]{1,0:T(8,128)S(1)}, bf16[192,2560]{1,0:T(8,128)(2,1)S(1)}) custom-call(bf16[192,2560]{1,0:T(8,128)(2,1)S(1)} %fusion.215.uo_ref, bf16[192,2560]{1,0:T(8,128)(2,1)S(1)} %collective-permute-done.115.ux_ref, bf16[2560,5120]{1,0:T(8,128)(2,1)} %bitcast.272, bf16[2560,5120]{1,0:T(8,128)(2,1)} %bitcast.297, bf16[5120,2560]{1,0:T(8,128)(2,1)} %bitcast.322), custom_call_target="tpu_custom_call" | custom-call | flops 30198988800 | bytes 78643200 | tf_op jit(solution)/shard_map/mlp/pallas_call | solution.py:200
  (830 shorter events, 945.6 us)
Async XLA Ops:
  88.7 347.8 %collective-permute-start.7 = (bf16[2560,2048]{1,0:T(8,128)(2,1)}, bf16[2560,2048]{1,0:T(8,128)(2,1)}, u32[]{:S(2)}, u32[]{:S(2)}) collective-permute-start(bf16[2560,2048]{1,0:T(8,128)(2,1)} %slice_dynamic-update-slice_fusion.2.w_ref), channel_id=1, source_target_pairs={{1,5},{5,1},{2,6},{6,2},{3,7},{7,3}} | collective-permute-start | bytes 31457288 | tf_op jit(solution)/shard_map/ppermute | solution.py:253
  144.1 285.4 %collective-permute-start.8 = (bf16[1024,2560]{1,0:T(8,128)(2,1)}, bf16[1024,2560]{1,0:T(8,128)(2,1)}, u32[]{:S(2)}, u32[]{:S(2)}) collective-permute-start(bf16[1024,2560]{1,0:T(8,128)(2,1)} %bitcast.216), channel_id=1, source_target_pairs={{1,5},{5,1},{2,6},{6,2},{3,7},{7,3}} | collective-permute-start | bytes 15728648 | tf_op jit(solution)/shard_map/ppermute | solution.py:253
  205.1 272.8 %collective-permute-start.11 = (bf16[192,2560]{1,0:T(8,128)(2,1)}, bf16[192,2560]{1,0:T(8,128)(2,1)S(1)}, u32[]{:S(2)}, u32[]{:S(2)}) collective-permute-start(bf16[192,2560]{1,0:T(8,128)(2,1)} %fusion.17.uo_ref), channel_id=1, source_target_pairs={{0,4},{4,0}} | collective-permute-start | bytes 2949128 | tf_op jit(solution)/shard_map/ppermute | solution.py:253
  704.6 73.8 %collective-permute-start.28 = (bf16[192,2560]{1,0:T(8,128)(2,1)S(1)}, bf16[192,2560]{1,0:T(8,128)(2,1)S(1)}, u32[]{:S(2)}, u32[]{:S(2)}) collective-permute-start(bf16[192,2560]{1,0:T(8,128)(2,1)S(1)} %fusion.53.uo_ref), channel_id=1, source_target_pairs={{0,4},{4,0},{1,5},{5,1},{2,6},{6,2}} | collective-permute-start | bytes 2949128 | tf_op jit(solution)/shard_map/ppermute | solution.py:253
  881.2 81.2 %collective-permute-start.35 = (bf16[192,2560]{1,0:T(8,128)(2,1)S(1)}, bf16[192,2560]{1,0:T(8,128)(2,1)S(1)}, u32[]{:S(2)}, u32[]{:S(2)}) collective-permute-start(bf16[192,2560]{1,0:T(8,128)(2,1)S(1)} %fusion.71.uo_ref), channel_id=1, source_target_pairs={{0,4},{4,0},{1,5},{5,1},{2,6},{6,2}} | collective-permute-start | bytes 2949128 | tf_op jit(solution)/shard_map/ppermute | solution.py:253
  1076.4 126.9 %collective-permute-start.44 = (bf16[192,2560]{1,0:T(8,128)(2,1)}, bf16[192,2560]{1,0:T(8,128)(2,1)S(1)}, u32[]{:S(2)}, u32[]{:S(2)}) collective-permute-start(bf16[192,2560]{1,0:T(8,128)(2,1)} %fusion.92.uo_ref), channel_id=1, source_target_pairs={{0,4},{4,0},{1,5},{5,1},{2,6},{6,2},{3,7},{7,3}} | collective-permute-start | bytes 2949128 | tf_op jit(solution)/shard_map/ppermute | solution.py:253
  1110.0 90.6 %collective-permute-start.41 = (bf16[192,2560]{1,0:T(8,128)(2,1)S(1)}, bf16[192,2560]{1,0:T(8,128)(2,1)S(1)}, u32[]{:S(2)}, u32[]{:S(2)}) collective-permute-start(bf16[192,2560]{1,0:T(8,128)(2,1)S(1)} %convert_element_type.884), channel_id=1, source_target_pairs={{0,4},{4,0}} | collective-permute-start | bytes 2949128 | tf_op jit(solution)/shard_map/ppermute | solution.py:253
  1114.4 125.5 %collective-permute-start.43 = (bf16[192,2560]{1,0:T(8,128)(2,1)}, bf16[192,2560]{1,0:T(8,128)(2,1)}, u32[]{:S(2)}, u32[]{:S(2)}) collective-permute-start(bf16[192,2560]{1,0:T(8,128)(2,1)} %fusion.253), channel_id=1, source_target_pairs={{0,1},{1,2},{2,3},{4,5},{5,6},{6,7}} | collective-permute-start | bytes 2949128 | tf_op jit(solution)/shard_map/ppermute | solution.py:311
  1115.7 166.5 %collective-permute-start.47 = (bf16[192,2560]{1,0:T(8,128)(2,1)}, bf16[192,2560]{1,0:T(8,128)(2,1)}, u32[]{:S(2)}, u32[]{:S(2)}) collective-permute-start(bf16[192,2560]{1,0:T(8,128)(2,1)} %fusion.253), channel_id=1, source_target_pairs={{3,0},{7,4}} | collective-permute-start | bytes 2949128 | tf_op jit(solution)/shard_map/ppermute | solution.py:320
  1184.1 100.4 %collective-permute-start.48 = (bf16[192,2560]{1,0:T(8,128)(2,1)}, bf16[192,2560]{1,0:T(8,128)(2,1)}, u32[]{:S(2)}, u32[]{:S(2)}) collective-permute-start(bf16[192,2560]{1,0:T(8,128)(2,1)} %fusion.253), channel_id=1, source_target_pairs={{3,4},{7,0}} | collective-permute-start | bytes 2949128 | tf_op jit(solution)/shard_map/ppermute | solution.py:321
  1203.1 82.6 %collective-permute-start.49 = (bf16[192,2560]{1,0:T(8,128)(2,1)S(1)}, bf16[192,2560]{1,0:T(8,128)(2,1)S(1)}, u32[]{:S(2)}, u32[]{:S(2)}) collective-permute-start(bf16[192,2560]{1,0:T(8,128)(2,1)S(1)} %fusion.98.uo_ref), channel_id=1, source_target_pairs={{0,4},{4,0},{1,5},{5,1},{2,6},{6,2},{3,7},{7,3}} | collective-permute-start | bytes 2949128 | tf_op jit(solution)/shard_map/ppermute | solution.py:253
  1272.3 91.5 %collective-permute-start.54 = (bf16[192,2560]{1,0:T(8,128)(2,1)}, bf16[192,2560]{1,0:T(8,128)(2,1)}, u32[]{:S(2)}, u32[]{:S(2)}) collective-permute-start(bf16[192,2560]{1,0:T(8,128)(2,1)} %fusion.251), channel_id=1, source_target_pairs={{3,0},{7,4}} | collective-permute-start | bytes 2949128 | tf_op jit(solution)/shard_map/ppermute | solution.py:320
  1282.2 83.8 %collective-permute-start.55 = (bf16[192,2560]{1,0:T(8,128)(2,1)}, bf16[192,2560]{1,0:T(8,128)(2,1)}, u32[]{:S(2)}, u32[]{:S(2)}) collective-permute-start(bf16[192,2560]{1,0:T(8,128)(2,1)} %fusion.251), channel_id=1, source_target_pairs={{3,4},{7,0}} | collective-permute-start | bytes 2949128 | tf_op jit(solution)/shard_map/ppermute | solution.py:321
  1284.5 81.8 %collective-permute-start.56 = (bf16[192,2560]{1,0:T(8,128)(2,1)S(1)}, bf16[192,2560]{1,0:T(8,128)(2,1)S(1)}, u32[]{:S(2)}, u32[]{:S(2)}) collective-permute-start(bf16[192,2560]{1,0:T(8,128)(2,1)S(1)} %fusion.107.uo_ref), channel_id=1, source_target_pairs={{0,4},{4,0},{1,5},{5,1},{2,6},{6,2},{3,7},{7,3}} | collective-permute-start | bytes 2949128 | tf_op jit(solution)/shard_map/ppermute | solution.py:253
  1342.4 61.8 %collective-permute-start.51 = (bf16[192,2560]{1,0:T(8,128)(2,1)}, bf16[192,2560]{1,0:T(8,128)(2,1)}, u32[]{:S(2)}, u32[]{:S(2)}) collective-permute-start(bf16[192,2560]{1,0:T(8,128)(2,1)} %fusion.250), channel_id=1, source_target_pairs={{0,1},{1,2},{2,3},{4,5},{5,6},{6,7}} | collective-permute-start | bytes 2949128 | tf_op jit(solution)/shard_map/ppermute | solution.py:311
  1358.1 87.2 %collective-permute-start.60 = (bf16[192,2560]{1,0:T(8,128)(2,1)}, bf16[192,2560]{1,0:T(8,128)(2,1)}, u32[]{:S(2)}, u32[]{:S(2)}) collective-permute-start(bf16[192,2560]{1,0:T(8,128)(2,1)} %fusion.250), channel_id=1, source_target_pairs={{3,0},{7,4}} | collective-permute-start | bytes 2949128 | tf_op jit(solution)/shard_map/ppermute | solution.py:320
  1363.8 83.8 %collective-permute-start.61 = (bf16[192,2560]{1,0:T(8,128)(2,1)}, bf16[192,2560]{1,0:T(8,128)(2,1)}, u32[]{:S(2)}, u32[]{:S(2)}) collective-permute-start(bf16[192,2560]{1,0:T(8,128)(2,1)} %fusion.250), channel_id=1, source_target_pairs={{3,4},{7,0}} | collective-permute-start | bytes 2949128 | tf_op jit(solution)/shard_map/ppermute | solution.py:321
  1366.1 82.7 %collective-permute-start.62 = (bf16[192,2560]{1,0:T(8,128)(2,1)S(1)}, bf16[192,2560]{1,0:T(8,128)(2,1)S(1)}, u32[]{:S(2)}, u32[]{:S(2)}) collective-permute-start(bf16[192,2560]{1,0:T(8,128)(2,1)S(1)} %fusion.119.uo_ref), channel_id=1, source_target_pairs={{0,4},{4,0},{1,5},{5,1},{2,6},{6,2},{3,7},{7,3}} | collective-permute-start | bytes 2949128 | tf_op jit(solution)/shard_map/ppermute | solution.py:253
  1435.7 90.0 %collective-permute-start.65 = (bf16[192,2560]{1,0:T(8,128)(2,1)}, bf16[192,2560]{1,0:T(8,128)(2,1)}, u32[]{:S(2)}, u32[]{:S(2)}) collective-permute-start(bf16[192,2560]{1,0:T(8,128)(2,1)} %fusion.247), channel_id=1, source_target_pairs={{3,0},{7,4}} | collective-permute-start | bytes 2949128 | tf_op jit(solution)/shard_map/ppermute | solution.py:320
  1445.2 82.8 %collective-permute-start.66 = (bf16[192,2560]{1,0:T(8,128)(2,1)}, bf16[192,2560]{1,0:T(8,128)(2,1)}, u32[]{:S(2)}, u32[]{:S(2)}) collective-permute-start(bf16[192,2560]{1,0:T(8,128)(2,1)} %fusion.247), channel_id=1, source_target_pairs={{3,4},{7,0}} | collective-permute-start | bytes 2949128 | tf_op jit(solution)/shard_map/ppermute | solution.py:321
  1447.6 80.9 %collective-permute-start.67 = (bf16[192,2560]{1,0:T(8,128)(2,1)S(1)}, bf16[192,2560]{1,0:T(8,128)(2,1)S(1)}, u32[]{:S(2)}, u32[]{:S(2)}) collective-permute-start(bf16[192,2560]{1,0:T(8,128)(2,1)S(1)} %fusion.125.uo_ref), channel_id=1, source_target_pairs={{0,4},{4,0},{1,5},{5,1},{2,6},{6,2},{3,7},{7,3}} | collective-permute-start | bytes 2949128 | tf_op jit(solution)/shard_map/ppermute | solution.py:253
  1521.9 93.2 %collective-permute-start.71 = (bf16[192,2560]{1,0:T(8,128)(2,1)}, bf16[192,2560]{1,0:T(8,128)(2,1)}, u32[]{:S(2)}, u32[]{:S(2)}) collective-permute-start(bf16[192,2560]{1,0:T(8,128)(2,1)} %fusion.245), channel_id=1, source_target_pairs={{3,1},{7,5}} | collective-permute-start | bytes 2949128 | tf_op jit(solution)/shard_map/ppermute | solution.py:320
  1525.7 89.3 %collective-permute-start.72 = (bf16[192,2560]{1,0:T(8,128)(2,1)}, bf16[192,2560]{1,0:T(8,128)(2,1)}, u32[]{:S(2)}, u32[]{:S(2)}) collective-permute-start(bf16[192,2560]{1,0:T(8,128)(2,1)} %fusion.245), channel_id=1, source_target_pairs={{3,5},{7,1}} | collective-permute-start | bytes 2949128 | tf_op jit(solution)/shard_map/ppermute | solution.py:321
  1528.0 87.1 %collective-permute-start.73 = (bf16[192,2560]{1,0:T(8,128)(2,1)S(1)}, bf16[192,2560]{1,0:T(8,128)(2,1)S(1)}, u32[]{:S(2)}, u32[]{:S(2)}) collective-permute-start(bf16[192,2560]{1,0:T(8,128)(2,1)S(1)} %fusion.134.uo_ref), channel_id=1, source_target_pairs={{0,4},{4,0},{1,5},{5,1},{2,6},{6,2},{3,7},{7,3}} | collective-permute-start | bytes 2949128 | tf_op jit(solution)/shard_map/ppermute | solution.py:253
  1655.0 71.1 %collective-permute-start.78 = (bf16[192,2560]{1,0:T(8,128)(2,1)}, bf16[192,2560]{1,0:T(8,128)(2,1)S(1)}, u32[]{:S(2)}, u32[]{:S(2)}) collective-permute-start(bf16[192,2560]{1,0:T(8,128)(2,1)} %fusion.146.uo_ref), channel_id=1, source_target_pairs={{1,5},{5,1},{2,6},{6,2},{3,7},{7,3}} | collective-permute-start | bytes 2949128 | tf_op jit(solution)/shard_map/ppermute | solution.py:253
  1658.9 61.6 %collective-permute-start.76 = (bf16[192,2560]{1,0:T(8,128)(2,1)}, bf16[192,2560]{1,0:T(8,128)(2,1)S(1)}, u32[]{:S(2)}, u32[]{:S(2)}) collective-permute-start(bf16[192,2560]{1,0:T(8,128)(2,1)} %fusion.244), channel_id=1, source_target_pairs={{3,1},{7,5}} | collective-permute-start | bytes 2949128 | tf_op jit(solution)/shard_map/ppermute | solution.py:320
  1680.6 84.8 %collective-permute-start.75 = (bf16[192,2560]{1,0:T(8,128)(2,1)}, bf16[192,2560]{1,0:T(8,128)(2,1)S(1)}, u32[]{:S(2)}, u32[]{:S(2)}) collective-permute-start(bf16[192,2560]{1,0:T(8,128)(2,1)} %fusion.241), channel_id=1, source_target_pairs={{0,1},{1,2},{2,3},{4,5},{5,6},{6,7}} | collective-permute-start | bytes 2949128 | tf_op jit(solution)/shard_map/ppermute | solution.py:311
  1688.8 108.0 %collective-permute-start.80 = (bf16[192,2560]{1,0:T(8,128)(2,1)}, bf16[192,2560]{1,0:T(8,128)(2,1)}, u32[]{:S(2)}, u32[]{:S(2)}) collective-permute-start(bf16[192,2560]{1,0:T(8,128)(2,1)} %fusion.241), channel_id=1, source_target_pairs={{3,1},{7,5}} | collective-permute-start | bytes 2949128 | tf_op jit(solution)/shard_map/ppermute | solution.py:320
  1720.6 76.3 %collective-permute-start.81 = (bf16[192,2560]{1,0:T(8,128)(2,1)}, bf16[192,2560]{1,0:T(8,128)(2,1)}, u32[]{:S(2)}, u32[]{:S(2)}) collective-permute-start(bf16[192,2560]{1,0:T(8,128)(2,1)} %fusion.241), channel_id=1, source_target_pairs={{3,5},{7,1}} | collective-permute-start | bytes 2949128 | tf_op jit(solution)/shard_map/ppermute | solution.py:321
  1723.5 73.4 %collective-permute-start.82 = (bf16[192,2560]{1,0:T(8,128)(2,1)S(1)}, bf16[192,2560]{1,0:T(8,128)(2,1)S(1)}, u32[]{:S(2)}, u32[]{:S(2)}) collective-permute-start(bf16[192,2560]{1,0:T(8,128)(2,1)S(1)} %fusion.152.uo_ref), channel_id=1, source_target_pairs={{1,5},{5,1},{2,6},{6,2},{3,7},{7,3}} | collective-permute-start | bytes 2949128 | tf_op jit(solution)/shard_map/ppermute | solution.py:253
  1840.0 62.4 %collective-permute-start.86 = (bf16[192,2560]{1,0:T(8,128)(2,1)}, bf16[192,2560]{1,0:T(8,128)(2,1)S(1)}, u32[]{:S(2)}, u32[]{:S(2)}) collective-permute-start(bf16[192,2560]{1,0:T(8,128)(2,1)} %fusion.239), channel_id=1, source_target_pairs={{3,1},{7,5}} | collective-permute-start | bytes 2949128 | tf_op jit(solution)/shard_map/ppermute | solution.py:320
  1864.9 82.8 %collective-permute-start.84 = (bf16[192,2560]{1,0:T(8,128)(2,1)}, bf16[192,2560]{1,0:T(8,128)(2,1)S(1)}, u32[]{:S(2)}, u32[]{:S(2)}) collective-permute-start(bf16[192,2560]{1,0:T(8,128)(2,1)} %fusion.238), channel_id=1, source_target_pairs={{1,2},{2,3},{5,6},{6,7}} | collective-permute-start | bytes 2949128 | tf_op jit(solution)/shard_map/ppermute | solution.py:311
  1866.2 113.8 %collective-permute-start.91 = (bf16[192,2560]{1,0:T(8,128)(2,1)}, bf16[192,2560]{1,0:T(8,128)(2,1)}, u32[]{:S(2)}, u32[]{:S(2)}) collective-permute-start(bf16[192,2560]{1,0:T(8,128)(2,1)} %fusion.238), channel_id=1, source_target_pairs={{3,2},{7,6}} | collective-permute-start | bytes 2949128 | tf_op jit(solution)/shard_map/ppermute | solution.py:320
  1902.3 77.7 %collective-permute-start.92 = (bf16[192,2560]{1,0:T(8,128)(2,1)}, bf16[192,2560]{1,0:T(8,128)(2,1)}, u32[]{:S(2)}, u32[]{:S(2)}) collective-permute-start(bf16[192,2560]{1,0:T(8,128)(2,1)} %fusion.238), channel_id=1, source_target_pairs={{3,6},{7,2}} | collective-permute-start | bytes 2949128 | tf_op jit(solution)/shard_map/ppermute | solution.py:321
  1905.7 74.3 %collective-permute-start.93 = (bf16[192,2560]{1,0:T(8,128)(2,1)S(1)}, bf16[192,2560]{1,0:T(8,128)(2,1)S(1)}, u32[]{:S(2)}, u32[]{:S(2)}) collective-permute-start(bf16[192,2560]{1,0:T(8,128)(2,1)S(1)} %fusion.173.uo_ref), channel_id=1, source_target_pairs={{2,6},{6,2},{3,7},{7,3}} | collective-permute-start | bytes 2949128 | tf_op jit(solution)/shard_map/ppermute | solution.py:253
  2022.8 61.2 %collective-permute-start.95 = (bf16[192,2560]{1,0:T(8,128)(2,1)}, bf16[192,2560]{1,0:T(8,128)(2,1)S(1)}, u32[]{:S(2)}, u32[]{:S(2)}) collective-permute-start(bf16[192,2560]{1,0:T(8,128)(2,1)} %fusion.235), channel_id=1, source_target_pairs={{3,2},{7,6}} | collective-permute-start | bytes 2949128 | tf_op jit(solution)/shard_map/ppermute | solution.py:320
  2027.0 61.3 %collective-permute-start.96 = (bf16[192,2560]{1,0:T(8,128)(2,1)}, bf16[192,2560]{1,0:T(8,128)(2,1)}, u32[]{:S(2)}, u32[]{:S(2)}) collective-permute-start(bf16[192,2560]{1,0:T(8,128)(2,1)} %fusion.235), channel_id=1, source_target_pairs={{3,6},{7,2}} | collective-permute-start | bytes 2949128 | tf_op jit(solution)/shard_map/ppermute | solution.py:321
  2029.4 61.9 %collective-permute-start.97 = (bf16[192,2560]{1,0:T(8,128)(2,1)}, bf16[192,2560]{1,0:T(8,128)(2,1)S(1)}, u32[]{:S(2)}, u32[]{:S(2)}) collective-permute-start(bf16[192,2560]{1,0:T(8,128)(2,1)} %fusion.179.uo_ref), channel_id=1, source_target_pairs={{2,6},{6,2},{3,7},{7,3}} | collective-permute-start | bytes 2949128 | tf_op jit(solution)/shard_map/ppermute | solution.py:253
  2049.1 82.0 %collective-permute-start.100 = (bf16[192,2560]{1,0:T(8,128)(2,1)}, bf16[192,2560]{1,0:T(8,128)(2,1)S(1)}, u32[]{:S(2)}, u32[]{:S(2)}) collective-permute-start(bf16[192,2560]{1,0:T(8,128)(2,1)} %fusion.233), channel_id=1, source_target_pairs={{2,3},{6,7}} | collective-permute-start | bytes 2949128 | tf_op jit(solution)/shard_map/ppermute | solution.py:311
  2050.4 112.1 %collective-permute-start.101 = (bf16[192,2560]{1,0:T(8,128)(2,1)}, bf16[192,2560]{1,0:T(8,128)(2,1)}, u32[]{:S(2)}, u32[]{:S(2)}) collective-permute-start(bf16[192,2560]{1,0:T(8,128)(2,1)} %fusion.233), channel_id=1, source_target_pairs={{3,2},{7,6}} | collective-permute-start | bytes 2949128 | tf_op jit(solution)/shard_map/ppermute | solution.py:320
  2084.0 78.4 %collective-permute-start.102 = (bf16[192,2560]{1,0:T(8,128)(2,1)}, bf16[192,2560]{1,0:T(8,128)(2,1)}, u32[]{:S(2)}, u32[]{:S(2)}) collective-permute-start(bf16[192,2560]{1,0:T(8,128)(2,1)} %fusion.233), channel_id=1, source_target_pairs={{3,6},{7,2}} | collective-permute-start | bytes 2949128 | tf_op jit(solution)/shard_map/ppermute | solution.py:321
  2088.2 74.2 %collective-permute-start.103 = (bf16[192,2560]{1,0:T(8,128)(2,1)S(1)}, bf16[192,2560]{1,0:T(8,128)(2,1)S(1)}, u32[]{:S(2)}, u32[]{:S(2)}) collective-permute-start(bf16[192,2560]{1,0:T(8,128)(2,1)S(1)} %fusion.188.uo_ref), channel_id=1, source_target_pairs={{2,6},{6,2},{3,7},{7,3}} | collective-permute-start | bytes 2949128 | tf_op jit(solution)/shard_map/ppermute | solution.py:253
  2228.8 75.0 %collective-permute-start.105 = (bf16[192,2560]{1,0:T(8,128)(2,1)}, bf16[192,2560]{1,0:T(8,128)(2,1)S(1)}, u32[]{:S(2)}, u32[]{:S(2)}) collective-permute-start(bf16[192,2560]{1,0:T(8,128)(2,1)} %get-tuple-element.663), channel_id=1, source_target_pairs={{2,3},{6,7}} | collective-permute-start | bytes 2949128 | tf_op jit(solution)/shard_map/ppermute | solution.py:311
  2230.1 107.8 %collective-permute-start.110 = (bf16[192,2560]{1,0:T(8,128)(2,1)}, bf16[192,2560]{1,0:T(8,128)(2,1)}, u32[]{:S(2)}, u32[]{:S(2)}) collective-permute-start(bf16[192,2560]{1,0:T(8,128)(2,1)} %get-tuple-element.663), channel_id=1, source_target_pairs={{3,7},{7,3}} | collective-permute-start | bytes 2949128 | tf_op jit(solution)/shard_map/ppermute | solution.py:321
  2260.9 77.0 %collective-permute-start.111 = (bf16[192,2560]{1,0:T(8,128)(2,1)S(1)}, bf16[192,2560]{1,0:T(8,128)(2,1)S(1)}, u32[]{:S(2)}, u32[]{:S(2)}) collective-permute-start(bf16[192,2560]{1,0:T(8,128)(2,1)S(1)} %fusion.206.uo_ref), channel_id=1, source_target_pairs={{3,7},{7,3}} | collective-permute-start | bytes 2949128 | tf_op jit(solution)/shard_map/ppermute | solution.py:253
  2331.4 64.1 %collective-permute-start.115 = (bf16[192,2560]{1,0:T(8,128)(2,1)S(1)}, bf16[192,2560]{1,0:T(8,128)(2,1)S(1)}, u32[]{:S(2)}, u32[]{:S(2)}) collective-permute-start(bf16[192,2560]{1,0:T(8,128)(2,1)S(1)} %fusion.215.uo_ref), channel_id=1, source_target_pairs={{3,7},{7,3}} | collective-permute-start | bytes 2949128 | tf_op jit(solution)/shard_map/ppermute | solution.py:253
  2335.7 59.9 %collective-permute-start.114 = (bf16[192,2560]{1,0:T(8,128)(2,1)S(1)}, bf16[192,2560]{1,0:T(8,128)(2,1)S(1)}, u32[]{:S(2)}, u32[]{:S(2)}) collective-permute-start(bf16[192,2560]{1,0:T(8,128)(2,1)S(1)} %get-tuple-element.661), channel_id=1, source_target_pairs={{3,7},{7,3}} | collective-permute-start | bytes 2949128 | tf_op jit(solution)/shard_map/ppermute | solution.py:321
  2392.5 59.8 %collective-permute-start.113 = (bf16[192,2560]{1,0:T(8,128)(2,1)S(1)}, bf16[192,2560]{1,0:T(8,128)(2,1)S(1)}, u32[]{:S(2)}, u32[]{:S(2)}) collective-permute-start(bf16[192,2560]{1,0:T(8,128)(2,1)S(1)} %get-tuple-element.657), channel_id=1, source_target_pairs={{3,7},{7,3}} | collective-permute-start | bytes 2949128 | tf_op jit(solution)/shard_map/ppermute | solution.py:321
  (220 other events, 3349.2 us)

commit v3 on v2

--- a/solution.py
+++ b/solution.py
@@ -35,15 +35,36 @@
     return jnp.cos(angles), jnp.sin(angles)
 
 
-def attn_kernel(meta, x_ref, w_ref, wo_ref, kc_ref, vc_ref, cos_ref, sin_ref, gain0_ref, gain_ref, o_ref, ko_ref, vo_ref, h_ref, acc, *, n_group, q_scale):
+def attn_kernel(meta, x_ref, w_ref, wo_ref, kc_ref, vc_ref, cos_ref, sin_ref, gain0_ref, gain_ref, o_ref, ko_ref, vo_ref, h_ref, acc, w_buf, wo_buf, sems, *, n_group, q_scale):
     head = pl.program_id(0)
+    kv_heads = w_buf.shape[0]
+    cols = w_buf.shape[2]
+    o_rows = wo_buf.shape[1]
+    cut = cols // 2
+
+    def fetches(h):
+        base = h * cols
+        if not isinstance(h, int):
+            base = pl.multiple_of(base, 128)
+        return (
+            pltpu.make_async_copy(w_ref.at[:, pl.ds(base, cut)], w_buf.at[h, :, pl.ds(0, cut)], sems.at[h, 0]),
+            pltpu.make_async_copy(w_ref.at[:, pl.ds(base + cut, cut)], w_buf.at[h, :, pl.ds(cut, cut)], sems.at[h, 1]),
+            pltpu.make_async_copy(wo_ref.at[pl.ds(h * o_rows, o_rows), :], wo_buf.at[h], sems.at[h, 2]),
+        )
+
+    @pl.when(head == 0)
+    def _():
+        for h in range(kv_heads):
+            for copy in fetches(h):
+                copy.start()
+
+    get_lo, get_hi, get_o = fetches(head)
     chunk = meta[1]
     is_glob = meta[2] == 1
     head_dim = ko_ref.shape[-1]
     half = head_dim // 2
     rows = x_ref.shape[0]
     n_rows = n_group * rows
-    q_cols = n_group * head_dim
     cos_b = cos_ref[...]
     sin_b = sin_ref[...]
 
@@ -62,12 +83,16 @@
         hi = x[:, half:]
         return jnp.concatenate([lo * cos_b - hi * sin_b, hi * cos_b + lo * sin_b], axis=-1).astype(jnp.bfloat16)
 
-    qkv = jnp.dot(h_ref[...], w_ref[...], preferred_element_type=jnp.float32)
-    k_new = norm_rope(qkv[:, q_cols:q_cols + head_dim], gain_ref[1:2, :])
-    v_new = qkv[:, q_cols + head_dim:].astype(jnp.bfloat16)
+    get_lo.wait()
+    kv_part = jnp.dot(h_ref[...], w_buf[head, :, :cut], preferred_element_type=jnp.float32)
+    k_new = norm_rope(kv_part[:, :head_dim], gain_ref[1:2, :])
+    v_new = kv_part[:, head_dim:].astype(jnp.bfloat16)
     ko_ref[0, 0] = k_new
     vo_ref[0, 0] = v_new
-    q_all = jnp.concatenate([norm_rope(qkv[:, g * head_dim:(g + 1) * head_dim], gain_ref[0:1, :]) for g in range(n_group)], axis=0)
+    get_hi.wait()
+    q_part = jnp.dot(h_ref[...], w_buf[head, :, cut:], preferred_element_type=jnp.float32)
+    get_o.wait()
+    q_all = jnp.concatenate([norm_rope(q_part[:, g * head_dim:(g + 1) * head_dim], gain_ref[0:1, :]) for g in range(n_group)], axis=0)
     start = chunk * rows
     span = jnp.where(is_glob, kc_ref.shape[2], WINDOW)
     first = jnp.where(is_glob, 0, jnp.maximum(start - WINDOW, 0))
@@ -84,7 +109,7 @@
     def emit(res):
         res = res.astype(jnp.bfloat16)
         att = jnp.concatenate([res[g * rows:(g + 1) * rows] for g in range(n_group)], axis=1)
-        acc[...] += jnp.dot(att, wo_ref[...], preferred_element_type=jnp.float32)
+        acc[...] += jnp.dot(att, wo_buf[head], preferred_element_type=jnp.float32)
 
     @pl.when(n_old == 0)
     def _():
@@ -130,8 +155,8 @@
         grid=(kv_heads,),
         in_specs=[
             pl.BlockSpec((rows, d_model), lambda h, m: (0, 0)),
-            pl.BlockSpec((d_model, cols), lambda h, m: (0, h)),
-            pl.BlockSpec((n_group * head_dim, d_model), lambda h, m: (h, 0)),
+            pl.BlockSpec(memory_space=pl.ANY),
+            pl.BlockSpec(memory_space=pl.ANY),
             cache_in,
             cache_in,
             table,
@@ -140,7 +165,13 @@
             pl.BlockSpec((2, head_dim), lambda h, m: (0, 0)),
         ],
         out_specs=[pl.BlockSpec((rows, d_model), lambda h, m: (0, 0)), cache_out, cache_out],
-        scratch_shapes=[pltpu.VMEM((rows, d_model), jnp.bfloat16), pltpu.VMEM((rows, d_model), jnp.float32)],
+        scratch_shapes=[
+            pltpu.VMEM((rows, d_model), jnp.bfloat16),
+            pltpu.VMEM((rows, d_model), jnp.float32),
+            pltpu.VMEM((kv_heads, d_model, cols), jnp.bfloat16),
+            pltpu.VMEM((kv_heads, n_group * head_dim, d_model), jnp.bfloat16),
+            pltpu.SemaphoreType.DMA((kv_heads, 3)),
+        ],
     )
     flops = 2 * rows * d_model * (w_qkv.shape[1] + w_o.shape[0]) + 4 * rows * w_o.shape[0] * 900
     return pl.pallas_call(
@@ -256,13 +287,11 @@
             groups = []
             for g in range(kv_heads):
                 at_kv = slice(g * head_dim, (g + 1) * head_dim)
-                groups += [wq_loc[0, 0][:, g * n_group * head_dim:(g + 1) * n_group * head_dim], wk_loc[0, 0][:, at_kv], wv_loc[0, 0][:, at_kv]]
+                groups += [wk_loc[0, 0][:, at_kv], wv_loc[0, 0][:, at_kv], wq_loc[0, 0][:, g * n_group * head_dim:(g + 1) * n_group * head_dim]]
             wqkv_own = jnp.concatenate(groups, axis=1)
             wo_own = wo_loc[0, 0]
-            later = range(1, n_stages)
-            wqkv_oth = jnp.where(at_first, wqkv_own, swap(wqkv_own, later))
-            wo_oth = jnp.where(at_first, wo_own, swap(wo_own, later))
-            fill = LAG - 1
+            two = [(wqkv_own, wo_own)]
+            got = [(swap(wqkv_own, [s]), swap(wo_own, [s])) for s in range(1, n_stages)]
             cos_tab, sin_tab = rope_tables(kind_val, seq_len, head_dim)
             caches = [jnp.zeros((n_own, kv_heads, seq_len, head_dim), jnp.bfloat16) for _ in range(4)]
 
@@ -292,7 +321,11 @@
                             x_own, x_two, _ = lax.optimization_barrier((x_own, x_two, d_own[slot - 2]))
                     else:
                         x_own = x_two = lax.optimization_barrier((x_recv[slot], d_own[slot - 2]))[0]
-                    wqkv_two, wo_two = (wqkv_oth, wo_oth) if slot > fill else (wqkv_own, wo_own)
+                    if slot % LAG == 0 and 0 < slot <= LAG * last_stage:
+                        new_qkv, new_o = lax.optimization_barrier((*got[slot // LAG - 1], x_two))[:2]
+                        here = stage == slot // LAG
+                        two.append((jnp.where(here, new_qkv, two[-1][0]), jnp.where(here, new_o, two[-1][1])))
+                    wqkv_two, wo_two = two[-1]
                     o_b, caches[2], caches[3] = attend(meta, x_two, wqkv_two, wo_two, caches[2], caches[3], cos_tab, sin_tab, gains[:1], qk_gain, q_scale)
                     if slot < n_units:
                         o_b = jnp.where(at_first, swap(o_b.astype(jnp.bfloat16), [0]).astype(f32), o_b)
@@ -304,7 +337,10 @@
                 x_out = None
                 if 0 <= slot - 2 < n_slots:
                     done = slot - 2
-                    d_sum = (d_own[done] + d_oth[done].astype(f32)).astype(jnp.bfloat16)
+                    d_mine = d_own[done]
+                    if slot < n_slots:
+                        d_mine = lax.optimization_barrier((d_mine, o_sum))[0]
+                    d_sum = (d_mine + d_oth[done].astype(f32)).astype(jnp.bfloat16)
                     x_out = x_mid[done] + rms_norm(d_sum, gains[3])
                     movers = [s for s in active(done) if s < last_stage]
                     if movers:

time: 2480 us -> 2440 us (0.984)
  waiting for transfers between devices: 322 us -> 145 us
  starting transfers between devices: 338 us -> 440 us
  Pallas kernels: 1540 us -> 1490 us
  local copies, waits for them, and re-layouts: 68.6 us -> 104 us
  other arithmetic: 203 us -> 237 us
    ppermute x68 -> x72, waiting for transfers between devices: 306 us -> 26.4 us  [swap(): return lax.ppermute(x, axes, pairs)]
    ppermute x12, starting transfers between devices: 127 us -> 240 us  [device_fn(): lax.ppermute(x_out, axes, [(dev(t, last_stage), dev(t, target)) for t in...]
    ppermute x22, waiting for transfers between devices: 6.75 us -> 109 us  [device_fn(): x_recv[done + LAG] = lax.ppermute(x_out, 'pp', [(s, s + 1) for s in movers])]
    pallas_call x50, Pallas kernels: 612 us -> 575 us  [attend(): pl.pallas_call(functools.partial(attn_kernel, n_group=n_group, q_scale=q_...]
    unnamed x305 -> x393, local copies, waits for them, and re-layouts: 58.3 us -> 92.9 us
    ppermute x68 -> x72, starting transfers between devices: 134 us -> 137 us  [swap(): return lax.ppermute(x, axes, pairs)]
  transfers between devices with their start and end apart: 118 -> 122, of which waited for: 13 -> 9; matrix products, arithmetic and copies ran while one was open for 7% -> 6% of each run, Pallas kernels for 50% -> 56%
where the time goes in v3:
time: 2440 us; the launch traced here: 2430 us
  Pallas kernels  1490 us (61%)
  starting transfers between devices  440 us (18%)
  other arithmetic  237 us (10%)
  waiting for transfers between devices  145 us (6%)
  local copies, waits for them, and re-layouts  104 us (4%)
    pallas_call x25, Pallas kernels, mlp(): pl.pallas_call(mlp_kernel, grid=(n_tiles + 1,), in_specs=[whole, whole, c...  920 us
    pallas_call x50, Pallas kernels, attend(): pl.pallas_call(functools.partial(attn_kernel, n_group=n_group, q_scale=q_...  575 us
    ppermute x12, starting transfers between devices, device_fn(): lax.ppermute(x_out, axes, [(dev(t, last_stage), dev(t, target)) for t in...  240 us
    ppermute x72, starting transfers between devices, swap(): return lax.ppermute(x, axes, pairs)  137 us
    ppermute x22, waiting for transfers between devices, device_fn(): x_recv[done + LAG] = lax.ppermute(x_out, 'pp', [(s, s + 1) for s in movers])  109 us
    unnamed x393, local copies, waits for them, and re-layouts  92.9 us
    reduce_sum x74, other arithmetic, rms_norm(): mean_sq = jnp.mean(x_f32 * x_f32, axis=-1, keepdims=True)  65.6 us
  transfers between devices with their start and end apart: 122, of which 9 were waited for; matrix products, arithmetic and copies ran while one was open for 6% of the time, Pallas kernels for 56%

profile of v3, /device:TPU:3, one launch (start us, length us, event | category | flops | bytes accessed | tf_op | source)
XLA Modules:
  0.0 2425.8 jit_solution(9778510132307860948)
XLA Ops:
  92.2 38.0 %mlp.25 = (f32[192,2560]{1,0:T(8,128)S(1)}, bf16[192,2560]{1,0:T(8,128)(2,1)S(1)}) custom-call(bf16[192,2560]{1,0:T(8,128)(2,1)} %get-tuple-element.366.uo_ref, bf16[192,2560]{1,0:T(8,128)(2,1)} %collective-permute-done.2.ux_ref, bf16[2560,5120]{1,0:T(8,128)(2,1)} %bitcast.221, bf16[2560,5120]{1,0:T(8,128)(2,1)} %bitcast.246, bf16[5120,2560]{1,0:T(8,128)(2,1)} %bitcast.271), custom_call_target="tpu_custom_call" | custom-call | flops 30198988800 | bytes 78643200 | tf_op jit(solution)/shard_map/mlp/pallas_call | solution.py:231
  173.0 37.6 %mlp.26 = (f32[192,2560]{1,0:T(8,128)S(1)}, bf16[192,2560]{1,0:T(8,128)(2,1)}) custom-call(bf16[192,2560]{1,0:T(8,128)(2,1)S(1)} %copy-done.121, bf16[192,2560]{1,0:T(8,128)(2,1)S(1)} %collective-permute-done.6.ux_ref, bf16[2560,5120]{1,0:T(8,128)(2,1)} %bitcast.222, bf16[2560,5120]{1,0:T(8,128)(2,1)} %bitcast.247, bf16[5120,2560]{1,0:T(8,128)(2,1)} %bitcast.272), custom_call_target="tpu_custom_call" | custom-call | flops 30198988800 | bytes 78643200 | tf_op jit(solution)/shard_map/mlp/pallas_call | solution.py:231
  269.5 36.6 %mlp.27 = (f32[192,2560]{1,0:T(8,128)S(1)}, bf16[192,2560]{1,0:T(8,128)(2,1)S(1)}) custom-call(bf16[192,2560]{1,0:T(8,128)(2,1)S(1)} %copy-done.114, bf16[192,2560]{1,0:T(8,128)(2,1)S(1)} %collective-permute-done.11.ux_ref, bf16[2560,5120]{1,0:T(8,128)(2,1)} %bitcast.223, bf16[2560,5120]{1,0:T(8,128)(2,1)} %bitcast.248, bf16[5120,2560]{1,0:T(8,128)(2,1)} %bitcast.273), custom_call_target="tpu_custom_call" | custom-call | flops 30198988800 | bytes 78643200 | tf_op jit(solution)/shard_map/mlp/pallas_call | solution.py:231
  343.8 36.6 %mlp.28 = (f32[192,2560]{1,0:T(8,128)S(1)}, bf16[192,2560]{1,0:T(8,128)(2,1)S(1)}) custom-call(bf16[192,2560]{1,0:T(8,128)(2,1)S(1)} %fusion.26.uo_ref, bf16[192,2560]{1,0:T(8,128)(2,1)S(1)} %collective-permute-done.16.ux_ref, bf16[2560,5120]{1,0:T(8,128)(2,1)} %bitcast.224, bf16[2560,5120]{1,0:T(8,128)(2,1)} %bitcast.249, bf16[5120,2560]{1,0:T(8,128)(2,1)} %bitcast.274), custom_call_target="tpu_custom_call" | custom-call | flops 30198988800 | bytes 78643200 | tf_op jit(solution)/shard_map/mlp/pallas_call | solution.py:231
  424.2 37.0 %mlp.29 = (f32[192,2560]{1,0:T(8,128)S(1)}, bf16[192,2560]{1,0:T(8,128)(2,1)S(1)}) custom-call(bf16[192,2560]{1,0:T(8,128)(2,1)S(1)} %copy-done.117, bf16[192,2560]{1,0:T(8,128)(2,1)S(1)} %collective-permute-done.20.ux_ref, bf16[2560,5120]{1,0:T(8,128)(2,1)} %bitcast.225, bf16[2560,5120]{1,0:T(8,128)(2,1)} %bitcast.250, bf16[5120,2560]{1,0:T(8,128)(2,1)} %bitcast.275), custom_call_target="tpu_custom_call" | custom-call | flops 30198988800 | bytes 78643200 | tf_op jit(solution)/shard_map/mlp/pallas_call | solution.py:231
  504.4 36.6 %mlp.30 = (f32[192,2560]{1,0:T(8,128)S(1)}, bf16[192,2560]{1,0:T(8,128)(2,1)S(1)}) custom-call(bf16[192,2560]{1,0:T(8,128)(2,1)S(1)} %fusion.44.uo_ref, bf16[192,2560]{1,0:T(8,128)(2,1)S(1)} %collective-permute-done.25.ux_ref, bf16[2560,5120]{1,0:T(8,128)(2,1)} %bitcast.226, bf16[2560,5120]{1,0:T(8,128)(2,1)} %bitcast.251, bf16[5120,2560]{1,0:T(8,128)(2,1)} %bitcast.276), custom_call_target="tpu_custom_call" | custom-call | flops 30198988800 | bytes 78643200 | tf_op jit(solution)/shard_map/mlp/pallas_call | solution.py:231
  585.6 36.6 %mlp.31 = (f32[192,2560]{1,0:T(8,128)S(1)}, bf16[192,2560]{1,0:T(8,128)(2,1)S(1)}) custom-call(bf16[192,2560]{1,0:T(8,128)(2,1)S(1)} %copy-done.118, bf16[192,2560]{1,0:T(8,128)(2,1)S(1)} %collective-permute-done.30.ux_ref, bf16[2560,5120]{1,0:T(8,128)(2,1)} %bitcast.227, bf16[2560,5120]{1,0:T(8,128)(2,1)} %bitcast.252, bf16[5120,2560]{1,0:T(8,128)(2,1)} %bitcast.277), custom_call_target="tpu_custom_call" | custom-call | flops 30198988800 | bytes 78643200 | tf_op jit(solution)/shard_map/mlp/pallas_call | solution.py:231
  667.6 37.6 %mlp.32 = (f32[192,2560]{1,0:T(8,128)S(1)}, bf16[192,2560]{1,0:T(8,128)(2,1)}) custom-call(bf16[192,2560]{1,0:T(8,128)(2,1)S(1)} %copy-done.120, bf16[192,2560]{1,0:T(8,128)(2,1)S(1)} %collective-permute-done.34.ux_ref, bf16[2560,5120]{1,0:T(8,128)(2,1)} %bitcast.228, bf16[2560,5120]{1,0:T(8,128)(2,1)} %bitcast.253, bf16[5120,2560]{1,0:T(8,128)(2,1)} %bitcast.278), custom_call_target="tpu_custom_call" | custom-call | flops 30198988800 | bytes 78643200 | tf_op jit(solution)/shard_map/mlp/pallas_call | solution.py:231
  705.2 76.0 %collective-permute-done.33 = bf16[192,2560]{1,0:T(8,128)(2,1)S(1)} collective-permute-done((bf16[192,2560]{1,0:T(8,128)(2,1)S(1)}, bf16[192,2560]{1,0:T(8,128)(2,1)S(1)}, u32[]{:S(2)}, u32[]{:S(2)}) %collective-permute-start.33) | collective-permute-done | bytes 983072 | tf_op jit(solution)/shard_map/ppermute | solution.py:347
  840.1 36.6 %mlp.33 = (f32[192,2560]{1,0:T(8,128)S(1)}, bf16[192,2560]{1,0:T(8,128)(2,1)S(1)}) custom-call(bf16[192,2560]{1,0:T(8,128)(2,1)S(1)} %copy-done.115, bf16[192,2560]{1,0:T(8,128)(2,1)S(1)} %collective-permute-done.39.ux_ref, bf16[2560,5120]{1,0:T(8,128)(2,1)} %bitcast.229, bf16[2560,5120]{1,0:T(8,128)(2,1)} %bitcast.254, bf16[5120,2560]{1,0:T(8,128)(2,1)} %bitcast.279), custom_call_target="tpu_custom_call" | custom-call | flops 30198988800 | bytes 78643200 | tf_op jit(solution)/shard_map/mlp/pallas_call | solution.py:231
  917.5 36.6 %mlp.34 = (f32[192,2560]{1,0:T(8,128)S(1)}, bf16[192,2560]{1,0:T(8,128)(2,1)S(1)}) custom-call(bf16[192,2560]{1,0:T(8,128)(2,1)S(1)} %fusion.80.uo_ref, bf16[192,2560]{1,0:T(8,128)(2,1)S(1)} %collective-permute-done.44.ux_ref, bf16[2560,5120]{1,0:T(8,128)(2,1)} %bitcast.230, bf16[2560,5120]{1,0:T(8,128)(2,1)} %bitcast.255, bf16[5120,2560]{1,0:T(8,128)(2,1)} %bitcast.280), custom_call_target="tpu_custom_call" | custom-call | flops 30198988800 | bytes 78643200 | tf_op jit(solution)/shard_map/mlp/pallas_call | solution.py:231
  954.1 16.8 collective-permute-done.43
  995.0 15.0 attend.72
  1016.9 36.6 %mlp.35 = (f32[192,2560]{1,0:T(8,128)S(1)}, bf16[192,2560]{1,0:T(8,128)(2,1)S(1)}) custom-call(bf16[192,2560]{1,0:T(8,128)(2,1)S(1)} %copy-done.119, bf16[192,2560]{1,0:T(8,128)(2,1)S(1)} %collective-permute-done.48.ux_ref, bf16[2560,5120]{1,0:T(8,128)(2,1)} %bitcast.231, bf16[2560,5120]{1,0:T(8,128)(2,1)} %bitcast.256, bf16[5120,2560]{1,0:T(8,128)(2,1)} %bitcast.281), custom_call_target="tpu_custom_call" | custom-call | flops 30198988800 | bytes 78643200 | tf_op jit(solution)/shard_map/mlp/pallas_call | solution.py:231
  1077.0 132.0 %collective-permute-start.51 = (bf16[192,2560]{1,0:T(8,128)(2,1)}, bf16[192,2560]{1,0:T(8,128)(2,1)}, u32[]{:S(2)}, u32[]{:S(2)}) collective-permute-start(bf16[192,2560]{1,0:T(8,128)(2,1)} %fusion.253), channel_id=1, source_target_pairs={{3,0},{7,4}} | collective-permute-start | bytes 2949128 | tf_op jit(solution)/shard_map/ppermute | solution.py:356
  1231.0 36.6 %mlp.36 = (f32[192,2560]{1,0:T(8,128)S(1)}, bf16[192,2560]{1,0:T(8,128)(2,1)S(1)}) custom-call(bf16[192,2560]{1,0:T(8,128)(2,1)S(1)} %fusion.98.uo_ref, bf16[192,2560]{1,0:T(8,128)(2,1)S(1)} %collective-permute-done.53.ux_ref, bf16[2560,5120]{1,0:T(8,128)(2,1)} %bitcast.232, bf16[2560,5120]{1,0:T(8,128)(2,1)} %bitcast.257, bf16[5120,2560]{1,0:T(8,128)(2,1)} %bitcast.282), custom_call_target="tpu_custom_call" | custom-call | flops 30198988800 | bytes 78643200 | tf_op jit(solution)/shard_map/mlp/pallas_call | solution.py:231
  1288.7 24.8 %collective-permute-start.58 = (bf16[192,2560]{1,0:T(8,128)(2,1)}, bf16[192,2560]{1,0:T(8,128)(2,1)S(1)}, u32[]{:S(2)}, u32[]{:S(2)}) collective-permute-start(bf16[192,2560]{1,0:T(8,128)(2,1)} %copy-done.188), channel_id=1, source_target_pairs={{3,0},{7,4}} | collective-permute-start | bytes 2949128 | tf_op jit(solution)/shard_map/ppermute | solution.py:356
  1339.2 36.9 %mlp.37 = (f32[192,2560]{1,0:T(8,128)S(1)}, bf16[192,2560]{1,0:T(8,128)(2,1)S(1)}) custom-call(bf16[192,2560]{1,0:T(8,128)(2,1)S(1)} %copy-done.116, bf16[192,2560]{1,0:T(8,128)(2,1)S(1)} %collective-permute-done.60.ux_ref, bf16[2560,5120]{1,0:T(8,128)(2,1)} %bitcast.233, bf16[2560,5120]{1,0:T(8,128)(2,1)} %bitcast.258, bf16[5120,2560]{1,0:T(8,128)(2,1)} %bitcast.283), custom_call_target="tpu_custom_call" | custom-call | flops 30198988800 | bytes 78643200 | tf_op jit(solution)/shard_map/mlp/pallas_call | solution.py:231
  1391.1 24.0 collective-permute-start.64
  1446.1 36.6 %mlp.38 = (f32[192,2560]{1,0:T(8,128)S(1)}, bf16[192,2560]{1,0:T(8,128)(2,1)S(1)}) custom-call(bf16[192,2560]{1,0:T(8,128)(2,1)S(1)} %fusion.119.uo_ref, bf16[192,2560]{1,0:T(8,128)(2,1)S(1)} %collective-permute-done.66.ux_ref, bf16[2560,5120]{1,0:T(8,128)(2,1)} %bitcast.234, bf16[2560,5120]{1,0:T(8,128)(2,1)} %bitcast.259, bf16[5120,2560]{1,0:T(8,128)(2,1)} %bitcast.284), custom_call_target="tpu_custom_call" | custom-call | flops 30198988800 | bytes 78643200 | tf_op jit(solution)/shard_map/mlp/pallas_call | solution.py:231
  1505.7 19.7 collective-permute-start.69
  1531.7 12.5 attend.80
  1568.3 36.6 %mlp.39 = (f32[192,2560]{1,0:T(8,128)S(1)}, bf16[192,2560]{1,0:T(8,128)(2,1)S(1)}) custom-call(bf16[192,2560]{1,0:T(8,128)(2,1)S(1)} %copy-done.113, bf16[192,2560]{1,0:T(8,128)(2,1)S(1)} %collective-permute-done.71.ux_ref, bf16[2560,5120]{1,0:T(8,128)(2,1)} %bitcast.235, bf16[2560,5120]{1,0:T(8,128)(2,1)} %bitcast.260, bf16[5120,2560]{1,0:T(8,128)(2,1)} %bitcast.285), custom_call_target="tpu_custom_call" | custom-call | flops 30198988800 | bytes 78643200 | tf_op jit(solution)/shard_map/mlp/pallas_call | solution.py:231
  1618.5 12.5 attend.83
  1648.8 36.6 %mlp.40 = (f32[192,2560]{1,0:T(8,128)S(1)}, bf16[192,2560]{1,0:T(8,128)(2,1)S(1)}) custom-call(bf16[192,2560]{1,0:T(8,128)(2,1)S(1)} %fusion.134.uo_ref, bf16[192,2560]{1,0:T(8,128)(2,1)S(1)} %collective-permute-done.77.ux_ref, bf16[2560,5120]{1,0:T(8,128)(2,1)} %bitcast.236, bf16[2560,5120]{1,0:T(8,128)(2,1)} %bitcast.261, bf16[5120,2560]{1,0:T(8,128)(2,1)} %bitcast.286), custom_call_target="tpu_custom_call" | custom-call | flops 30198988800 | bytes 78643200 | tf_op jit(solution)/shard_map/mlp/pallas_call | solution.py:231
  1698.9 12.5 attend.85
  1731.9 36.6 %mlp.41 = (f32[192,2560]{1,0:T(8,128)S(1)}, bf16[192,2560]{1,0:T(8,128)(2,1)S(1)}) custom-call(bf16[192,2560]{1,0:T(8,128)(2,1)S(1)} %fusion.146.uo_ref, bf16[192,2560]{1,0:T(8,128)(2,1)S(1)} %collective-permute-done.82.ux_ref, bf16[2560,5120]{1,0:T(8,128)(2,1)} %bitcast.237, bf16[2560,5120]{1,0:T(8,128)(2,1)} %bitcast.262, bf16[5120,2560]{1,0:T(8,128)(2,1)} %bitcast.287), custom_call_target="tpu_custom_call" | custom-call | flops 30198988800 | bytes 78643200 | tf_op jit(solution)/shard_map/mlp/pallas_call | solution.py:231
  1783.9 12.6 attend.87
  1816.8 36.6 %mlp.42 = (f32[192,2560]{1,0:T(8,128)S(1)}, bf16[192,2560]{1,0:T(8,128)(2,1)S(1)}) custom-call(bf16[192,2560]{1,0:T(8,128)(2,1)S(1)} %fusion.152.uo_ref, bf16[192,2560]{1,0:T(8,128)(2,1)S(1)} %collective-permute-done.86.ux_ref, bf16[2560,5120]{1,0:T(8,128)(2,1)} %bitcast.238, bf16[2560,5120]{1,0:T(8,128)(2,1)} %bitcast.263, bf16[5120,2560]{1,0:T(8,128)(2,1)} %bitcast.288), custom_call_target="tpu_custom_call" | custom-call | flops 30198988800 | bytes 78643200 | tf_op jit(solution)/shard_map/mlp/pallas_call | solution.py:231
  1856.5 12.7 attend.88
  1869.2 13.0 attend.89
  1897.8 36.6 %mlp.43 = (f32[192,2560]{1,0:T(8,128)S(1)}, bf16[192,2560]{1,0:T(8,128)(2,1)S(1)}) custom-call(bf16[192,2560]{1,0:T(8,128)(2,1)S(1)} %fusion.161.uo_ref, bf16[192,2560]{1,0:T(8,128)(2,1)S(1)} %collective-permute-done.92.ux_ref, bf16[2560,5120]{1,0:T(8,128)(2,1)} %bitcast.239, bf16[2560,5120]{1,0:T(8,128)(2,1)} %bitcast.264, bf16[5120,2560]{1,0:T(8,128)(2,1)} %bitcast.289), custom_call_target="tpu_custom_call" | custom-call | flops 30198988800 | bytes 78643200 | tf_op jit(solution)/shard_map/mlp/pallas_call | solution.py:231
  1937.5 12.6 attend.90
  1950.2 13.0 attend.91
  1978.6 36.6 %mlp.44 = (f32[192,2560]{1,0:T(8,128)S(1)}, bf16[192,2560]{1,0:T(8,128)(2,1)S(1)}) custom-call(bf16[192,2560]{1,0:T(8,128)(2,1)S(1)} %fusion.173.uo_ref, bf16[192,2560]{1,0:T(8,128)(2,1)S(1)} %collective-permute-done.97.ux_ref, bf16[2560,5120]{1,0:T(8,128)(2,1)} %bitcast.240, bf16[2560,5120]{1,0:T(8,128)(2,1)} %bitcast.265, bf16[5120,2560]{1,0:T(8,128)(2,1)} %bitcast.290), custom_call_target="tpu_custom_call" | custom-call | flops 30198988800 | bytes 78643200 | tf_op jit(solution)/shard_map/mlp/pallas_call | solution.py:231
  2018.3 12.6 attend.92
  2030.9 13.0 attend.93
  2058.7 36.6 %mlp.45 = (f32[192,2560]{1,0:T(8,128)S(1)}, bf16[192,2560]{1,0:T(8,128)(2,1)S(1)}) custom-call(bf16[192,2560]{1,0:T(8,128)(2,1)S(1)} %fusion.179.uo_ref, bf16[192,2560]{1,0:T(8,128)(2,1)S(1)} %collective-permute-done.101.ux_ref, bf16[2560,5120]{1,0:T(8,128)(2,1)} %bitcast.241, bf16[2560,5120]{1,0:T(8,128)(2,1)} %bitcast.266, bf16[5120,2560]{1,0:T(8,128)(2,1)} %bitcast.291), custom_call_target="tpu_custom_call" | custom-call | flops 30198988800 | bytes 78643200 | tf_op jit(solution)/shard_map/mlp/pallas_call | solution.py:231
  2098.5 12.7 attend.94
  2111.1 13.0 attend.95
  2141.6 36.6 %mlp.46 = (f32[192,2560]{1,0:T(8,128)S(1)}, bf16[192,2560]{1,0:T(8,128)(2,1)S(1)}) custom-call(bf16[192,2560]{1,0:T(8,128)(2,1)S(1)} %fusion.188.uo_ref, bf16[192,2560]{1,0:T(8,128)(2,1)S(1)} %collective-permute-done.107.ux_ref, bf16[2560,5120]{1,0:T(8,128)(2,1)} %bitcast.242, bf16[2560,5120]{1,0:T(8,128)(2,1)} %bitcast.267, bf16[5120,2560]{1,0:T(8,128)(2,1)} %bitcast.292), custom_call_target="tpu_custom_call" | custom-call | flops 30198988800 | bytes 78643200 | tf_op jit(solution)/shard_map/mlp/pallas_call | solution.py:231
  2181.3 12.7 attend.96
  2193.9 13.0 attend.97
  2217.7 36.6 %mlp.47 = (f32[192,2560]{1,0:T(8,128)S(1)}, bf16[192,2560]{1,0:T(8,128)(2,1)S(1)}) custom-call(bf16[192,2560]{1,0:T(8,128)(2,1)S(1)} %fusion.200.uo_ref, bf16[192,2560]{1,0:T(8,128)(2,1)S(1)} %collective-permute-done.112.ux_ref, bf16[2560,5120]{1,0:T(8,128)(2,1)} %bitcast.243, bf16[2560,5120]{1,0:T(8,128)(2,1)} %bitcast.268, bf16[5120,2560]{1,0:T(8,128)(2,1)} %bitcast.293), custom_call_target="tpu_custom_call" | custom-call | flops 30198988800 | bytes 78643200 | tf_op jit(solution)/shard_map/mlp/pallas_call | solution.py:231
  2256.6 12.7 attend.98
  2269.3 13.0 attend.99
  2292.4 36.6 %mlp.48 = (f32[192,2560]{1,0:T(8,128)S(1)}, bf16[192,2560]{1,0:T(8,128)(2,1)S(1)}) custom-call(bf16[192,2560]{1,0:T(8,128)(2,1)S(1)} %fusion.206.uo_ref, bf16[192,2560]{1,0:T(8,128)(2,1)S(1)} %collective-permute-done.115.ux_ref, bf16[2560,5120]{1,0:T(8,128)(2,1)} %bitcast.244, bf16[2560,5120]{1,0:T(8,128)(2,1)} %bitcast.269, bf16[5120,2560]{1,0:T(8,128)(2,1)} %bitcast.294), custom_call_target="tpu_custom_call" | custom-call | flops 30198988800 | bytes 78643200 | tf_op jit(solution)/shard_map/mlp/pallas_call | solution.py:231
  2349.9 36.8 %mlp.49 = (f32[192,2560]{1,0:T(8,128)S(1)}, bf16[192,2560]{1,0:T(8,128)(2,1)S(1)}) custom-call(bf16[192,2560]{1,0:T(8,128)(2,1)S(1)} %fusion.215.uo_ref, bf16[192,2560]{1,0:T(8,128)(2,1)S(1)} %collective-permute-done.119.ux_ref, bf16[2560,5120]{1,0:T(8,128)(2,1)} %bitcast.245, bf16[2560,5120]{1,0:T(8,128)(2,1)} %bitcast.270, bf16[5120,2560]{1,0:T(8,128)(2,1)} %bitcast.295), custom_call_target="tpu_custom_call" | custom-call | flops 30198988800 | bytes 78643200 | tf_op jit(solution)/shard_map/mlp/pallas_call | solution.py:231
  (931 shorter events, 989.3 us)
Async XLA Ops:
  87.6 126.3 %collective-permute-start.7 = (bf16[2560,2048]{1,0:T(8,128)(2,1)}, bf16[2560,2048]{1,0:T(8,128)(2,1)}, u32[]{:S(2)}, u32[]{:S(2)}) collective-permute-start(bf16[2560,2048]{1,0:T(8,128)(2,1)} %slice_dynamic-update-slice_fusion.w_ref), channel_id=1, source_target_pairs={{1,5},{5,1}} | collective-permute-start | bytes 31457288 | tf_op jit(solution)/shard_map/ppermute | solution.py:284
  148.4 65.5 %collective-permute-start.8 = (bf16[1024,2560]{1,0:T(8,128)(2,1)}, bf16[1024,2560]{1,0:T(8,128)(2,1)}, u32[]{:S(2)}, u32[]{:S(2)}) collective-permute-start(bf16[1024,2560]{1,0:T(8,128)(2,1)} %bitcast.13.wo_ref), channel_id=1, source_target_pairs={{1,5},{5,1}} | collective-permute-start | bytes 15728648 | tf_op jit(solution)/shard_map/ppermute | solution.py:284
  321.5 141.5 %collective-permute-start.21 = (bf16[2560,2048]{1,0:T(8,128)(2,1)}, bf16[2560,2048]{1,0:T(8,128)(2,1)}, u32[]{:S(2)}, u32[]{:S(2)}) collective-permute-start(bf16[2560,2048]{1,0:T(8,128)(2,1)} %slice_dynamic-update-slice_fusion.w_ref), channel_id=1, source_target_pairs={{2,6},{6,2}} | collective-permute-start | bytes 31457288 | tf_op jit(solution)/shard_map/ppermute | solution.py:284
  400.0 62.9 %collective-permute-start.22 = (bf16[1024,2560]{1,0:T(8,128)(2,1)}, bf16[1024,2560]{1,0:T(8,128)(2,1)}, u32[]{:S(2)}, u32[]{:S(2)}) collective-permute-start(bf16[1024,2560]{1,0:T(8,128)(2,1)} %bitcast.13.wo_ref), channel_id=1, source_target_pairs={{2,6},{6,2}} | collective-permute-start | bytes 15728648 | tf_op jit(solution)/shard_map/ppermute | solution.py:284
  560.6 223.2 %collective-permute-start.35 = (bf16[2560,2048]{1,0:T(8,128)(2,1)}, bf16[2560,2048]{1,0:T(8,128)(2,1)}, u32[]{:S(2)}, u32[]{:S(2)}) collective-permute-start(bf16[2560,2048]{1,0:T(8,128)(2,1)} %slice_dynamic-update-slice_fusion.w_ref), channel_id=1, source_target_pairs={{3,7},{7,3}} | collective-permute-start | bytes 31457288 | tf_op jit(solution)/shard_map/ppermute | solution.py:284
  643.0 140.8 %collective-permute-start.36 = (bf16[1024,2560]{1,0:T(8,128)(2,1)}, bf16[1024,2560]{1,0:T(8,128)(2,1)}, u32[]{:S(2)}, u32[]{:S(2)}) collective-permute-start(bf16[1024,2560]{1,0:T(8,128)(2,1)} %bitcast.13.wo_ref), channel_id=1, source_target_pairs={{3,7},{7,3}} | collective-permute-start | bytes 15728648 | tf_op jit(solution)/shard_map/ppermute | solution.py:284
  666.2 115.0 %collective-permute-start.33 = (bf16[192,2560]{1,0:T(8,128)(2,1)S(1)}, bf16[192,2560]{1,0:T(8,128)(2,1)S(1)}, u32[]{:S(2)}, u32[]{:S(2)}) collective-permute-start(bf16[192,2560]{1,0:T(8,128)(2,1)S(1)} %fusion.259), channel_id=1, source_target_pairs={{0,1},{1,2},{2,3},{4,5},{5,6},{6,7}} | collective-permute-start | bytes 2949128 | tf_op jit(solution)/shard_map/ppermute | solution.py:347
  914.9 56.0 %collective-permute-start.43 = (bf16[192,2560]{1,0:T(8,128)(2,1)S(1)}, bf16[192,2560]{1,0:T(8,128)(2,1)S(1)}, u32[]{:S(2)}, u32[]{:S(2)}) collective-permute-start(bf16[192,2560]{1,0:T(8,128)(2,1)S(1)} %fusion.256), channel_id=1, source_target_pairs={{0,1},{1,2},{2,3},{4,5},{5,6},{6,7}} | collective-permute-start | bytes 2949128 | tf_op jit(solution)/shard_map/ppermute | solution.py:347
  1074.8 149.0 %collective-permute-start.49 = (bf16[192,2560]{1,0:T(8,128)(2,1)S(1)}, bf16[192,2560]{1,0:T(8,128)(2,1)S(1)}, u32[]{:S(2)}, u32[]{:S(2)}) collective-permute-start(bf16[192,2560]{1,0:T(8,128)(2,1)S(1)} %convert_element_type.895), channel_id=1, source_target_pairs={{0,4},{4,0}} | collective-permute-start | bytes 2949128 | tf_op jit(solution)/shard_map/ppermute | solution.py:284
  1075.6 148.7 %collective-permute-start.50 = (bf16[192,2560]{1,0:T(8,128)(2,1)S(1)}, bf16[192,2560]{1,0:T(8,128)(2,1)}, u32[]{:S(2)}, u32[]{:S(2)}) collective-permute-start(bf16[192,2560]{1,0:T(8,128)(2,1)S(1)} %get-tuple-element.504), channel_id=1, source_target_pairs={{0,4},{4,0},{1,5},{5,1},{2,6},{6,2},{3,7},{7,3}} | collective-permute-start | bytes 2949128 | tf_op jit(solution)/shard_map/ppermute | solution.py:284
  1077.0 153.9 %collective-permute-start.51 = (bf16[192,2560]{1,0:T(8,128)(2,1)}, bf16[192,2560]{1,0:T(8,128)(2,1)}, u32[]{:S(2)}, u32[]{:S(2)}) collective-permute-start(bf16[192,2560]{1,0:T(8,128)(2,1)} %fusion.253), channel_id=1, source_target_pairs={{3,0},{7,4}} | collective-permute-start | bytes 2949128 | tf_op jit(solution)/shard_map/ppermute | solution.py:356
  1391.1 54.9 %collective-permute-start.64 = (bf16[192,2560]{1,0:T(8,128)(2,1)}, bf16[192,2560]{1,0:T(8,128)(2,1)}, u32[]{:S(2)}, u32[]{:S(2)}) collective-permute-start(bf16[192,2560]{1,0:T(8,128)(2,1)} %fusion.250), channel_id=1, source_target_pairs={{3,0},{7,4}} | collective-permute-start | bytes 2949128 | tf_op jit(solution)/shard_map/ppermute | solution.py:356
  1550.5 55.6 %collective-permute-start.72 = (bf16[192,2560]{1,0:T(8,128)(2,1)}, bf16[192,2560]{1,0:T(8,128)(2,1)S(1)}, u32[]{:S(2)}, u32[]{:S(2)}) collective-permute-start(bf16[192,2560]{1,0:T(8,128)(2,1)} %fusion.245), channel_id=1, source_target_pairs={{0,1},{1,2},{2,3},{4,5},{5,6},{6,7}} | collective-permute-start | bytes 2949128 | tf_op jit(solution)/shard_map/ppermute | solution.py:347
  1551.8 92.5 %collective-permute-start.75 = (bf16[192,2560]{1,0:T(8,128)(2,1)}, bf16[192,2560]{1,0:T(8,128)(2,1)}, u32[]{:S(2)}, u32[]{:S(2)}) collective-permute-start(bf16[192,2560]{1,0:T(8,128)(2,1)} %fusion.245), channel_id=1, source_target_pairs={{3,1},{7,5}} | collective-permute-start | bytes 2949128 | tf_op jit(solution)/shard_map/ppermute | solution.py:356
  1555.1 91.6 %collective-permute-start.76 = (bf16[192,2560]{1,0:T(8,128)(2,1)}, bf16[192,2560]{1,0:T(8,128)(2,1)}, u32[]{:S(2)}, u32[]{:S(2)}) collective-permute-start(bf16[192,2560]{1,0:T(8,128)(2,1)} %fusion.245), channel_id=1, source_target_pairs={{3,5},{7,1}} | collective-permute-start | bytes 2949128 | tf_op jit(solution)/shard_map/ppermute | solution.py:357
  1557.5 91.4 %collective-permute-start.77 = (bf16[192,2560]{1,0:T(8,128)(2,1)S(1)}, bf16[192,2560]{1,0:T(8,128)(2,1)S(1)}, u32[]{:S(2)}, u32[]{:S(2)}) collective-permute-start(bf16[192,2560]{1,0:T(8,128)(2,1)S(1)} %fusion.134.uo_ref), channel_id=1, source_target_pairs={{0,4},{4,0},{1,5},{5,1},{2,6},{6,2},{3,7},{7,3}} | collective-permute-start | bytes 2949128 | tf_op jit(solution)/shard_map/ppermute | solution.py:284
  1635.7 51.0 %collective-permute-start.74 = (bf16[192,2560]{1,0:T(8,128)(2,1)}, bf16[192,2560]{1,0:T(8,128)(2,1)S(1)}, u32[]{:S(2)}, u32[]{:S(2)}) collective-permute-start(bf16[192,2560]{1,0:T(8,128)(2,1)} %fusion.244), channel_id=1, source_target_pairs={{0,1},{1,2},{2,3},{4,5},{5,6},{6,7}} | collective-permute-start | bytes 2949128 | tf_op jit(solution)/shard_map/ppermute | solution.py:347
  1637.0 82.8 %collective-permute-start.80 = (bf16[192,2560]{1,0:T(8,128)(2,1)}, bf16[192,2560]{1,0:T(8,128)(2,1)}, u32[]{:S(2)}, u32[]{:S(2)}) collective-permute-start(bf16[192,2560]{1,0:T(8,128)(2,1)} %fusion.244), channel_id=1, source_target_pairs={{3,1},{7,5}} | collective-permute-start | bytes 2949128 | tf_op jit(solution)/shard_map/ppermute | solution.py:356
  1644.3 77.7 %collective-permute-start.81 = (bf16[192,2560]{1,0:T(8,128)(2,1)}, bf16[192,2560]{1,0:T(8,128)(2,1)}, u32[]{:S(2)}, u32[]{:S(2)}) collective-permute-start(bf16[192,2560]{1,0:T(8,128)(2,1)} %fusion.244), channel_id=1, source_target_pairs={{3,5},{7,1}} | collective-permute-start | bytes 2949128 | tf_op jit(solution)/shard_map/ppermute | solution.py:357
  1646.6 85.2 %collective-permute-start.82 = (bf16[192,2560]{1,0:T(8,128)(2,1)S(1)}, bf16[192,2560]{1,0:T(8,128)(2,1)S(1)}, u32[]{:S(2)}, u32[]{:S(2)}) collective-permute-start(bf16[192,2560]{1,0:T(8,128)(2,1)S(1)} %fusion.146.uo_ref), channel_id=1, source_target_pairs={{1,5},{5,1},{2,6},{6,2},{3,7},{7,3}} | collective-permute-start | bytes 2949128 | tf_op jit(solution)/shard_map/ppermute | solution.py:284
  1714.4 57.2 %collective-permute-start.79 = (bf16[192,2560]{1,0:T(8,128)(2,1)}, bf16[192,2560]{1,0:T(8,128)(2,1)S(1)}, u32[]{:S(2)}, u32[]{:S(2)}) collective-permute-start(bf16[192,2560]{1,0:T(8,128)(2,1)} %fusion.241), channel_id=1, source_target_pairs={{0,1},{1,2},{2,3},{4,5},{5,6},{6,7}} | collective-permute-start | bytes 2949128 | tf_op jit(solution)/shard_map/ppermute | solution.py:347
  1715.7 95.7 %collective-permute-start.84 = (bf16[192,2560]{1,0:T(8,128)(2,1)}, bf16[192,2560]{1,0:T(8,128)(2,1)}, u32[]{:S(2)}, u32[]{:S(2)}) collective-permute-start(bf16[192,2560]{1,0:T(8,128)(2,1)} %fusion.241), channel_id=1, source_target_pairs={{3,1},{7,5}} | collective-permute-start | bytes 2949128 | tf_op jit(solution)/shard_map/ppermute | solution.py:356
  1719.8 93.9 %collective-permute-start.85 = (bf16[192,2560]{1,0:T(8,128)(2,1)}, bf16[192,2560]{1,0:T(8,128)(2,1)}, u32[]{:S(2)}, u32[]{:S(2)}) collective-permute-start(bf16[192,2560]{1,0:T(8,128)(2,1)} %fusion.241), channel_id=1, source_target_pairs={{3,5},{7,1}} | collective-permute-start | bytes 2949128 | tf_op jit(solution)/shard_map/ppermute | solution.py:357
  1722.1 94.7 %collective-permute-start.86 = (bf16[192,2560]{1,0:T(8,128)(2,1)S(1)}, bf16[192,2560]{1,0:T(8,128)(2,1)S(1)}, u32[]{:S(2)}, u32[]{:S(2)}) collective-permute-start(bf16[192,2560]{1,0:T(8,128)(2,1)S(1)} %fusion.152.uo_ref), channel_id=1, source_target_pairs={{1,5},{5,1},{2,6},{6,2},{3,7},{7,3}} | collective-permute-start | bytes 2949128 | tf_op jit(solution)/shard_map/ppermute | solution.py:284
  1801.1 55.4 %collective-permute-start.87 = (bf16[192,2560]{1,0:T(8,128)(2,1)}, bf16[192,2560]{1,0:T(8,128)(2,1)S(1)}, u32[]{:S(2)}, u32[]{:S(2)}) collective-permute-start(bf16[192,2560]{1,0:T(8,128)(2,1)} %fusion.239), channel_id=1, source_target_pairs={{1,2},{2,3},{5,6},{6,7}} | collective-permute-start | bytes 2949128 | tf_op jit(solution)/shard_map/ppermute | solution.py:347
  1802.3 91.0 %collective-permute-start.90 = (bf16[192,2560]{1,0:T(8,128)(2,1)}, bf16[192,2560]{1,0:T(8,128)(2,1)}, u32[]{:S(2)}, u32[]{:S(2)}) collective-permute-start(bf16[192,2560]{1,0:T(8,128)(2,1)} %fusion.239), channel_id=1, source_target_pairs={{3,1},{7,5}} | collective-permute-start | bytes 2949128 | tf_op jit(solution)/shard_map/ppermute | solution.py:356
  1811.4 84.1 %collective-permute-start.91 = (bf16[192,2560]{1,0:T(8,128)(2,1)}, bf16[192,2560]{1,0:T(8,128)(2,1)}, u32[]{:S(2)}, u32[]{:S(2)}) collective-permute-start(bf16[192,2560]{1,0:T(8,128)(2,1)} %fusion.239), channel_id=1, source_target_pairs={{3,5},{7,1}} | collective-permute-start | bytes 2949128 | tf_op jit(solution)/shard_map/ppermute | solution.py:357
  1813.7 84.1 %collective-permute-start.92 = (bf16[192,2560]{1,0:T(8,128)(2,1)S(1)}, bf16[192,2560]{1,0:T(8,128)(2,1)S(1)}, u32[]{:S(2)}, u32[]{:S(2)}) collective-permute-start(bf16[192,2560]{1,0:T(8,128)(2,1)S(1)} %fusion.161.uo_ref), channel_id=1, source_target_pairs={{1,5},{5,1},{2,6},{6,2},{3,7},{7,3}} | collective-permute-start | bytes 2949128 | tf_op jit(solution)/shard_map/ppermute | solution.py:284
  1885.2 52.3 %collective-permute-start.89 = (bf16[192,2560]{1,0:T(8,128)(2,1)}, bf16[192,2560]{1,0:T(8,128)(2,1)S(1)}, u32[]{:S(2)}, u32[]{:S(2)}) collective-permute-start(bf16[192,2560]{1,0:T(8,128)(2,1)} %fusion.238), channel_id=1, source_target_pairs={{1,2},{2,3},{5,6},{6,7}} | collective-permute-start | bytes 2949128 | tf_op jit(solution)/shard_map/ppermute | solution.py:347
  1886.5 87.6 %collective-permute-start.95 = (bf16[192,2560]{1,0:T(8,128)(2,1)}, bf16[192,2560]{1,0:T(8,128)(2,1)}, u32[]{:S(2)}, u32[]{:S(2)}) collective-permute-start(bf16[192,2560]{1,0:T(8,128)(2,1)} %fusion.238), channel_id=1, source_target_pairs={{3,2},{7,6}} | collective-permute-start | bytes 2949128 | tf_op jit(solution)/shard_map/ppermute | solution.py:356
  1893.3 83.0 %collective-permute-start.96 = (bf16[192,2560]{1,0:T(8,128)(2,1)}, bf16[192,2560]{1,0:T(8,128)(2,1)}, u32[]{:S(2)}, u32[]{:S(2)}) collective-permute-start(bf16[192,2560]{1,0:T(8,128)(2,1)} %fusion.238), channel_id=1, source_target_pairs={{3,6},{7,2}} | collective-permute-start | bytes 2949128 | tf_op jit(solution)/shard_map/ppermute | solution.py:357
  1895.6 83.1 %collective-permute-start.97 = (bf16[192,2560]{1,0:T(8,128)(2,1)S(1)}, bf16[192,2560]{1,0:T(8,128)(2,1)S(1)}, u32[]{:S(2)}, u32[]{:S(2)}) collective-permute-start(bf16[192,2560]{1,0:T(8,128)(2,1)S(1)} %fusion.173.uo_ref), channel_id=1, source_target_pairs={{2,6},{6,2},{3,7},{7,3}} | collective-permute-start | bytes 2949128 | tf_op jit(solution)/shard_map/ppermute | solution.py:284
  1969.1 84.2 %collective-permute-start.99 = (bf16[192,2560]{1,0:T(8,128)(2,1)}, bf16[192,2560]{1,0:T(8,128)(2,1)}, u32[]{:S(2)}, u32[]{:S(2)}) collective-permute-start(bf16[192,2560]{1,0:T(8,128)(2,1)} %fusion.235), channel_id=1, source_target_pairs={{3,2},{7,6}} | collective-permute-start | bytes 2949128 | tf_op jit(solution)/shard_map/ppermute | solution.py:356
  1974.1 81.5 %collective-permute-start.100 = (bf16[192,2560]{1,0:T(8,128)(2,1)}, bf16[192,2560]{1,0:T(8,128)(2,1)}, u32[]{:S(2)}, u32[]{:S(2)}) collective-permute-start(bf16[192,2560]{1,0:T(8,128)(2,1)} %fusion.235), channel_id=1, source_target_pairs={{3,6},{7,2}} | collective-permute-start | bytes 2949128 | tf_op jit(solution)/shard_map/ppermute | solution.py:357
  1976.3 82.4 %collective-permute-start.101 = (bf16[192,2560]{1,0:T(8,128)(2,1)S(1)}, bf16[192,2560]{1,0:T(8,128)(2,1)S(1)}, u32[]{:S(2)}, u32[]{:S(2)}) collective-permute-start(bf16[192,2560]{1,0:T(8,128)(2,1)S(1)} %fusion.179.uo_ref), channel_id=1, source_target_pairs={{2,6},{6,2},{3,7},{7,3}} | collective-permute-start | bytes 2949128 | tf_op jit(solution)/shard_map/ppermute | solution.py:284
  2047.0 51.5 %collective-permute-start.102 = (bf16[192,2560]{1,0:T(8,128)(2,1)}, bf16[192,2560]{1,0:T(8,128)(2,1)S(1)}, u32[]{:S(2)}, u32[]{:S(2)}) collective-permute-start(bf16[192,2560]{1,0:T(8,128)(2,1)} %fusion.233), channel_id=1, source_target_pairs={{2,3},{6,7}} | collective-permute-start | bytes 2949128 | tf_op jit(solution)/shard_map/ppermute | solution.py:347
  2048.3 88.8 %collective-permute-start.105 = (bf16[192,2560]{1,0:T(8,128)(2,1)}, bf16[192,2560]{1,0:T(8,128)(2,1)}, u32[]{:S(2)}, u32[]{:S(2)}) collective-permute-start(bf16[192,2560]{1,0:T(8,128)(2,1)} %fusion.233), channel_id=1, source_target_pairs={{3,2},{7,6}} | collective-permute-start | bytes 2949128 | tf_op jit(solution)/shard_map/ppermute | solution.py:356
  2053.3 86.0 %collective-permute-start.106 = (bf16[192,2560]{1,0:T(8,128)(2,1)}, bf16[192,2560]{1,0:T(8,128)(2,1)}, u32[]{:S(2)}, u32[]{:S(2)}) collective-permute-start(bf16[192,2560]{1,0:T(8,128)(2,1)} %fusion.233), channel_id=1, source_target_pairs={{3,6},{7,2}} | collective-permute-start | bytes 2949128 | tf_op jit(solution)/shard_map/ppermute | solution.py:357
  2055.6 86.0 %collective-permute-start.107 = (bf16[192,2560]{1,0:T(8,128)(2,1)S(1)}, bf16[192,2560]{1,0:T(8,128)(2,1)S(1)}, u32[]{:S(2)}, u32[]{:S(2)}) collective-permute-start(bf16[192,2560]{1,0:T(8,128)(2,1)S(1)} %fusion.188.uo_ref), channel_id=1, source_target_pairs={{2,6},{6,2},{3,7},{7,3}} | collective-permute-start | bytes 2949128 | tf_op jit(solution)/shard_map/ppermute | solution.py:284
  2128.8 52.5 %collective-permute-start.104 = (bf16[192,2560]{1,0:T(8,128)(2,1)}, bf16[192,2560]{1,0:T(8,128)(2,1)S(1)}, u32[]{:S(2)}, u32[]{:S(2)}) collective-permute-start(bf16[192,2560]{1,0:T(8,128)(2,1)} %fusion.232), channel_id=1, source_target_pairs={{2,3},{6,7}} | collective-permute-start | bytes 2949128 | tf_op jit(solution)/shard_map/ppermute | solution.py:347
  2130.1 84.6 %collective-permute-start.110 = (bf16[192,2560]{1,0:T(8,128)(2,1)}, bf16[192,2560]{1,0:T(8,128)(2,1)}, u32[]{:S(2)}, u32[]{:S(2)}) collective-permute-start(bf16[192,2560]{1,0:T(8,128)(2,1)} %fusion.232), channel_id=1, source_target_pairs={{3,2},{7,6}} | collective-permute-start | bytes 2949128 | tf_op jit(solution)/shard_map/ppermute | solution.py:356
  2137.1 80.6 %collective-permute-start.111 = (bf16[192,2560]{1,0:T(8,128)(2,1)}, bf16[192,2560]{1,0:T(8,128)(2,1)}, u32[]{:S(2)}, u32[]{:S(2)}) collective-permute-start(bf16[192,2560]{1,0:T(8,128)(2,1)} %fusion.232), channel_id=1, source_target_pairs={{3,6},{7,2}} | collective-permute-start | bytes 2949128 | tf_op jit(solution)/shard_map/ppermute | solution.py:357
  2139.3 78.4 %collective-permute-start.112 = (bf16[192,2560]{1,0:T(8,128)(2,1)S(1)}, bf16[192,2560]{1,0:T(8,128)(2,1)S(1)}, u32[]{:S(2)}, u32[]{:S(2)}) collective-permute-start(bf16[192,2560]{1,0:T(8,128)(2,1)S(1)} %fusion.200.uo_ref), channel_id=1, source_target_pairs={{3,7},{7,3}} | collective-permute-start | bytes 2949128 | tf_op jit(solution)/shard_map/ppermute | solution.py:284
  2211.4 81.0 %collective-permute-start.114 = (bf16[192,2560]{1,0:T(8,128)(2,1)}, bf16[192,2560]{1,0:T(8,128)(2,1)}, u32[]{:S(2)}, u32[]{:S(2)}) collective-permute-start(bf16[192,2560]{1,0:T(8,128)(2,1)} %get-tuple-element.721), channel_id=1, source_target_pairs={{3,7},{7,3}} | collective-permute-start | bytes 2949128 | tf_op jit(solution)/shard_map/ppermute | solution.py:357
  2214.7 77.7 %collective-permute-start.115 = (bf16[192,2560]{1,0:T(8,128)(2,1)S(1)}, bf16[192,2560]{1,0:T(8,128)(2,1)S(1)}, u32[]{:S(2)}, u32[]{:S(2)}) collective-permute-start(bf16[192,2560]{1,0:T(8,128)(2,1)S(1)} %fusion.206.uo_ref), channel_id=1, source_target_pairs={{3,7},{7,3}} | collective-permute-start | bytes 2949128 | tf_op jit(solution)/shard_map/ppermute | solution.py:284
  2283.6 66.4 %collective-permute-start.119 = (bf16[192,2560]{1,0:T(8,128)(2,1)S(1)}, bf16[192,2560]{1,0:T(8,128)(2,1)S(1)}, u32[]{:S(2)}, u32[]{:S(2)}) collective-permute-start(bf16[192,2560]{1,0:T(8,128)(2,1)S(1)} %fusion.215.uo_ref), channel_id=1, source_target_pairs={{3,7},{7,3}} | collective-permute-start | bytes 2949128 | tf_op jit(solution)/shard_map/ppermute | solution.py:284
  2290.0 59.9 %collective-permute-start.118 = (bf16[192,2560]{1,0:T(8,128)(2,1)S(1)}, bf16[192,2560]{1,0:T(8,128)(2,1)S(1)}, u32[]{:S(2)}, u32[]{:S(2)}) collective-permute-start(bf16[192,2560]{1,0:T(8,128)(2,1)S(1)} %get-tuple-element.719), channel_id=1, source_target_pairs={{3,7},{7,3}} | collective-permute-start | bytes 2949128 | tf_op jit(solution)/shard_map/ppermute | solution.py:357
  2346.9 60.0 %collective-permute-start.117 = (bf16[192,2560]{1,0:T(8,128)(2,1)S(1)}, bf16[192,2560]{1,0:T(8,128)(2,1)S(1)}, u32[]{:S(2)}, u32[]{:S(2)}) collective-permute-start(bf16[192,2560]{1,0:T(8,128)(2,1)S(1)} %get-tuple-element.715), channel_id=1, source_target_pairs={{3,7},{7,3}} | collective-permute-start | bytes 2949128 | tf_op jit(solution)/shard_map/ppermute | solution.py:357
  (268 other events, 3751.9 us)
